TPU v7x, 32 devices: a whole 2x2x4 slice. The times are simulated.
32 devices in a mesh: section: 2 (over y), dp: 4 (over x, core), mp: 4 (over z).
Axes of the slice: x: 2, y: 2, z: 4, core: 2. Of those that a mesh axis runs over, the one named last changes fastest.
Arguments:
- latents_in: bfloat16 [2, 4, 512, 1152], P(None, 'dp', 'mp'), may hold values from -6 to 6
- condition: bfloat16 [2, 4, 1152], P(None, 'dp'), may hold values from -1.5 to 1.5
- cotangent: bfloat16 [2, 4, 512, 1152], P(None, 'dp', 'mp'), may hold values from -6 to 6
- modulation_weight: bfloat16 [2, 1152, 6912], P('section', 'dp', 'mp'), may hold values from -0.1875 to 0.1875
- modulation_bias: bfloat16 [2, 6912], P('section', 'mp'), may hold values from -2.5 to 2.5
- query_key_value_weight: bfloat16 [2, 1152, 3, 1152], P('section', 'dp', None, 'mp'), may hold values from -0.1875 to 0.1875
- query_value_bias: bfloat16 [2, 2, 1152], P('section', None, 'mp'), may hold values from -2.5 to 2.5
- output_proj_weight: bfloat16 [2, 1152, 1152], P('section', 'mp', 'dp'), may hold values from -2 to 2
- output_proj_bias: bfloat16 [2, 1152], P('section'), may hold values from -2.5 to 2.5
- first_dense_weight: bfloat16 [2, 1152, 4608], P('section', 'dp', 'mp'), may hold values from -0.1875 to 0.1875
- first_dense_bias: bfloat16 [2, 4608], P('section', 'mp'), may hold values from -2.5 to 2.5
- second_dense_weight: bfloat16 [2, 4608, 1152], P('section', 'mp', 'dp'), may hold values from -0.09375 to 0.09375
- second_dense_bias: bfloat16 [2, 1152], P('section'), may hold values from -2.5 to 2.5
Outputs:
- acts: bfloat16 [2, 2, 4, 512, 1152], P('section', None, 'dp', 'mp')
- grad_input: float32 [2, 2, 4, 512, 1152], P('section', None, 'dp', 'mp')
- grad_cond: float32 [2, 4, 1152], P(None, 'dp')
- grad_weight_ada: float32 [2, 1152, 6912], P('section', 'dp', 'mp')
- grad_bias_ada: float32 [2, 6912], P('section', ('mp', 'dp'))
- grad_weight_qkv: float32 [2, 1152, 3, 1152], P('section', 'dp', None, 'mp')
- grad_bias_qv: float32 [2, 2, 1152], P('section', None, ('mp', 'dp'))
- grad_weight_proj: float32 [2, 1152, 1152], P('section', 'mp', 'dp')
- grad_bias_proj: float32 [2, 1152], P('section', 'dp')
- grad_weight_fc1: float32 [2, 1152, 4608], P('section', 'dp', 'mp')
- grad_bias_fc1: float32 [2, 4608], P('section', ('mp', 'dp'))
- grad_weight_fc2: float32 [2, 4608, 1152], P('section', 'mp', 'dp')
- grad_bias_fc2: float32 [2, 1152], P('section', 'dp')
All inputs are finite; a program needn't handle non-finite values.
Results may differ from a plain program's by a relative error of at most 0.015.
Values may be sent and summed in bfloat16 or wider, within the bound.
A program may use at most 192 MiB of HBM per device.

v0:
```python
import jax
import jax.numpy as jnp
from jax import lax
from jax.sharding import PartitionSpec as P

HEAD_SIZE = 72


def from_behind(block, axis, distance):
    devices = range(lax.axis_size(axis))
    route = [(i - distance, i) for i in devices if i - distance in devices]
    return lax.ppermute(block, axis, route)


def norm_rows(values):
    center = values - jnp.mean(values, axis=-1, keepdims=True)
    spread = jnp.mean(center * center, axis=-1, keepdims=True)
    return center * lax.rsqrt(spread + 1e-06)


def modulate(values, shift_vec, scale_vec):
    return norm_rows(values) * (1.0 + scale_vec[:, None, :]) + shift_vec[:, None, :]


def split_modul(modul, width):
    return tuple(
        (modul[:, block_index * width : (block_index + 1) * width] for block_index in range(6))
    )


def gather_tokens(local_rows):
    return lax.all_gather(local_rows, "mp", axis=1, tiled=True)


def reduce_tokens(partial_rows):
    return lax.psum_scatter(partial_rows, "mp", scatter_dimension=1, tiled=True)


def gather_cotangent(local_rows):
    return lax.all_gather(local_rows, "mp", axis=1, tiled=True)


def reduce_cotangent(partial_rows):
    return lax.psum_scatter(
        partial_rows.astype(jnp.bfloat16), "mp", scatter_dimension=1, tiled=True
    ).astype(jnp.float32)


def scatter_grads(
    grad_w_ada,
    grad_w_qkv,
    grad_w_proj,
    grad_w_fc1,
    grad_w_fc2,
    grad_b_ada,
    grad_b_qv,
    grad_b_proj,
    grad_b_fc1,
    grad_b_fc2,
):
    return (
        lax.psum_scatter(
            grad_w_ada.astype(jnp.bfloat16), "dp", scatter_dimension=0, tiled=True
        ).astype(jnp.float32),
        lax.psum_scatter(
            grad_w_qkv.astype(jnp.bfloat16), "dp", scatter_dimension=0, tiled=True
        ).astype(jnp.float32),
        lax.psum_scatter(
            grad_w_proj.astype(jnp.bfloat16), "dp", scatter_dimension=1, tiled=True
        ).astype(jnp.float32),
        lax.psum_scatter(
            grad_w_fc1.astype(jnp.bfloat16), "dp", scatter_dimension=0, tiled=True
        ).astype(jnp.float32),
        lax.psum_scatter(
            grad_w_fc2.astype(jnp.bfloat16), "dp", scatter_dimension=1, tiled=True
        ).astype(jnp.float32),
        lax.psum_scatter(
            grad_b_ada.astype(jnp.bfloat16), "dp", scatter_dimension=0, tiled=True
        ).astype(jnp.float32),
        lax.psum_scatter(
            grad_b_qv.astype(jnp.bfloat16), "dp", scatter_dimension=1, tiled=True
        ).astype(jnp.float32),
        lax.psum_scatter(
            grad_b_proj.astype(jnp.bfloat16), "dp", scatter_dimension=0, tiled=True
        ).astype(jnp.float32),
        lax.psum_scatter(
            grad_b_fc1.astype(jnp.bfloat16), "dp", scatter_dimension=0, tiled=True
        ).astype(jnp.float32),
        lax.psum_scatter(
            grad_b_fc2.astype(jnp.bfloat16), "dp", scatter_dimension=0, tiled=True
        ).astype(jnp.float32),
    )


def split_heads(triple_in):
    seq_len = triple_in.shape[0]
    head_count = triple_in.shape[-1] // HEAD_SIZE
    query_rows = triple_in[:, 0].reshape(seq_len, head_count, HEAD_SIZE)
    key_input = triple_in[:, 1].reshape(seq_len, head_count, HEAD_SIZE)
    value_input = triple_in[:, 2].reshape(seq_len, head_count, HEAD_SIZE)
    return (query_rows, key_input, value_input)


def softmax_rows(query_rows, key_input):
    logit_scores = jnp.einsum(
        "cla,vla->lcv", query_rows, key_input, preferred_element_type=jnp.float32
    ) * HEAD_SIZE ** (-0.5)
    powered = jnp.exp(logit_scores)
    return powered / jnp.sum(powered, axis=-1, keepdims=True)


def attend_latent(triple_in):
    query_rows, key_input, value_input = split_heads(triple_in)
    attention_probs = softmax_rows(query_rows, key_input).astype(jnp.bfloat16)
    attn_out = jnp.einsum(
        "cad,dce->ace", attention_probs, value_input, preferred_element_type=jnp.float32
    )
    return attn_out.reshape(triple_in.shape[0], -1).astype(jnp.bfloat16)


def attend_back(pair_in):
    triple_in, grad_out = pair_in
    query_rows, key_input, value_input = split_heads(triple_in)
    weights_full = softmax_rows(query_rows, key_input)
    head_gradient = grad_out.reshape(query_rows.shape)
    grad_values = jnp.einsum(
        "zyj,yzv->jzv",
        weights_full.astype(jnp.bfloat16),
        head_gradient,
        preferred_element_type=jnp.float32,
    )
    grad_weights = jnp.einsum(
        "cla,vla->lcv", head_gradient, value_input, preferred_element_type=jnp.float32
    )
    score_gradient = (
        weights_full * (grad_weights - jnp.sum(weights_full * grad_weights, axis=-1, keepdims=True))
    ).astype(jnp.bfloat16)
    grad_queries = jnp.einsum(
        "cad,dce->ace", score_gradient, key_input, preferred_element_type=jnp.float32
    ) * HEAD_SIZE ** (-0.5)
    grad_keys = jnp.einsum(
        "zyj,yzv->jzv", score_gradient, query_rows, preferred_element_type=jnp.float32
    ) * HEAD_SIZE ** (-0.5)
    stacked = jnp.stack([grad_queries, grad_keys, grad_values], axis=1)
    return stacked.reshape(triple_in.shape).astype(jnp.bfloat16)


def forward_layer(hidden_input, condition, gathered, bias_set):
    (
        modulation_weight,
        query_key_value_weight,
        output_proj_weight,
        first_dense_weight,
        second_dense_weight,
    ) = gathered
    modulation_bias, query_value_bias, output_proj_bias, first_dense_bias, second_dense_bias = (
        bias_set
    )
    width = hidden_input.shape[-1]
    cond_act = jax.nn.silu(condition.astype(jnp.float32)).astype(jnp.bfloat16)
    modul_part = (
        jnp.dot(cond_act, modulation_weight, preferred_element_type=jnp.float32) + modulation_bias
    )
    modul = lax.all_gather(modul_part, "mp", axis=1, tiled=True)
    shift_att, scale_att, gate_att, shift_mlp, scale_mlp, gate_mlp = split_modul(modul, width)
    normed_all = gather_tokens(modulate(hidden_input, shift_att, scale_att).astype(jnp.bfloat16))
    project = jnp.einsum(
        "lsd,dcf->lscf", normed_all, query_key_value_weight, preferred_element_type=jnp.float32
    )
    qkv_bias = jnp.stack(
        [query_value_bias[0], jnp.zeros_like(query_value_bias[0]), query_value_bias[1]]
    )
    project_low = (project + qkv_bias).astype(jnp.bfloat16)
    attended_rows = lax.map(attend_latent, project_low)
    attention_branch = (
        reduce_tokens(
            jnp.einsum(
                "qru,uw->qrw", attended_rows, output_proj_weight, preferred_element_type=jnp.float32
            )
        )
        + output_proj_bias
    )
    middle = hidden_input + gate_att[:, None, :] * attention_branch
    dense_normed_full = gather_tokens(modulate(middle, shift_mlp, scale_mlp).astype(jnp.bfloat16))
    preactivation = (
        jnp.einsum(
            "vya,ae->vye", dense_normed_full, first_dense_weight, preferred_element_type=jnp.float32
        )
        + first_dense_bias
    )
    gelu_result = jax.nn.gelu(preactivation, approximate=True).astype(jnp.bfloat16)
    dense_branch = (
        reduce_tokens(
            jnp.einsum(
                "qru,uw->qrw", gelu_result, second_dense_weight, preferred_element_type=jnp.float32
            )
        )
        + second_dense_bias
    )
    result = middle + gate_mlp[:, None, :] * dense_branch
    kept = (
        modul,
        cond_act,
        normed_all,
        project_low,
        attended_rows,
        attention_branch,
        middle,
        dense_normed_full,
        preactivation,
        gelu_result,
        dense_branch,
    )
    return (result, kept)


def backward_layer(hidden_input, condition, gathered, grad_out, stored):
    (
        modulation_weight,
        query_key_value_weight,
        output_proj_weight,
        first_dense_weight,
        second_dense_weight,
    ) = gathered
    (
        modul,
        cond_act,
        normed_all,
        project_low,
        attended_rows,
        attention_branch,
        middle,
        dense_normed_full,
        preactivation,
        gelu_result,
        dense_branch,
    ) = stored
    shift_att, scale_att, gate_att, shift_mlp, scale_mlp, gate_mlp = split_modul(
        modul, hidden_input.shape[-1]
    )
    grad_gate_mlp = jnp.sum(grad_out * dense_branch, axis=1)
    branch_gradient = gather_cotangent((grad_out * gate_mlp[:, None, :]).astype(jnp.bfloat16))
    grad_b_fc2 = jnp.sum(branch_gradient, axis=(0, 1), dtype=jnp.float32)
    grad_w_fc2 = jnp.einsum(
        "vwc,vwg->cg", gelu_result, branch_gradient, preferred_element_type=jnp.float32
    )
    grad_gelu = jnp.einsum(
        "aju,cu->ajc", branch_gradient, second_dense_weight, preferred_element_type=jnp.float32
    )
    gelu_value, gelu_back = jax.vjp(
        lambda values: jax.nn.gelu(values, approximate=True), preactivation
    )
    preact_gradient = gelu_back(grad_gelu)[0].astype(jnp.bfloat16)
    grad_b_fc1 = jnp.sum(preact_gradient, axis=(0, 1), dtype=jnp.float32)
    grad_w_fc1 = jnp.einsum(
        "vpa,vph->ah", dense_normed_full, preact_gradient, preferred_element_type=jnp.float32
    )
    grad_normed_mlp = reduce_cotangent(
        jnp.einsum(
            "vja,qa->vjq", preact_gradient, first_dense_weight, preferred_element_type=jnp.float32
        )
    )
    norm_value, norm_back = jax.vjp(modulate, middle, shift_mlp, scale_mlp)
    grad_middle, grad_shift_mlp, grad_scale_mlp = norm_back(grad_normed_mlp)
    grad_middle = grad_middle + grad_out
    grad_gate_att = jnp.sum(grad_middle * attention_branch, axis=1)
    attention_branch_gradient = gather_cotangent(
        (grad_middle * gate_att[:, None, :]).astype(jnp.bfloat16)
    )
    grad_b_proj = jnp.sum(attention_branch_gradient, axis=(0, 1), dtype=jnp.float32)
    grad_w_proj = jnp.einsum(
        "vwc,vwg->cg", attended_rows, attention_branch_gradient, preferred_element_type=jnp.float32
    )
    grad_attended = jnp.einsum(
        "aju,cu->ajc",
        attention_branch_gradient,
        output_proj_weight,
        preferred_element_type=jnp.float32,
    ).astype(jnp.bfloat16)
    grad_project = lax.map(attend_back, (project_low, grad_attended))
    grad_b_qv = jnp.stack(
        [
            jnp.sum(grad_project[:, :, 0], axis=(0, 1), dtype=jnp.float32),
            jnp.sum(grad_project[:, :, 2], axis=(0, 1), dtype=jnp.float32),
        ]
    )
    grad_w_qkv = jnp.einsum(
        "lsd,lscf->dcf", normed_all, grad_project, preferred_element_type=jnp.float32
    )
    grad_normed = reduce_cotangent(
        jnp.einsum(
            "lscf,dcf->lsd",
            grad_project,
            query_key_value_weight,
            preferred_element_type=jnp.float32,
        )
    )
    first_value, first_back = jax.vjp(modulate, hidden_input, shift_att, scale_att)
    grad_hidden, grad_shift_att, grad_scale_att = first_back(grad_normed)
    grad_hidden = grad_hidden + grad_middle
    grad_modul = jnp.concatenate(
        [
            grad_shift_att,
            grad_scale_att,
            grad_gate_att,
            grad_shift_mlp,
            grad_scale_mlp,
            grad_gate_mlp,
        ],
        axis=1,
    )
    grad_modul = lax.psum_scatter(grad_modul, "mp", scatter_dimension=1, tiled=True).astype(
        jnp.bfloat16
    )
    grad_b_ada = jnp.sum(grad_modul, axis=0, dtype=jnp.float32)
    grad_w_ada = jnp.dot(cond_act.T, grad_modul, preferred_element_type=jnp.float32)
    grad_act = jnp.dot(grad_modul, modulation_weight.T, preferred_element_type=jnp.float32)
    silu_value, silu_back = jax.vjp(jax.nn.silu, condition.astype(jnp.float32))
    grad_cond = silu_back(grad_act)[0]
    weight_grads = (
        grad_w_ada,
        grad_w_qkv,
        grad_w_proj,
        grad_w_fc1,
        grad_w_fc2,
        grad_b_ada,
        grad_b_qv,
        grad_b_proj,
        grad_b_fc1,
        grad_b_fc2,
    )
    return (grad_hidden, grad_cond, weight_grads)


def per_device(
    latents_in,
    condition,
    cotangent,
    modulation_weight,
    modulation_bias,
    query_key_value_weight,
    query_value_bias,
    output_proj_weight,
    output_proj_bias,
    first_dense_weight,
    first_dense_bias,
    second_dense_weight,
    second_dense_bias,
):
    section_first = lax.axis_index("section") == 0
    micro = latents_in.shape[0]
    bias_set = (
        modulation_bias[0].astype(jnp.float32),
        query_value_bias[0].astype(jnp.float32),
        output_proj_bias[0].astype(jnp.float32),
        first_dense_bias[0].astype(jnp.float32),
        second_dense_bias[0].astype(jnp.float32),
    )
    gathered = (
        lax.all_gather(modulation_weight[0], "dp", axis=0, tiled=True),
        lax.all_gather(query_key_value_weight[0], "dp", axis=0, tiled=True),
        lax.all_gather(output_proj_weight[0], "dp", axis=1, tiled=True),
        lax.all_gather(first_dense_weight[0], "dp", axis=0, tiled=True),
        lax.all_gather(second_dense_weight[0], "dp", axis=1, tiled=True),
    )
    received = jnp.zeros(latents_in.shape[1:], jnp.bfloat16)
    tick_inputs = []
    tick_outputs = []
    tick_kept = []
    for moment in range(micro + 1):
        own_micro = min(moment, micro - 1)
        prior_micro = max(moment - 1, 0)
        layer_in = jnp.where(section_first, latents_in[own_micro], received)
        cond_now = jnp.where(section_first, condition[own_micro], condition[prior_micro])
        layer_result, layer_kept = forward_layer(
            layer_in.astype(jnp.float32), cond_now, gathered, bias_set
        )
        layer_out = layer_result.astype(jnp.bfloat16)
        received = from_behind(layer_out, "section", 1)
        tick_inputs.append(layer_in)
        tick_outputs.append(layer_out)
        tick_kept.append(layer_kept)
    saved_inputs = [
        jnp.where(section_first, tick_inputs[slot_index], tick_inputs[slot_index + 1])
        for slot_index in range(micro)
    ]
    acts_out = jnp.stack(
        [
            jnp.where(section_first, tick_outputs[slot_index], tick_outputs[slot_index + 1])
            for slot_index in range(micro)
        ]
    )[None]
    gathered_back = (
        lax.all_gather(modulation_weight[0], "dp", axis=0, tiled=True),
        lax.all_gather(query_key_value_weight[0], "dp", axis=0, tiled=True),
        lax.all_gather(output_proj_weight[0], "dp", axis=1, tiled=True),
        lax.all_gather(first_dense_weight[0], "dp", axis=0, tiled=True),
        lax.all_gather(second_dense_weight[0], "dp", axis=1, tiled=True),
    )
    back_received = jnp.zeros(latents_in.shape[1:], jnp.bfloat16)
    cond_grads = jnp.zeros(condition.shape, jnp.float32)
    grad_sums = None
    tick_grads = []
    for moment in range(micro + 1):
        last_micro = min(moment, micro - 1)
        first_micro = max(moment - 1, 0)
        if moment < micro:
            from_cot = cotangent[moment].astype(jnp.float32)
        else:
            from_cot = jnp.zeros(latents_in.shape[1:], jnp.float32)
        grad_in = jnp.where(section_first, back_received.astype(jnp.float32), from_cot)
        layer_in = jnp.where(section_first, saved_inputs[first_micro], saved_inputs[last_micro])
        cond_now = jnp.where(section_first, condition[first_micro], condition[last_micro])
        stored = jax.tree.map(
            lambda early, late: jnp.where(section_first, early, late),
            tick_kept[first_micro],
            tick_kept[last_micro + 1],
        )
        grad_hidden, grad_cond, weight_grads = backward_layer(
            layer_in.astype(jnp.float32), cond_now, gathered_back, grad_in, stored
        )
        back_received = from_behind(grad_hidden.astype(jnp.bfloat16), "section", -1)
        tick_grads.append(grad_hidden)
        micro_index = jnp.where(section_first, first_micro, last_micro)
        selector = (jnp.arange(micro) == micro_index).astype(jnp.float32)
        cond_grads = cond_grads + selector[:, None, None] * grad_cond[None]
        grad_sums = (
            weight_grads if grad_sums is None else jax.tree.map(jnp.add, grad_sums, weight_grads)
        )
    final_grads = scatter_grads(*grad_sums)
    grad_input = jnp.stack(
        [
            jnp.where(section_first, tick_grads[slot_index + 1], tick_grads[slot_index])
            for slot_index in range(micro)
        ]
    )[None]
    grad_cond_all = lax.psum(cond_grads, ("section", "mp"))
    return (
        acts_out,
        grad_input,
        grad_cond_all,
        final_grads[0][None],
        final_grads[5][None],
        final_grads[1][None],
        final_grads[6][None],
        final_grads[2][None],
        final_grads[7][None],
        final_grads[3][None],
        final_grads[8][None],
        final_grads[4][None],
        final_grads[9][None],
    )


def solution(mesh):
    in_specs = (
        P(None, "dp", "mp", None),
        P(None, "dp", None),
        P(None, "dp", "mp", None),
        P("section", "dp", "mp"),
        P("section", "mp"),
        P("section", "dp", None, "mp"),
        P("section", None, "mp"),
        P("section", "mp", "dp"),
        P("section", None),
        P("section", "dp", "mp"),
        P("section", "mp"),
        P("section", "mp", "dp"),
        P("section", None),
    )
    out_specs = (
        P("section", None, "dp", "mp", None),
        P("section", None, "dp", "mp", None),
        P(None, "dp", None),
        P("section", "dp", "mp"),
        P("section", ("mp", "dp")),
        P("section", "dp", None, "mp"),
        P("section", None, ("mp", "dp")),
        P("section", "mp", "dp"),
        P("section", "dp"),
        P("section", "dp", "mp"),
        P("section", ("mp", "dp")),
        P("section", "mp", "dp"),
        P("section", "dp"),
    )
    return jax.shard_map(
        per_device, mesh=mesh, in_specs=in_specs, out_specs=out_specs, check_vma=False
    )
```

profile of v0, /device:TPU:4, one launch (start us, length us, event | category | flops | bytes accessed | tf_op | source)
XLA Modules:
  0.0 1524.8 jit_solution(13788046298628970407)
XLA Ops:
  12.7 32.2 %all-gather.49.cloned.1.call-done = bf16[1,1152,1728]{2,1,0:T(8,128)(2,1)} async-done(((bf16[1,288,1728]{2,1,0:T(8,128)(2,1)}), bf16[1,1152,1728]{2,1,0:T(8,128)(2,1)}) %all-gather.49.cloned.1.call-update) | async-done | bytes 3981328 | tf_op jit(solution)/shard_map/all_gather | solution.py:360
  52.5 32.6 %all-reduce.12.cloned.1.call-done = (f32[6912]{0:T(1024)}, f32[6912]{0:T(1024)}, f32[6912]{0:T(1024)}) async-done(((f32[6912]{0:T(1024)}, f32[6912]{0:T(1024)}, f32[6912]{0:T(1024)}), (f32[6912]{0:T(1024)}, f32[6912]{0:T(1024)}, f32[6912]{0:T(1024)})) %all-reduce.12.cloned.1.call-update) | async-done | bytes 82960
  87.8 18.3 %all-gather.3 = bf16[1,288,1152]{1,0,2:T(2,128)(2,1)} all-gather(bf16[1,288,288]{1,0,2:T(2,128)(2,1)S(1)} %copy.67), channel_id=5, replica_groups=mesh['section'=2,'dp'=4,'mp'=4] {'dp'}, dimensions={2}, use_global_device_ids=true | all-gather | bytes 829440 | tf_op jit(solution)/shard_map/all_gather | solution.py:362
  106.1 4.4 copy.68
  110.7 10.6 all-gather.51.cloned.1.call-done
  121.3 7.0 copy.65
  128.4 24.4 %all-gather.25.cloned.1.call-done = bf16[1,512,1152]{2,1,0:T(8,128)(2,1)} async-done(((bf16[1,128,1152]{2,1,0:T(8,128)(2,1)}), bf16[1,512,1152]{2,1,0:T(8,128)(2,1)}) %all-gather.25.cloned.1.call-update) | async-done | bytes 1179664 | tf_op jit(solution)/shard_map/all_gather | solution.py:32
  161.7 46.4 %reduce-scatter.30.cloned.1.call-done = f32[1,128,1152]{2,1,0:T(8,128)} async-done(((f32[1,512,1152]{2,1,0:T(8,128)}), f32[1,128,1152]{2,1,0:T(8,128)}) %reduce-scatter.30.cloned.1.call-update) | async-done | bytes 589840 | tf_op jit(solution)/shard_map/reduce_scatter | solution.py:36
  211.6 23.1 %all-gather.53.cloned.1.call-done = bf16[1,1152,1152]{2,1,0:T(8,128)(2,1)} async-done(((bf16[1,288,1152]{2,1,0:T(8,128)(2,1)}), bf16[1,1152,1152]{2,1,0:T(8,128)(2,1)}) %all-gather.53.cloned.1.call-update) | async-done | bytes 2654224 | tf_op jit(solution)/shard_map/all_gather | solution.py:363
  234.7 32.4 %all-gather.27.cloned.1.call-done = bf16[1,512,1152]{2,1,0:T(8,128)(2,1)} async-done(((bf16[1,128,1152]{2,1,0:T(8,128)(2,1)}), bf16[1,512,1152]{2,1,0:T(8,128)(2,1)}) %all-gather.27.cloned.1.call-update) | async-done | bytes 1179664 | tf_op jit(solution)/shard_map/all_gather | solution.py:32
  267.1 5.4 convolution_add_fusion.6
  272.5 21.1 %all-gather.55.cloned.1.call-done = bf16[1,1152,1152]{1,2,0:T(8,128)(2,1)} async-done(((bf16[1,1152,288]{1,2,0:T(8,128)(2,1)}), bf16[1,1152,1152]{1,2,0:T(8,128)(2,1)}) %all-gather.55.cloned.1.call-update) | async-done | bytes 2654224 | tf_op jit(solution)/shard_map/all_gather | solution.py:364
  293.6 6.1 convolution_bitcast_fusion.7
  300.4 47.2 %reduce-scatter.32.cloned.1.call-done = f32[1,128,1152]{2,1,0:T(8,128)} async-done(((f32[1,512,1152]{2,1,0:T(8,128)}), f32[1,128,1152]{2,1,0:T(8,128)}) %reduce-scatter.32.cloned.1.call-update) | async-done | bytes 589840 | tf_op jit(solution)/shard_map/reduce_scatter | solution.py:36
  350.1 8.8 collective-permute-done
  360.4 30.1 %all-gather.29.cloned.1.call-done = bf16[1,512,1152]{2,1,0:T(8,128)(2,1)} async-done(((bf16[1,128,1152]{2,1,0:T(8,128)(2,1)}), bf16[1,512,1152]{2,1,0:T(8,128)(2,1)}) %all-gather.29.cloned.1.call-update) | async-done | bytes 1179664 | tf_op jit(solution)/shard_map/all_gather | solution.py:32
  398.8 47.0 %reduce-scatter.34.cloned.1.call-done = f32[1,128,1152]{2,1,0:T(8,128)} async-done(((f32[1,512,1152]{2,1,0:T(8,128)}), f32[1,128,1152]{2,1,0:T(8,128)}) %reduce-scatter.34.cloned.1.call-update) | async-done | bytes 589840 | tf_op jit(solution)/shard_map/reduce_scatter | solution.py:36
  450.6 27.6 %all-gather.31.cloned.1.call-done = bf16[1,512,1152]{2,1,0:T(8,128)(2,1)} async-done(((bf16[1,128,1152]{2,1,0:T(8,128)(2,1)}), bf16[1,512,1152]{2,1,0:T(8,128)(2,1)}) %all-gather.31.cloned.1.call-update) | async-done | bytes 1179664 | tf_op jit(solution)/shard_map/all_gather | solution.py:32
  478.2 5.4 convolution_add_fusion.5
  483.6 26.3 %all-gather.37.cloned.1.call-done = bf16[1,512,1152]{2,1,0:T(8,128)(2,1)} async-done(((bf16[1,128,1152]{2,1,0:T(8,128)(2,1)}), bf16[1,512,1152]{2,1,0:T(8,128)(2,1)}) %all-gather.37.cloned.1.call-update) | async-done | bytes 1179664 | tf_op jit(solution)/shard_map/all_gather | solution.py:40
  509.8 6.2 convert_reduce_fusion.5
  520.0 6.1 convolution_bitcast_fusion.5
  526.2 22.5 %reduce-scatter.42.cloned.1.call-done = bf16[1,128,1152]{2,1,0:T(8,128)(2,1)} async-done(((bf16[1,512,1152]{2,1,0:T(8,128)(2,1)}), bf16[1,128,1152]{2,1,0:T(8,128)(2,1)}) %reduce-scatter.42.cloned.1.call-update) | async-done | bytes 294928 | tf_op jit(solution)/shard_map/reduce_scatter | solution.py:44
  553.6 43.5 %reduce-scatter.36.cloned.1.call-done = f32[1,128,1152]{2,1,0:T(8,128)} async-done(((f32[1,512,1152]{2,1,0:T(8,128)}), f32[1,128,1152]{2,1,0:T(8,128)}) %reduce-scatter.36.cloned.1.call-update) | async-done | bytes 589840 | tf_op jit(solution)/shard_map/reduce_scatter | solution.py:36
  601.0 8.3 collective-permute-done.1
  612.4 15.9 %all-gather.39.cloned.1.call-done = bf16[1,512,1152]{2,1,0:T(8,128)(2,1)} async-done(((bf16[1,128,1152]{2,1,0:T(8,128)(2,1)}), bf16[1,512,1152]{2,1,0:T(8,128)(2,1)}) %all-gather.39.cloned.1.call-update) | async-done | bytes 1179664 | tf_op jit(solution)/shard_map/all_gather | solution.py:40
  630.8 29.0 %all-gather.33.cloned.1.call-done = bf16[1,512,1152]{2,1,0:T(8,128)(2,1)} async-done(((bf16[1,128,1152]{2,1,0:T(8,128)(2,1)}), bf16[1,512,1152]{2,1,0:T(8,128)(2,1)}) %all-gather.33.cloned.1.call-update) | async-done | bytes 1179664 | tf_op jit(solution)/shard_map/all_gather | solution.py:32
  659.8 5.2 broadcast_select_fusion
  681.6 21.2 %reduce-scatter.44.cloned.1.call-done = bf16[1,128,1152]{2,1,0:T(8,128)(2,1)} async-done(((bf16[1,512,1152]{2,1,0:T(8,128)(2,1)}), bf16[1,128,1152]{2,1,0:T(8,128)(2,1)}) %reduce-scatter.44.cloned.1.call-update) | async-done | bytes 294928 | tf_op jit(solution)/shard_map/reduce_scatter | solution.py:44
  704.0 47.4 %reduce-scatter.38.cloned.1.call-done = f32[1,128,1152]{2,1,0:T(8,128)} async-done(((f32[1,512,1152]{2,1,0:T(8,128)}), f32[1,128,1152]{2,1,0:T(8,128)}) %reduce-scatter.38.cloned.1.call-update) | async-done | bytes 589840 | tf_op jit(solution)/shard_map/reduce_scatter | solution.py:36
  760.5 5.8 collective-permute-done.2
  768.0 15.8 %all-gather.35.cloned.1.call-done = bf16[1,512,1152]{2,1,0:T(8,128)(2,1)} async-done(((bf16[1,128,1152]{2,1,0:T(8,128)(2,1)}), bf16[1,512,1152]{2,1,0:T(8,128)(2,1)}) %all-gather.35.cloned.1.call-update) | async-done | bytes 1179664 | tf_op jit(solution)/shard_map/all_gather | solution.py:32
  783.8 5.5 convolution_add_fusion.4
  789.3 26.2 %all-gather.41.cloned.1.call-done = bf16[1,512,1152]{2,1,0:T(8,128)(2,1)} async-done(((bf16[1,128,1152]{2,1,0:T(8,128)(2,1)}), bf16[1,512,1152]{2,1,0:T(8,128)(2,1)}) %all-gather.41.cloned.1.call-update) | async-done | bytes 1179664 | tf_op jit(solution)/shard_map/all_gather | solution.py:40
  815.5 5.6 convert_reduce_fusion.4
  825.1 28.7 %reduce-scatter.46.cloned.1.call-done = bf16[1,128,1152]{2,1,0:T(8,128)(2,1)} async-done(((bf16[1,512,1152]{2,1,0:T(8,128)(2,1)}), bf16[1,128,1152]{2,1,0:T(8,128)(2,1)}) %reduce-scatter.46.cloned.1.call-update) | async-done | bytes 294928 | tf_op jit(solution)/shard_map/reduce_scatter | solution.py:44
  863.4 24.2 %all-gather.43.cloned.1.call-done = bf16[1,512,1152]{2,1,0:T(8,128)(2,1)} async-done(((bf16[1,128,1152]{2,1,0:T(8,128)(2,1)}), bf16[1,512,1152]{2,1,0:T(8,128)(2,1)}) %all-gather.43.cloned.1.call-update) | async-done | bytes 1179664 | tf_op jit(solution)/shard_map/all_gather | solution.py:40
  889.5 3.3 convert_reduce_fusion.23
  899.5 6.1 convolution_bitcast_fusion.3
  905.6 22.5 %reduce-scatter.48.cloned.1.call-done = bf16[1,128,1152]{2,1,0:T(8,128)(2,1)} async-done(((bf16[1,512,1152]{2,1,0:T(8,128)(2,1)}), bf16[1,128,1152]{2,1,0:T(8,128)(2,1)}) %reduce-scatter.48.cloned.1.call-update) | async-done | bytes 294928 | tf_op jit(solution)/shard_map/reduce_scatter | solution.py:44
  936.5 40.2 %reduce-scatter.40.cloned.1.call-done = f32[1,128,1152]{2,1,0:T(8,128)} async-done(((f32[1,512,1152]{2,1,0:T(8,128)}), f32[1,128,1152]{2,1,0:T(8,128)}) %reduce-scatter.40.cloned.1.call-update) | async-done | bytes 589840 | tf_op jit(solution)/shard_map/reduce_scatter | solution.py:36
  979.9 29.4 %all-gather.45.cloned.1.call-done = bf16[1,512,1152]{2,1,0:T(8,128)(2,1)} async-done(((bf16[1,128,1152]{2,1,0:T(8,128)(2,1)}), bf16[1,512,1152]{2,1,0:T(8,128)(2,1)}) %all-gather.45.cloned.1.call-update) | async-done | bytes 1179664 | tf_op jit(solution)/shard_map/all_gather | solution.py:40
  1009.3 5.6 convert_reduce_fusion.3
  1018.9 28.6 %reduce-scatter.50.cloned.1.call-done = bf16[1,128,1152]{2,1,0:T(8,128)(2,1)} async-done(((bf16[1,512,1152]{2,1,0:T(8,128)(2,1)}), bf16[1,128,1152]{2,1,0:T(8,128)(2,1)}) %reduce-scatter.50.cloned.1.call-update) | async-done | bytes 294928 | tf_op jit(solution)/shard_map/reduce_scatter | solution.py:44
  1054.4 5.8 fusion.148
  1063.8 19.6 %all-gather.47.cloned.1.call-done = bf16[1,512,1152]{2,1,0:T(8,128)(2,1)} async-done(((bf16[1,128,1152]{2,1,0:T(8,128)(2,1)}), bf16[1,512,1152]{2,1,0:T(8,128)(2,1)}) %all-gather.47.cloned.1.call-update) | async-done | bytes 1179664 | tf_op jit(solution)/shard_map/all_gather | solution.py:40
  1085.3 3.3 convert_reduce_fusion.21
  1095.8 6.9 convolution_add_fusion.3
  1107.8 16.6 %reduce-scatter.52.cloned.1.call-done = bf16[1,128,1152]{2,1,0:T(8,128)(2,1)} async-done(((bf16[1,512,1152]{2,1,0:T(8,128)(2,1)}), bf16[1,128,1152]{2,1,0:T(8,128)(2,1)}) %reduce-scatter.52.cloned.1.call-update) | async-done | bytes 294928 | tf_op jit(solution)/shard_map/reduce_scatter | solution.py:44
  1130.9 6.7 fusion
  1138.8 5.0 fusion.161
  1146.6 4.4 fusion.1
  1159.0 3.4 fusion.144
  1164.3 3.4 add_convert_fusion.1
  1168.5 23.3 %reduce-scatter.62.cloned.1.call-done = f32[1728,1]{1,0:T(8,128)} async-done(((f32[6912,1]{1,0:T(8,128)}), f32[1728,1]{1,0:T(8,128)}) %reduce-scatter.62.cloned.1.call-update) | async-done | bytes 6928
  1193.2 67.6 %reduce-scatter.64.cloned.1.call-done = f32[1728,1]{1,0:T(8,128)} async-done(((f32[6912,1]{1,0:T(8,128)}), f32[1728,1]{1,0:T(8,128)}) %reduce-scatter.64.cloned.1.call-update) | async-done | bytes 6928
  1262.3 67.6 %reduce-scatter.66.cloned.1.call-done = f32[1728,1]{1,0:T(8,128)} async-done(((f32[6912,1]{1,0:T(8,128)}), f32[1728,1]{1,0:T(8,128)}) %reduce-scatter.66.cloned.1.call-update) | async-done | bytes 6928
  1349.7 17.4 %reduce-scatter.58.cloned.1.call-done = bf16[288,1152]{1,0:T(8,128)(2,1)} async-done(((bf16[1152,1152]{1,0:T(8,128)(2,1)}), bf16[288,1152]{1,0:T(8,128)(2,1)}) %reduce-scatter.58.cloned.1.call-update) | async-done | bytes 663568 | tf_op jit(solution)/shard_map/reduce_scatter | solution.py:71
  1369.4 35.1 %reduce-scatter.60.cloned.1.call-done = bf16[1152,288]{0,1:T(8,128)(2,1)} async-done(((bf16[1152,1152]{0,1:T(8,128)(2,1)}), bf16[1152,288]{0,1:T(8,128)(2,1)}) %reduce-scatter.60.cloned.1.call-update) | async-done | bytes 663568 | tf_op jit(solution)/shard_map/reduce_scatter | solution.py:74
  1406.7 24.7 %reduce-scatter.68.cloned.1.call-done = bf16[288,288]{1,0:T(8,128)(2,1)} async-done(((bf16[1152,288]{1,0:T(8,128)(2,1)}), bf16[288,288]{1,0:T(8,128)(2,1)}) %reduce-scatter.68.cloned.1.call-update) | async-done | bytes 165904
  1434.8 10.5 all-reduce.9
  1447.2 3.4 fusion.203
  1450.7 21.9 %psum.7 = f32[2,1,1152]{2,1,0:T(1,128)} all-reduce(f32[2,1,1152]{2,1,0:T(1,128)S(1)} %multiply_add_fusion), channel_id=1, replica_groups=mesh['section'=2,'dp'=4,'mp'=4] {'section','mp'}, use_global_device_ids=true, to_apply=%region_78.79 | all-reduce | flops 2304 | bytes 18432 | tf_op jit(solution)/shard_map/psum | solution.py:437
  1476.1 39.0 %reduce-scatter.54.cloned.1.call-done = bf16[288,1728]{1,0:T(8,128)(2,1)} async-done(((bf16[1152,1728]{1,0:T(8,128)(2,1)}), bf16[288,1728]{1,0:T(8,128)(2,1)}) %reduce-scatter.54.cloned.1.call-update) | async-done | bytes 995344 | tf_op jit(solution)/shard_map/reduce_scatter | solution.py:62
  (505 shorter events, 211.2 us)
Async XLA Ops:
  7.2 37.7 %all-gather.49.cloned.1.call-start = ((), (), s32[]{:S(2)}) async-start(), calls=%async_computation.48 | async-start | bytes 5160960 | tf_op jit(solution)/shard_map/all_gather | solution.py:360
  7.9 77.2 %all-reduce.12.cloned.1.call-start = ((), (), s32[]{:S(2)}) async-start(), calls=%async_computation.56 | async-start | bytes 172032
  49.8 37.1 %copy-start.83 = (bf16[1,2,288]{2,1,0:T(2,128)(2,1)S(1)}, bf16[1,2,288]{2,1,0:T(2,128)(2,1)}, u32[]{:S(2)}) copy-start(bf16[1,2,288]{2,1,0:T(2,128)(2,1)} %param.19) | copy-start | bytes 3460
  49.8 37.1 %copy-start.62 = (bf16[1,288,288]{2,1,0:T(8,128)(2,1)S(1)}, bf16[1,288,288]{2,1,0:T(8,128)(2,1)}, u32[]{:S(2)}) copy-start(bf16[1,288,288]{2,1,0:T(8,128)(2,1)} %param.20) | copy-start | bytes 497668
  50.6 70.7 %all-gather.51.cloned.1.call-start = ((), (), s32[]{:S(2)}) async-start(), calls=%async_computation.49 | async-start | bytes 4423680 | tf_op jit(solution)/shard_map/all_gather | solution.py:361
  52.0 100.8 %all-gather.25.cloned.1.call-start = ((), (), s32[]{:S(2)}) async-start(), calls=%async_computation.20 | async-start | bytes 1474560 | tf_op jit(solution)/shard_map/all_gather | solution.py:32
  86.9 121.3 %reduce-scatter.30.cloned.1.call-start = ((), (), s32[]{:S(2)}) async-start(), calls=%async_computation.21 | async-start | bytes 2949120 | tf_op jit(solution)/shard_map/reduce_scatter | solution.py:36
  161.0 50.5 %copy-start.80 = (bf16[1,1152]{1,0:T(2,128)(2,1)S(1)}, bf16[1,1152]{1,0:T(2,128)(2,1)}, u32[]{:S(2)}) copy-start(bf16[1,1152]{1,0:T(2,128)(2,1)} %param.23) | copy-start | bytes 6916
  161.1 73.6 %all-gather.53.cloned.1.call-start = ((), (), s32[]{:S(2)}) async-start(), calls=%async_computation.50 | async-start | bytes 3317760 | tf_op jit(solution)/shard_map/all_gather | solution.py:363
  161.6 105.5 %all-gather.27.cloned.1.call-start = ((), (), s32[]{:S(2)}) async-start(), calls=%async_computation.22 | async-start | bytes 1474560 | tf_op jit(solution)/shard_map/all_gather | solution.py:32
  210.5 83.1 %all-gather.55.cloned.1.call-start = ((), (), s32[]{:S(2)}) async-start(), calls=%async_computation.51 | async-start | bytes 3317760 | tf_op jit(solution)/shard_map/all_gather | solution.py:364
  211.3 136.3 %reduce-scatter.32.cloned.1.call-start = ((), (), s32[]{:S(2)}) async-start(), calls=%async_computation.23 | async-start | bytes 2949120 | tf_op jit(solution)/shard_map/reduce_scatter | solution.py:36
  299.7 50.3 %copy-start.65 = (f32[6912]{0:T(1024)S(1)}, f32[6912]{0:T(1024)}, u32[]{:S(2)}) copy-start(f32[6912]{0:T(1024)} %get-tuple-element.193) | copy-start | bytes 82948
  299.7 90.8 %all-gather.29.cloned.1.call-start = ((), (), s32[]{:S(2)}) async-start(), calls=%async_computation.24 | async-start | bytes 1474560 | tf_op jit(solution)/shard_map/all_gather | solution.py:32
  348.7 10.3 collective-permute-start
  360.4 85.4 %reduce-scatter.34.cloned.1.call-start = ((), (), s32[]{:S(2)}) async-start(), calls=%async_computation.25 | async-start | bytes 2949120 | tf_op jit(solution)/shard_map/reduce_scatter | solution.py:36
  398.7 79.4 %all-gather.31.cloned.1.call-start = ((), (), s32[]{:S(2)}) async-start(), calls=%async_computation.26 | async-start | bytes 1474560 | tf_op jit(solution)/shard_map/all_gather | solution.py:32
  448.3 61.5 %all-gather.37.cloned.1.call-start = ((), (), s32[]{:S(2)}) async-start(), calls=%async_computation.32 | async-start | bytes 1474560 | tf_op jit(solution)/shard_map/all_gather | solution.py:40
  450.3 98.4 %reduce-scatter.42.cloned.1.call-start = ((), (), s32[]{:S(2)}) async-start(), calls=%async_computation.33 | async-start | bytes 1474560 | tf_op jit(solution)/shard_map/reduce_scatter | solution.py:44
  509.8 7.2 copy-start.84
  520.0 77.2 %reduce-scatter.36.cloned.1.call-start = ((), (), s32[]{:S(2)}) async-start(), calls=%async_computation.27 | async-start | bytes 2949120 | tf_op jit(solution)/shard_map/reduce_scatter | solution.py:36
  526.1 102.2 %all-gather.39.cloned.1.call-start = ((), (), s32[]{:S(2)}) async-start(), calls=%async_computation.34 | async-start | bytes 1474560 | tf_op jit(solution)/shard_map/all_gather | solution.py:40
  553.6 106.2 %all-gather.33.cloned.1.call-start = ((), (), s32[]{:S(2)}) async-start(), calls=%async_computation.28 | async-start | bytes 1474560 | tf_op jit(solution)/shard_map/all_gather | solution.py:32
  599.1 10.2 collective-permute-start.1
  610.5 54.5 %copy-start.6 = (bf16[1,128,1152]{2,1,0:T(8,128)(2,1)}, bf16[1,128,1152]{2,1,0:T(8,128)(2,1)S(1)}, u32[]{:S(2)}) copy-start(bf16[1,128,1152]{2,1,0:T(8,128)(2,1)S(1)} %get-tuple-element.205) | copy-start | bytes 884740
  611.9 90.9 %reduce-scatter.44.cloned.1.call-start = ((), (), s32[]{:S(2)}) async-start(), calls=%async_computation.35 | async-start | bytes 1474560 | tf_op jit(solution)/shard_map/reduce_scatter | solution.py:44
  674.1 77.3 %reduce-scatter.38.cloned.1.call-start = ((), (), s32[]{:S(2)}) async-start(), calls=%async_computation.29 | async-start | bytes 2949120 | tf_op jit(solution)/shard_map/reduce_scatter | solution.py:36
  680.5 103.3 %all-gather.35.cloned.1.call-start = ((), (), s32[]{:S(2)}) async-start(), calls=%async_computation.30 | async-start | bytes 1474560 | tf_op jit(solution)/shard_map/all_gather | solution.py:32
  681.4 70.0 %copy-start.7 = (bf16[1,128,1152]{2,1,0:T(8,128)(2,1)}, bf16[1,128,1152]{2,1,0:T(8,128)(2,1)S(1)}, u32[]{:S(2)}) copy-start(bf16[1,128,1152]{2,1,0:T(8,128)(2,1)S(1)} %get-tuple-element.211) | copy-start | bytes 884740
  754.0 13.0 copy-start.14
  754.0 61.5 %all-gather.41.cloned.1.call-start = ((), (), s32[]{:S(2)}) async-start(), calls=%async_computation.36 | async-start | bytes 1474560 | tf_op jit(solution)/shard_map/all_gather | solution.py:40
  757.9 8.3 collective-permute-start.2
  767.8 86.0 %reduce-scatter.46.cloned.1.call-start = ((), (), s32[]{:S(2)}) async-start(), calls=%async_computation.37 | async-start | bytes 1474560 | tf_op jit(solution)/shard_map/reduce_scatter | solution.py:44
  815.5 6.6 copy-start.85
  825.1 62.5 %all-gather.43.cloned.1.call-start = ((), (), s32[]{:S(2)}) async-start(), calls=%async_computation.38 | async-start | bytes 1474560 | tf_op jit(solution)/shard_map/all_gather | solution.py:40
  858.6 72.3 %copy-start.13 = (f32[1,128,1152]{2,1,0:T(8,128)}, f32[1,128,1152]{2,1,0:T(8,128)S(1)}, u32[]{:S(2)}) copy-start(f32[1,128,1152]{2,1,0:T(8,128)S(1)} %get-tuple-element.213) | copy-start | bytes 1769476
  858.6 69.5 %reduce-scatter.48.cloned.1.call-start = ((), (), s32[]{:S(2)}) async-start(), calls=%async_computation.39 | async-start | bytes 1474560 | tf_op jit(solution)/shard_map/reduce_scatter | solution.py:44
  899.4 77.3 %reduce-scatter.40.cloned.1.call-start = ((), (), s32[]{:S(2)}) async-start(), calls=%async_computation.31 | async-start | bytes 2949120 | tf_op jit(solution)/shard_map/reduce_scatter | solution.py:36
  905.5 22.6 %copy-start.20 = (bf16[1,128,1152]{2,1,0:T(8,128)(2,1)S(1)}, bf16[1,128,1152]{2,1,0:T(8,128)(2,1)}, u32[]{:S(2)}) copy-start(bf16[1,128,1152]{2,1,0:T(8,128)(2,1)} %get-tuple-element.210) | copy-start | bytes 884740
  905.5 103.7 %all-gather.45.cloned.1.call-start = ((), (), s32[]{:S(2)}) async-start(), calls=%async_computation.40 | async-start | bytes 1474560 | tf_op jit(solution)/shard_map/all_gather | solution.py:40
  929.4 47.4 %copy-start.15 = (bf16[2,1,128,1152]{3,2,1,0:T(8,128)(2,1)S(1)}, bf16[2,1,128,1152]{3,2,1,0:T(8,128)(2,1)}, u32[]{:S(2)}) copy-start(bf16[2,1,128,1152]{3,2,1,0:T(8,128)(2,1)} %param.15) | copy-start | bytes 1769476
  934.2 42.6 %collective-permute-start.3 = (bf16[1,128,1152]{2,1,0:T(8,128)(2,1)S(1)}, bf16[1,128,1152]{2,1,0:T(8,128)(2,1)S(1)}, u32[]{:S(2)}, u32[]{:S(2)}) collective-permute-start(bf16[1,128,1152]{2,1,0:T(8,128)(2,1)S(1)} %convert_element_type.784), channel_id=1, source_target_pairs={{16,0},{17,1},{18,2},{19,3},{20,4},{21,5},{22,6},{23,7},{24,8},{25... | collective-permute-start | bytes 884744 | tf_op jit(solution)/shard_map/ppermute | solution.py:12
  976.7 38.2 %copy-start.30 = (bf16[1,128,1152]{2,1,0:T(8,128)(2,1)}, bf16[1,128,1152]{2,1,0:T(8,128)(2,1)S(1)}, u32[]{:S(2)}) copy-start(bf16[1,128,1152]{2,1,0:T(8,128)(2,1)S(1)} %collective-permute-done.3) | copy-start | bytes 884740
  979.5 68.1 %reduce-scatter.50.cloned.1.call-start = ((), (), s32[]{:S(2)}) async-start(), calls=%async_computation.41 | async-start | bytes 1474560 | tf_op jit(solution)/shard_map/reduce_scatter | solution.py:44
  1009.3 6.7 copy-start.86
  1018.9 64.5 %all-gather.47.cloned.1.call-start = ((), (), s32[]{:S(2)}) async-start(), calls=%async_computation.42 | async-start | bytes 1474560 | tf_op jit(solution)/shard_map/all_gather | solution.py:40
  1054.4 70.1 %reduce-scatter.52.cloned.1.call-start = ((), (), s32[]{:S(2)}) async-start(), calls=%async_computation.43 | async-start | bytes 1474560 | tf_op jit(solution)/shard_map/reduce_scatter | solution.py:44
  1054.4 5.8 copy-start.42
  1095.7 96.0 %reduce-scatter.62.cloned.1.call-start = ((), (), s32[]{:S(2)}) async-start(), calls=%async_computation.52 | async-start | bytes 4423680
  1105.2 155.6 %reduce-scatter.64.cloned.1.call-start = ((), (), s32[]{:S(2)}) async-start(), calls=%async_computation.53 | async-start | bytes 4423680
  1107.8 222.0 %reduce-scatter.66.cloned.1.call-start = ((), (), s32[]{:S(2)}) async-start(), calls=%async_computation.54 | async-start | bytes 4423680
  1129.6 237.5 %reduce-scatter.58.cloned.1.call-start = ((), (), s32[]{:S(2)}) async-start(), calls=%async_computation.46 | async-start | bytes 3317760 | tf_op jit(solution)/shard_map/reduce_scatter | solution.py:71
  1137.6 6.2 copy-start.34
  1137.6 266.9 %reduce-scatter.60.cloned.1.call-start = ((), (), s32[]{:S(2)}) async-start(), calls=%async_computation.47 | async-start | bytes 3317760 | tf_op jit(solution)/shard_map/reduce_scatter | solution.py:74
  1138.8 5.0 copy-start.94
  1151.1 280.4 %reduce-scatter.68.cloned.1.call-start = ((), (), s32[]{:S(2)}) async-start(), calls=%async_computation.55 | async-start | bytes 1105920
  1158.7 315.2 %reduce-scatter.56.cloned.1.call-start = ((), (), s32[]{:S(2)}) async-start(), calls=%async_computation.45 | async-start | bytes 3317760 | tf_op jit(solution)/shard_map/reduce_scatter | solution.py:65
  1167.8 347.3 %reduce-scatter.54.cloned.1.call-start = ((), (), s32[]{:S(2)}) async-start(), calls=%async_computation.44 | async-start | bytes 5160960 | tf_op jit(solution)/shard_map/reduce_scatter | solution.py:62
  1337.7 5.4 copy-start.74
  1349.7 83.6 %copy-start.12 = (f32[1,128,1152]{2,1,0:T(8,128)S(1)}, f32[1,128,1152]{2,1,0:T(8,128)}, u32[]{:S(2)}) copy-start(f32[1,128,1152]{2,1,0:T(8,128)} %copy-done.11) | copy-start | bytes 1769476
  1349.7 83.6 %copy-start.17 = (f32[1,128,1152]{2,1,0:T(8,128)S(1)}, f32[1,128,1152]{2,1,0:T(8,128)}, u32[]{:S(2)}) copy-start(f32[1,128,1152]{2,1,0:T(8,128)} %copy-done.16) | copy-start | bytes 1769476
  1349.7 83.6 %copy-start.22 = (bf16[1,128,1152]{2,1,0:T(8,128)(2,1)S(1)}, bf16[1,128,1152]{2,1,0:T(8,128)(2,1)}, u32[]{:S(2)}) copy-start(bf16[1,128,1152]{2,1,0:T(8,128)(2,1)} %reduce-scatter.52.cloned.1.call-done) | copy-start | bytes 884740
  1369.4 64.3 %copy-start.23 = (f32[1,1,128,1152]{3,2,1,0:T(8,128)S(1)}, f32[1,1,128,1152]{3,2,1,0:T(8,128)}, u32[]{:S(2)}) copy-start(f32[1,1,128,1152]{3,2,1,0:T(8,128)} %get-tuple-element.201) | copy-start | bytes 1769476
  1434.8 15.7 %copy-start.70 = (f32[1152]{0:T(1024)S(1)}, f32[1152]{0:T(1024)}, u32[]{:S(2)}) copy-start(f32[1152]{0:T(1024)} %copy-done.69) | copy-start | bytes 13828
  (73 other events, 157.9 us)
Sparse Core Ops, SparseCore 0:
  9.5 35.2 all-gather.48
  50.7 34.3 all-reduce.11
  87.2 34.0 all-gather.50
  123.3 29.4 all-gather.24
  161.2 46.9 reduce-scatter.29
  209.5 25.0 all-gather.52
  236.8 30.2 all-gather.26
  268.7 24.9 all-gather.54
  299.8 47.6 reduce-scatter.31
  360.5 29.9 all-gather.28
  398.8 46.9 reduce-scatter.33
  448.5 29.6 all-gather.30
  480.3 29.4 all-gather.36
  520.1 28.5 reduce-scatter.41
  550.8 46.2 reduce-scatter.35
  598.6 29.6 all-gather.38
  630.3 29.4 all-gather.32
  674.2 28.5 reduce-scatter.43
  705.1 46.2 reduce-scatter.37
  754.1 29.6 all-gather.34
  786.0 29.4 all-gather.40
  825.2 28.5 reduce-scatter.45
  858.7 28.8 all-gather.42
  899.5 28.5 reduce-scatter.47
  930.4 46.2 reduce-scatter.39
  979.6 29.6 all-gather.44
  1019.0 28.5 reduce-scatter.49
  1054.5 28.8 all-gather.46
  1095.9 28.5 reduce-scatter.51
  1126.6 65.0 reduce-scatter.61
  1194.1 66.6 reduce-scatter.63
  1263.1 66.6 reduce-scatter.65
  1332.2 34.8 reduce-scatter.57
  1369.7 34.7 reduce-scatter.59
  1407.6 23.8 reduce-scatter.67
  1433.8 34.6 reduce-scatter.55
  1470.9 44.1 reduce-scatter.53
where the time goes:
time: 1540 us; the launch traced here: 1520 us
  waiting for transfers between devices  1130 us (73%)
  matrix products  175 us (11%)
  other arithmetic  83.7 us (5%)
  local copies, waits for them, and re-layouts  53.4 us (3%)
  blocking collectives  50.8 us (3%)
  between operations  19 us (1%)
    reduce_scatter x6, waiting for transfers between devices, reduce_tokens(): return lax.psum_scatter(partial_rows, 'mp', scatter_dimension=1, tiled=True)  272 us
    unnamed x42, waiting for transfers between devices  218 us
    all_gather x6, waiting for transfers between devices, gather_tokens(): return lax.all_gather(local_rows, 'mp', axis=1, tiled=True)  159 us
    all_gather x6, waiting for transfers between devices, gather_cotangent(): return lax.all_gather(local_rows, 'mp', axis=1, tiled=True)  141 us
    reduce_scatter x6, waiting for transfers between devices, reduce_cotangent(): lax.psum_scatter(partial_rows.astype(jnp.bfloat16), 'mp', scatter_dimensi...  140 us
    reduce_scatter x1, waiting for transfers between devices, scatter_grads(): lax.psum_scatter(grad_w_ada.astype(jnp.bfloat16), 'dp', scatter_dimension...  39 us
    reduce_scatter x1, waiting for transfers between devices, scatter_grads(): lax.psum_scatter(grad_w_fc2.astype(jnp.bfloat16), 'dp', scatter_dimension...  35.1 us
    unnamed x222, local copies, waits for them, and re-layouts  34.6 us
  transfers between devices with their start and end apart: 41, of which 39 were waited for; matrix products, arithmetic and copies ran while one was open for 12% of the time, Pallas kernels for 0%

commit v1 on v0

v1 whole, which is shorter than its diff:
```python
import functools

import jax
import jax.numpy as jnp
from jax import lax
from jax.experimental import pallas as pl
from jax.experimental.pallas import tpu as pltpu
from jax.sharding import Mesh
from jax.sharding import PartitionSpec as P

HEAD_SIZE = 72
EPS = 1e-06
MESH = pl.DeviceIdType.MESH
BF16 = jnp.bfloat16
F32 = jnp.float32
GELU_C = 0.7978845608028654
GELU_A = 0.044715
NT = (((1,), (1,)), ((), ()))
TN = (((0,), (0,)), ((), ()))
GROUP = ("section", "ml")
OTHERS = ("mh", "dp")
VMEM_LIMIT = 60 * 1024 * 1024


def dot_nn(a, b):
    return jnp.dot(a, b, preferred_element_type=F32)


def dot_nt(a, b):
    return lax.dot_general(a, b, NT, preferred_element_type=F32)


def dot_tn(a, b):
    return lax.dot_general(a, b, TN, preferred_element_type=F32)


def norm_parts(values):
    center = values - jnp.mean(values, axis=-1, keepdims=True)
    spread = jnp.mean(center * center, axis=-1, keepdims=True)
    rstd = lax.rsqrt(spread + EPS)
    return center * rstd, rstd


def norm_back(grad, normed, rstd, scale):
    dn = grad * (1.0 + scale)
    first = jnp.mean(dn, axis=-1, keepdims=True)
    second = jnp.mean(dn * normed, axis=-1, keepdims=True)
    return (dn - first - normed * second) * rstd


def col_sum(values):
    return jnp.sum(values, axis=0, keepdims=True)


class Group:
    def __init__(self):
        self.low = lax.axis_size("ml")
        self.size = lax.axis_size("section") * self.low
        self.me = lax.axis_index("section") * self.low + lax.axis_index("ml")

    def device(self, member):
        return (
            lax.div(member, self.low),
            lax.axis_index("dp"),
            lax.axis_index("mh"),
            lax.rem(member, self.low),
        )

    def peer(self, step):
        return lax.rem(self.me + step, self.size)

    def enter(self):
        barrier = pltpu.get_barrier_semaphore()
        for step in range(1, self.size):
            pl.semaphore_signal(
                barrier, inc=1, device_id=self.device(self.peer(step)), device_id_type=MESH
            )
        pl.semaphore_wait(barrier, self.size - 1)

    def copy(self, src, dst, send_sem, recv_sem, member):
        return pltpu.make_async_remote_copy(
            src_ref=src,
            dst_ref=dst,
            send_sem=send_sem,
            recv_sem=recv_sem,
            device_id=self.device(member),
            device_id_type=MESH,
        )

    def spread(self, buf, send_sem, recv_sem):
        me = self.me
        for step in range(1, self.size):
            self.copy(
                buf.at[me], buf.at[me], send_sem.at[step], recv_sem.at[me], self.peer(step)
            ).start()

    def spread_wait(self, buf, send_sem, recv_sem, member):
        self.copy(buf.at[member], buf.at[member], send_sem.at[1], recv_sem.at[member], member).wait_recv()

    def spread_sent(self, buf, send_sem, recv_sem):
        me = self.me
        for step in range(1, self.size):
            self.copy(
                buf.at[me], buf.at[me], send_sem.at[step], recv_sem.at[me], self.peer(step)
            ).wait_send()

    def reduce_copy(self, stage, landing, send_sem, recv_sem, member):
        return self.copy(
            stage.at[member], landing.at[self.me], send_sem.at[member], recv_sem.at[self.me], member
        )

    def reduce_wait(self, landing, send_sem, recv_sem, member):
        self.copy(
            landing.at[member], landing.at[member], send_sem.at[member], recv_sem.at[member], member
        ).wait_recv()

    def landed_sum(self, own, stage, landing, send_sem, recv_sem):
        total = own
        for step in range(1, self.size):
            member = self.peer(step)
            self.reduce_wait(landing, send_sem, recv_sem, member)
            total = total + landing[member].astype(F32)
        for step in range(1, self.size):
            self.reduce_copy(stage, landing, send_sem, recv_sem, self.peer(step)).wait_send()
        return total


def load_rows(src, dst, sems, chunk):
    copies = []
    for part in range(src.shape[0]):
        copies.append(
            pltpu.make_async_copy(src.at[part], dst.at[pl.ds(part * chunk, chunk)], sems.at[part])
        )
    return copies


def load_stack(src, dst, sems, chunk):
    copies = []
    for part in range(src.shape[0]):
        copies.append(
            pltpu.make_async_copy(
                src.at[part], dst.at[:, pl.ds(part * chunk, chunk), :], sems.at[part]
            )
        )
    return copies


def lane_mask(shape, head):
    lanes = lax.broadcasted_iota(jnp.int32, shape, len(shape) - 1)
    return (lanes >= head * HEAD_SIZE) & (lanes < (head + 1) * HEAD_SIZE)


def row_mask(shape, head):
    rows = lax.broadcasted_iota(jnp.int32, shape, 0)
    return (rows >= head * HEAD_SIZE) & (rows < (head + 1) * HEAD_SIZE)


def stack_heads(block):
    heads = block.shape[-1] // HEAD_SIZE
    zero = jnp.zeros_like(block)
    return jnp.concatenate(
        [jnp.where(lane_mask(block.shape, head), block, zero) for head in range(heads)], axis=0
    )


def identity(size):
    rows = lax.broadcasted_iota(jnp.int32, (size, size), 0)
    cols = lax.broadcasted_iota(jnp.int32, (size, size), 1)
    return jnp.where(rows == cols, 1.0, 0.0).astype(BF16)


def att_fwd_kernel(
    hidden_ref, mod_ref, bias_ref, bproj_ref, w_ref,
    middle_ref, normed_ref, proj_ref, att_ref, branch_ref,
    w_buf, stage, landing, w_sem, ag_send, ag_recv, rs_send, rs_recv,
):
    group = Group()
    me, size = group.me, group.size
    tokens, width = hidden_ref.shape
    heads = att_ref.shape[-1] // HEAD_SIZE
    loads = load_stack(w_ref, w_buf, w_sem, w_ref.shape[2])
    for copy in loads:
        copy.start()
    hidden = hidden_ref[...].astype(F32)
    normed, _ = norm_parts(hidden)
    normed_ref[me] = (normed * (1.0 + mod_ref[1:2]) + mod_ref[0:1]).astype(BF16)
    group.enter()
    group.spread(normed_ref, ag_send, ag_recv)
    for copy in loads:
        copy.wait()

    def project(step, carry):
        member = group.peer(step)

        @pl.when(step > 0)
        def _():
            group.spread_wait(normed_ref, ag_send, ag_recv, member)

        rows = normed_ref[member]
        for part in range(3):
            out = dot_nn(rows, w_buf[part]) + bias_ref[part]
            proj_ref[part, member] = out.astype(BF16)
        return carry

    lax.fori_loop(0, size, project, 0)
    seq = size * tokens
    keys = proj_ref[1].reshape(seq, -1)
    values = proj_ref[2].reshape(seq, -1)

    def attend(member):
        stacked = stack_heads(proj_ref[0, member])
        powered = jnp.exp(dot_nt(stacked, keys) * HEAD_SIZE**-0.5)
        probs = powered * (1.0 / jnp.sum(powered, axis=-1, keepdims=True))
        mixed = dot_nn(probs.astype(BF16), values)
        out = mixed[:tokens]
        for head in range(1, heads):
            part = mixed[head * tokens : (head + 1) * tokens]
            out = jnp.where(lane_mask(part.shape, head), part, out)
        low = out.astype(BF16)
        att_ref[member] = low
        return dot_nt(low, w_buf[3])

    def send(step, carry):
        member = group.peer(step)
        stage[member] = attend(member).astype(BF16)
        group.reduce_copy(stage, landing, rs_send, rs_recv, member).start()
        return carry

    lax.fori_loop(1, size, send, 0)
    own = attend(me)
    group.spread_sent(normed_ref, ag_send, ag_recv)
    branch = group.landed_sum(own, stage, landing, rs_send, rs_recv) + bproj_ref[...]
    branch_ref[...] = branch
    middle_ref[...] = hidden_ref[...].astype(F32) + mod_ref[2:3] * branch


def mlp_fwd_kernel(
    middle_ref, mod_ref, b1_ref, b2_ref, w1_ref, w2_ref,
    out_ref, normed_ref, pre_ref, gelu_ref, branch_ref,
    w1_buf, w2_buf, stage, landing, w1_sem, w2_sem, ag_send, ag_recv, rs_send, rs_recv,
):
    group = Group()
    me, size = group.me, group.size
    loads = load_rows(w1_ref, w1_buf, w1_sem, w1_ref.shape[1]) + load_rows(
        w2_ref, w2_buf, w2_sem, w2_ref.shape[1]
    )
    for copy in loads:
        copy.start()
    normed, _ = norm_parts(middle_ref[...])
    normed_ref[me] = (normed * (1.0 + mod_ref[4:5]) + mod_ref[3:4]).astype(BF16)
    group.enter()
    group.spread(normed_ref, ag_send, ag_recv)
    for copy in loads:
        copy.wait()

    def dense(member):
        pre = dot_nn(normed_ref[member], w1_buf[...]) + b1_ref[...]
        pre_ref[member] = pre
        bent = jnp.tanh(GELU_C * (pre + GELU_A * pre * pre * pre))
        low = (0.5 * pre * (1.0 + bent)).astype(BF16)
        gelu_ref[member] = low
        return dot_nt(low, w2_buf[...])

    own = dense(me)

    def send(step, carry):
        member = group.peer(step)
        group.spread_wait(normed_ref, ag_send, ag_recv, member)
        stage[member] = dense(member).astype(BF16)
        group.reduce_copy(stage, landing, rs_send, rs_recv, member).start()
        return carry

    stage[me] = own.astype(BF16)
    lax.fori_loop(1, size, send, 0)
    group.spread_sent(normed_ref, ag_send, ag_recv)
    own = stage[me].astype(F32)
    branch = group.landed_sum(own, stage, landing, rs_send, rs_recv) + b2_ref[...]
    branch_ref[...] = branch
    out_ref[...] = (middle_ref[...] + mod_ref[5:6] * branch).astype(BF16)


def weight_grad(lhs_ref, rhs, out_ref, tile):
    def body(index, carry):
        cols = pl.ds(pl.multiple_of(index * tile, tile), tile)
        out_ref[cols, :] = dot_tn(lhs_ref[:, cols], rhs).astype(BF16)
        return carry

    lax.fori_loop(0, lhs_ref.shape[-1] // tile, body, 0)


def mlp_bwd_kernel(
    grad_ref, middle_ref, mod_ref, branch_ref, normed_ref, pre_ref, gelu_ref, w1_ref, w2_ref,
    gmid_ref, dw1_ref, dw2_ref, db1_ref, db2_ref, dmod_ref,
    w1_buf, w2_buf, dbr, dpre, stage, landing, w1_sem, w2_sem, ag_send, ag_recv, rs_send, rs_recv,
):
    group = Group()
    me, size = group.me, group.size
    tokens, width = grad_ref.shape
    loads = load_rows(w1_ref, w1_buf, w1_sem, w1_ref.shape[1]) + load_rows(
        w2_ref, w2_buf, w2_sem, w2_ref.shape[1]
    )
    for copy in loads:
        copy.start()
    grad = grad_ref[...].astype(F32)
    dbr[me] = (grad * mod_ref[5:6]).astype(BF16)
    group.enter()
    group.spread(dbr, ag_send, ag_recv)
    dmod_ref[2:3] = col_sum(grad * branch_ref[...])
    for copy in loads:
        copy.wait()

    def back(member):
        dgelu = dot_nn(dbr[member], w2_buf[...])
        pre = pre_ref[member]
        bent = jnp.tanh(GELU_C * (pre + GELU_A * pre * pre * pre))
        slope = 0.5 * (1.0 + bent) + 0.5 * pre * (1.0 - bent * bent) * (
            GELU_C * (1.0 + 3.0 * GELU_A * pre * pre)
        )
        low = (dgelu * slope).astype(BF16)
        dpre[member] = low
        return dot_nt(low, w1_buf[...])

    stage[me] = back(me).astype(BF16)

    def send(step, carry):
        member = group.peer(step)
        group.spread_wait(dbr, ag_send, ag_recv, member)
        stage[member] = back(member).astype(BF16)
        group.reduce_copy(stage, landing, rs_send, rs_recv, member).start()
        return carry

    lax.fori_loop(1, size, send, 0)
    seq = size * tokens
    dpre_all = dpre[...].reshape(seq, -1)
    gelu_all = gelu_ref[...].reshape(seq, -1)
    db1_ref[...] = col_sum(dpre_all.astype(F32))
    db2_ref[...] = col_sum(dbr[...].reshape(seq, -1).astype(F32))
    weight_grad(normed_ref.reshape(seq, width), dpre_all, dw1_ref, 128)
    weight_grad(dbr.reshape(seq, width), gelu_all, dw2_ref, 128)
    group.spread_sent(dbr, ag_send, ag_recv)
    total = group.landed_sum(stage[me].astype(F32), stage, landing, rs_send, rs_recv)
    normed, rstd = norm_parts(middle_ref[...])
    dmod_ref[0:1] = col_sum(total)
    dmod_ref[1:2] = col_sum(total * normed)
    gmid_ref[...] = norm_back(total, normed, rstd, mod_ref[4:5]) + grad_ref[...].astype(F32)


def att_bwd_kernel(
    gmid_ref, hidden_ref, mod_ref, branch_ref, normed_ref, proj_ref, att_ref, w_ref,
    gin_ref, dw_ref, dbqkv_ref, dbproj_ref, dmod_ref,
    w_buf, dba, dproj, dkey, dval, stage, landing, w_sem, ag_send, ag_recv, rs_send, rs_recv,
):
    group = Group()
    me, size = group.me, group.size
    tokens, width = gmid_ref.shape
    seq = size * tokens
    part_width = att_ref.shape[-1]
    heads = part_width // HEAD_SIZE
    loads = load_stack(w_ref, w_buf, w_sem, w_ref.shape[2])
    for copy in loads:
        copy.start()
    gmid = gmid_ref[...]
    dba[me] = (gmid * mod_ref[2:3]).astype(BF16)
    group.enter()
    group.spread(dba, ag_send, ag_recv)
    dmod_ref[2:3] = col_sum(gmid * branch_ref[...])
    keys = proj_ref[1].reshape(seq, part_width)
    values = proj_ref[2].reshape(seq, part_width)
    keys_t = dot_nt(identity(part_width), keys).astype(BF16)
    dkey[...] = jnp.zeros_like(dkey)
    dval[...] = jnp.zeros_like(dval)
    for copy in loads:
        copy.wait()

    def back(step, carry):
        member = group.peer(step)

        @pl.when(step > 0)
        def _():
            group.spread_wait(dba, ag_send, ag_recv, member)

        datt = dot_nn(dba[member], w_buf[3]).astype(BF16)
        datt_st = stack_heads(datt)
        query_st = stack_heads(proj_ref[0, member])
        powered = jnp.exp(dot_nt(keys, query_st) * HEAD_SIZE**-0.5)
        probs = powered * (1.0 / jnp.sum(powered, axis=0, keepdims=True))
        dval[...] += dot_nn(probs.astype(BF16), datt_st)
        dprobs = dot_nt(values, datt_st)
        dscore = (probs * (dprobs - jnp.sum(probs * dprobs, axis=0, keepdims=True))).astype(BF16)
        dkey[...] += dot_nn(dscore, query_st)
        dq_t = dot_nn(keys_t, dscore)
        picked = dq_t[:, :tokens]
        for head in range(1, heads):
            part = dq_t[:, head * tokens : (head + 1) * tokens]
            picked = jnp.where(row_mask(part.shape, head), part, picked)
        low = (picked * HEAD_SIZE**-0.5).astype(BF16)
        dproj[0, member] = dot_nt(identity(tokens), low).astype(BF16)
        return carry

    lax.fori_loop(0, size, back, 0)
    for member in range(size):
        rows = slice(member * tokens, (member + 1) * tokens)
        dproj[1, member] = (dkey[rows] * HEAD_SIZE**-0.5).astype(BF16)
        dproj[2, member] = dval[rows].astype(BF16)

    def partial_rows(member):
        total = dot_nt(dproj[0, member], w_buf[0])
        total += dot_nt(dproj[1, member], w_buf[1])
        return total + dot_nt(dproj[2, member], w_buf[2])

    def send(step, carry):
        member = group.peer(step)
        stage[member] = partial_rows(member).astype(BF16)
        group.reduce_copy(stage, landing, rs_send, rs_recv, member).start()
        return carry

    lax.fori_loop(1, size, send, 0)
    stage[me] = partial_rows(me).astype(BF16)
    for part in range(3):
        grads = dproj[part].reshape(seq, part_width)
        dbqkv_ref[part] = col_sum(grads.astype(F32))
        weight_grad(normed_ref.reshape(seq, width), grads, dw_ref.at[part], 128)
    dbproj_ref[...] = col_sum(dba[...].reshape(seq, width).astype(F32))
    weight_grad(
        dba.reshape(seq, width), att_ref[...].reshape(seq, part_width), dw_ref.at[3], 128
    )
    group.spread_sent(dba, ag_send, ag_recv)
    total = group.landed_sum(stage[me].astype(F32), stage, landing, rs_send, rs_recv)
    hidden = hidden_ref[...].astype(F32)
    normed, rstd = norm_parts(hidden)
    dmod_ref[0:1] = col_sum(total)
    dmod_ref[1:2] = col_sum(total * normed)
    gin_ref[...] = norm_back(total, normed, rstd, mod_ref[1:2]) + gmid_ref[...]


VM = pl.BlockSpec(memory_space=pltpu.VMEM)
ANY = pl.BlockSpec(memory_space=pl.ANY)


def call(kernel, outs, in_specs, scratch, cid, name):
    return pl.pallas_call(
        kernel,
        out_shape=tuple(jax.ShapeDtypeStruct(shape, dtype) for shape, dtype in outs),
        in_specs=in_specs,
        out_specs=tuple(VM for _ in outs),
        scratch_shapes=scratch,
        compiler_params=pltpu.CompilerParams(
            collective_id=cid, has_side_effects=True, vmem_limit_bytes=VMEM_LIMIT
        ),
        name=name,
    )


def comm_scratch(size, tokens, width):
    dma = pltpu.SemaphoreType.DMA((size,))
    return [pltpu.VMEM((size, tokens, width), BF16)] * 2, [dma] * 4


def att_fwd(hidden, mod, bias, bproj, w):
    tokens, width = hidden.shape
    size = lax.axis_size("section") * lax.axis_size("ml")
    parts, part_width = w.shape[1], w.shape[3]
    bufs, sems = comm_scratch(size, tokens, width)
    return call(
        att_fwd_kernel,
        [
            ((tokens, width), F32),
            ((size, tokens, width), BF16),
            ((3, size, tokens, part_width), BF16),
            ((size, tokens, part_width), BF16),
            ((tokens, width), F32),
        ],
        [VM, VM, VM, VM, ANY],
        [pltpu.VMEM((parts, width, part_width), BF16)]
        + bufs
        + [pltpu.SemaphoreType.DMA((w.shape[0],))]
        + sems,
        1,
        "att_fwd",
    )(hidden, mod, bias, bproj, w)


def mlp_fwd(middle, mod, b1, b2, w1, w2):
    tokens, width = middle.shape
    size = lax.axis_size("section") * lax.axis_size("ml")
    units = w1.shape[2]
    bufs, sems = comm_scratch(size, tokens, width)
    return call(
        mlp_fwd_kernel,
        [
            ((tokens, width), BF16),
            ((size, tokens, width), BF16),
            ((size, tokens, units), F32),
            ((size, tokens, units), BF16),
            ((tokens, width), F32),
        ],
        [VM, VM, VM, VM, ANY, ANY],
        [pltpu.VMEM((width, units), BF16)] * 2
        + bufs
        + [pltpu.SemaphoreType.DMA((w1.shape[0],))] * 2
        + sems,
        2,
        "mlp_fwd",
    )(middle, mod, b1, b2, w1, w2)


def mlp_bwd(grad, middle, mod, branch, normed, pre, gelu, w1, w2):
    tokens, width = middle.shape
    size = lax.axis_size("section") * lax.axis_size("ml")
    units = w1.shape[2]
    bufs, sems = comm_scratch(size, tokens, width)
    return call(
        mlp_bwd_kernel,
        [
            ((tokens, width), F32),
            ((width, units), BF16),
            ((width, units), BF16),
            ((1, units), F32),
            ((1, width), F32),
            ((3, width), F32),
        ],
        [VM] * 7 + [ANY, ANY],
        [pltpu.VMEM((width, units), BF16)] * 2
        + [pltpu.VMEM((size, tokens, width), BF16), pltpu.VMEM((size, tokens, units), BF16)]
        + bufs
        + [pltpu.SemaphoreType.DMA((w1.shape[0],))] * 2
        + sems,
        3,
        "mlp_bwd",
    )(grad, middle, mod, branch, normed, pre, gelu, w1, w2)


def att_bwd(gmid, hidden, mod, branch, normed, proj, att, w):
    tokens, width = gmid.shape
    size = lax.axis_size("section") * lax.axis_size("ml")
    parts, part_width = w.shape[1], w.shape[3]
    bufs, sems = comm_scratch(size, tokens, width)
    seq = size * tokens
    return call(
        att_bwd_kernel,
        [
            ((tokens, width), F32),
            ((parts, width, part_width), BF16),
            ((3, 1, part_width), F32),
            ((1, width), F32),
            ((3, width), F32),
        ],
        [VM] * 7 + [ANY],
        [
            pltpu.VMEM((parts, width, part_width), BF16),
            pltpu.VMEM((size, tokens, width), BF16),
            pltpu.VMEM((3, size, tokens, part_width), BF16),
            pltpu.VMEM((seq, part_width), F32),
            pltpu.VMEM((seq, part_width), F32),
        ]
        + bufs
        + [pltpu.SemaphoreType.DMA((w.shape[0],))]
        + sems,
        4,
        "att_bwd",
    )(gmid, hidden, mod, branch, normed, proj, att, w)


def swap(block):
    return lax.ppermute(
        block, ("section", "mh"), [(s * 2 + h, h * 2 + s) for s in range(2) for h in range(2)]
    )


def per_device(
    latents_in, condition, cotangent,
    modulation_weight, modulation_bias, query_key_value_weight, query_value_bias,
    output_proj_weight, output_proj_bias, first_dense_weight, first_dense_bias,
    second_dense_weight, second_dense_bias,
):
    section, dp = lax.axis_index("section"), lax.axis_index("dp")
    high, low = lax.axis_index("mh"), lax.axis_index("ml")
    n_dp, n_low = lax.axis_size("dp"), lax.axis_size("ml")
    n_mp = 2 * n_low
    mp = high * n_low + low
    member = section * n_low + low
    width = latents_in.shape[-1]
    rows = modulation_weight.shape[1]
    cols = modulation_weight.shape[2]
    part_width = query_key_value_weight.shape[3]
    units = first_dense_weight.shape[2]
    local = section == high

    both = jnp.stack([latents_in[:, 0], cotangent[:, 0]], axis=1)
    sent = lax.dynamic_index_in_dim(both, 1 - high, 0, keepdims=False)
    kept = lax.dynamic_index_in_dim(both, high, 0, keepdims=False)
    got = lax.ppermute(sent, "mh", [(0, 1), (1, 0)])
    mine = jnp.where(local, kept, got)
    latent, cot = mine[0], mine[1]

    cond_all = lax.all_gather(condition[:, 0], "dp", axis=1).reshape(2 * n_dp, width)
    cond_all = cond_all.astype(F32)
    act_all = jax.nn.silu(cond_all).astype(BF16)
    act_rows = lax.dynamic_slice_in_dim(act_all, dp * rows, rows, 1)
    share = jnp.dot(act_rows, modulation_weight[0], preferred_element_type=F32)
    share = share.reshape(2, n_dp, cols)
    share = lax.psum_scatter(share, "dp", scatter_dimension=1, tiled=False)
    share = share + modulation_bias[0].astype(F32)
    full = lax.all_gather(share, ("section", "mh", "ml")).reshape(2, n_mp, 2, cols)
    full = lax.dynamic_index_in_dim(full, high, 2, keepdims=False)
    modul = full.reshape(2, 6, width)

    packed = jnp.concatenate(
        [query_value_bias[0].reshape(-1), first_dense_bias[0], output_proj_bias[0], second_dense_bias[0]]
    )
    packed = lax.all_gather(packed, ("section", "mh", "ml")).reshape(2, n_mp, -1)
    packed = lax.dynamic_index_in_dim(packed, member, 1, keepdims=False).astype(F32)
    bounds = [0, 2 * part_width, 2 * part_width + units, 2 * part_width + units + width]
    bqv = packed[:, : bounds[1]].reshape(2, 2, 1, part_width)
    bqkv = jnp.stack([bqv[:, 0], jnp.zeros_like(bqv[:, 0]), bqv[:, 1]], axis=1)
    b1 = packed[:, None, bounds[1] : bounds[2]]
    bproj = packed[:, None, bounds[2] : bounds[3]]
    b2 = packed[:, None, bounds[3] :]

    w_att = jnp.concatenate(
        [query_key_value_weight[0].transpose(1, 0, 2), output_proj_weight[0].T[None]], axis=0
    )
    w_one = first_dense_weight[0]
    w_two = second_dense_weight[0].T

    def collect(block):
        out = lax.all_gather(swap(block), OTHERS)
        return out.reshape((2, n_dp) + block.shape)

    w_att, w_one, w_two = collect(w_att), collect(w_one), collect(w_two)

    saved = []
    hidden = latent
    for layer in range(2):
        middle, normed, proj, att, branch = att_fwd(
            hidden, modul[layer], bqkv[layer], bproj[layer], w_att[layer]
        )
        out, normed2, pre, gelu, branch2 = mlp_fwd(
            middle, modul[layer], b1[layer], b2[layer], w_one[layer], w_two[layer]
        )
        saved.append((hidden, middle, normed, proj, att, branch, normed2, pre, gelu, branch2))
        hidden = out
    acts = [saved[1][0], hidden]

    grad = cot
    grad_in, d_att, d_one, d_two, d_bias, d_mod = {}, {}, {}, {}, {}, {}
    for layer in (1, 0):
        hidden, middle, normed, proj, att, branch, normed2, pre, gelu, branch2 = saved[layer]
        gmid, dw1, dw2, db1, db2, dmod2 = mlp_bwd(
            grad, middle, modul[layer], branch2, normed2, pre, gelu, w_one[layer], w_two[layer]
        )
        gin, dw, dbqkv, dbproj, dmod1 = att_bwd(
            gmid, hidden, modul[layer], branch, normed, proj, att, w_att[layer]
        )
        grad_in[layer] = gin
        d_att[layer], d_one[layer], d_two[layer] = dw, dw1, dw2
        d_bias[layer] = (
            jnp.concatenate([dbqkv[0, 0], dbqkv[2, 0], db1[0]]),
            jnp.concatenate([dbproj[0], db2[0]]),
        )
        d_mod[layer] = jnp.concatenate([dmod1.reshape(-1), dmod2.reshape(-1)])
        grad = gin.astype(BF16)

    def disperse(pair):
        block = jnp.stack([pair[0], pair[1]])
        return block

    def reduce_rows(first, second, axis):
        block = jnp.stack([first, second])
        axis += 1
        shape = block.shape
        block = block.reshape(shape[:axis] + (n_dp, rows) + shape[axis + 1 :])
        block = jnp.moveaxis(block, axis, 1).reshape((2 * n_dp,) + shape[1:axis] + (rows,) + shape[axis + 1 :])
        out = lax.psum_scatter(block, OTHERS, scatter_dimension=0, tiled=False)
        return swap(out).astype(F32)

    g_att = reduce_rows(d_att[0], d_att[1], 1)
    g_one = reduce_rows(d_one[0], d_one[1], 0)
    g_two = reduce_rows(d_two[0], d_two[1], 0)

    per_unit = lax.psum(jnp.stack([d_bias[0][0], d_bias[1][0]]), OTHERS)
    shared = lax.psum(jnp.stack([d_bias[0][1], d_bias[1][1]]), OTHERS)
    per_unit = lax.all_gather(per_unit, "section")
    per_unit = lax.dynamic_index_in_dim(per_unit, high, 0, keepdims=False)
    per_unit = lax.dynamic_index_in_dim(per_unit, section, 0, keepdims=False)
    shared = lax.dynamic_index_in_dim(shared, section, 0, keepdims=False)

    def dp_part(vec):
        size = vec.shape[-1] // n_dp
        return lax.dynamic_slice_in_dim(vec, dp * size, size, vec.ndim - 1)

    g_bqv = dp_part(per_unit[: 2 * part_width].reshape(2, part_width))
    g_b1 = dp_part(per_unit[2 * part_width :])
    g_bproj = dp_part(shared[:width])
    g_b2 = dp_part(shared[width:])

    dmod = lax.psum(jnp.stack([d_mod[0], d_mod[1]]), GROUP).astype(BF16)
    dmod = lax.all_gather(dmod, OTHERS)
    dmod = lax.dynamic_index_in_dim(dmod, section, 1, keepdims=False)
    dmod = lax.dynamic_slice_in_dim(dmod, mp * cols, cols, 1)
    g_bada = dp_part(jnp.sum(dmod, axis=0, dtype=F32))
    g_wada = jnp.dot(act_rows.T, dmod, preferred_element_type=F32)
    g_act = jnp.dot(dmod, modulation_weight[0].T, preferred_element_type=F32)
    g_act = lax.psum(g_act, ("section", "mh", "ml"))
    g_act = lax.all_gather(g_act, "dp", axis=1, tiled=True).reshape(2, n_dp, width)
    g_act = lax.dynamic_index_in_dim(g_act, dp, 1, keepdims=False)
    _, silu_back = jax.vjp(jax.nn.silu, condition[:, 0].astype(F32))
    g_cond = silu_back(g_act)[0][:, None]

    def deliver(first, second):
        block = jnp.stack([first, second])
        block = lax.all_to_all(block, "section", 0, 0, tiled=True)
        return lax.all_to_all(block, "mh", 0, 0, tiled=True)[None, :, None]

    acts_out = deliver(*acts)
    grad_input = deliver(grad_in[0], grad_in[1])
    return (
        acts_out,
        grad_input,
        g_cond,
        g_wada[None],
        g_bada[None],
        g_att[:3].transpose(1, 0, 2)[None],
        g_bqv[None],
        g_att[3].T[None],
        g_bproj[None],
        g_one[None],
        g_b1[None],
        g_two.T[None],
        g_b2[None],
    )


def solution(mesh):
    sizes = mesh.shape
    grid = mesh.devices.reshape(sizes["section"], sizes["dp"], 2, sizes["mp"] // 2)
    fine = Mesh(grid, ("section", "dp", "mh", "ml"))
    mp = ("mh", "ml")
    in_specs = (
        P(None, "dp", mp, None),
        P(None, "dp", None),
        P(None, "dp", mp, None),
        P("section", "dp", mp),
        P("section", mp),
        P("section", "dp", None, mp),
        P("section", None, mp),
        P("section", mp, "dp"),
        P("section", None),
        P("section", "dp", mp),
        P("section", mp),
        P("section", mp, "dp"),
        P("section", None),
    )
    mpdp = ("mh", "ml", "dp")
    out_specs = (
        P("section", None, "dp", mp, None),
        P("section", None, "dp", mp, None),
        P(None, "dp", None),
        P("section", "dp", mp),
        P("section", mpdp),
        P("section", "dp", None, mp),
        P("section", None, mpdp),
        P("section", mp, "dp"),
        P("section", "dp"),
        P("section", "dp", mp),
        P("section", mpdp),
        P("section", mp, "dp"),
        P("section", "dp"),
    )
    return jax.shard_map(
        per_device, mesh=fine, in_specs=in_specs, out_specs=out_specs, check_vma=False
    )
```

time: 1540 us -> 1020 us (0.66)
  waiting for transfers between devices: 1130 us -> 282 us
  Pallas kernels: 0 us -> 288 us
  blocking collectives: 50.8 us -> 309 us
  matrix products: 175 us -> 2.36 us
  other arithmetic: 83.7 us -> 31.8 us
  starting transfers between devices: 10.7 us -> 43.3 us
    reduce_scatter x16 -> x3, waiting for transfers between devices: 503 us -> 94.5 us  [reduce_rows(): out = lax.psum_scatter(block, OTHERS, scatter_dimension=0, tiled=False)]
    all_gather x16 -> x3, waiting for transfers between devices: 388 us -> 0.02 us  [collect(): out = lax.all_gather(swap(block), OTHERS)]
    pallas_call x0 -> x8, Pallas kernels: none -> 288 us  [the longest x2 85.3 us: att_bwd(): call(att_bwd_kernel, [((tokens, width), F32), ((parts, width, part_width)...]
    unnamed x42 -> x6, waiting for transfers between devices: 218 us -> 0.1 us
    dot_general x63 -> x3, matrix products: 175 us -> 2.36 us  [the longest x1 1.78 us: per_device(): g_wada = jnp.dot(act_rows.T, dmod, preferred_element_type=F32)]
    ppermute x4 -> x7, waiting for transfers between devices: 22.9 us -> 176 us  [the longest x6 176 us: swap(): lax.ppermute(block, ('section', 'mh'), [(s * 2 + h, h * 2 + s) for s in r...]
    psum x1 -> x3, blocking collectives: 21.9 us -> 145 us  [the longest x1 83.6 us: per_device(): g_act = lax.psum(g_act, ('section', 'mh', 'ml'))]
    unnamed x1 -> x2, blocking collectives: 10.5 us -> 90.1 us
  transfers between devices with their start and end apart: 41 -> 17, of which waited for: 39 -> 7; matrix products, arithmetic and copies ran while one was open for 12% -> 5% of each run, Pallas kernels for 0% -> 3%
where the time goes in v1:
time: 1020 us; the launch traced here: 1010 us
  blocking collectives  309 us (30%)
  Pallas kernels  288 us (28%)
  waiting for transfers between devices  282 us (28%)
  starting transfers between devices  43.3 us (4%)
  local copies, waits for them, and re-layouts  39.5 us (4%)
  other arithmetic  31.8 us (3%)
  between operations  15.8 us (2%)
    ppermute x6, waiting for transfers between devices, swap(): lax.ppermute(block, ('section', 'mh'), [(s * 2 + h, h * 2 + s) for s in r...  176 us
    reduce_scatter x3, waiting for transfers between devices, reduce_rows(): out = lax.psum_scatter(block, OTHERS, scatter_dimension=0, tiled=False)  94.5 us
    unnamed x2, blocking collectives  90.1 us
    pallas_call x2, Pallas kernels, att_bwd(): call(att_bwd_kernel, [((tokens, width), F32), ((parts, width, part_width)...  85.3 us
    psum x1, blocking collectives, per_device(): g_act = lax.psum(g_act, ('section', 'mh', 'ml'))  83.6 us
    pallas_call x2, Pallas kernels, att_fwd(): call(att_fwd_kernel, [((tokens, width), F32), ((size, tokens, width), BF1...  70.4 us
    pallas_call x2, Pallas kernels, mlp_fwd(): call(mlp_fwd_kernel, [((tokens, width), BF16), ((size, tokens, width), BF...  68.8 us
    pallas_call x2, Pallas kernels, mlp_bwd(): call(mlp_bwd_kernel, [((tokens, width), F32), ((width, units), BF16), ((w...  63.4 us
  transfers between devices with their start and end apart: 17, of which 7 were waited for; matrix products, arithmetic and copies ran while one was open for 5% of the time, Pallas kernels for 3%

profile of v1, /device:TPU:4, one launch (start us, length us, event | category | flops | bytes accessed | tf_op | source)
XLA Modules:
  0.0 1012.1 jit_solution(7496718047869797851)
XLA Ops:
  7.2 1.2 copy.75
  8.5 1.3 pad_maximum_fusion.4
  9.7 4.4 collective-permute-start.1
  14.2 39.6 %collective-permute-done.1 = bf16[4,288,288]{2,1,0:T(8,128)(2,1)S(1)} collective-permute-done((bf16[4,288,288]{2,1,0:T(8,128)(2,1)S(1)}, bf16[4,288,288]{2,1,0:T(8,128)(2,1)S(1)}, u32[]{:S(2)}, u32[]{:S(2)}) %collective-permute-start.1) | collective-permute-done | bytes 663584 | tf_op jit(solution)/shard_map/ppermute | solution.py:565
  53.8 0.9 copy-done.5
  54.8 1.9 collective-permute-start.2
  56.8 50.8 %collective-permute-done.2 = bf16[288,1152]{1,0:T(8,128)(2,1)S(1)} collective-permute-done((bf16[288,1152]{1,0:T(8,128)(2,1)S(1)}, bf16[288,1152]{1,0:T(8,128)(2,1)S(1)}, u32[]{:S(2)}, u32[]{:S(2)}) %collective-permute-start.2) | collective-permute-done | bytes 663584 | tf_op jit(solution)/shard_map/ppermute | solution.py:565
  107.5 0.8 copy-done.6
  108.4 1.9 collective-permute-start.3
  110.4 61.9 %collective-permute-done.3 = bf16[288,1152]{1,0:T(8,128)(2,1)S(1)} collective-permute-done((bf16[288,1152]{1,0:T(8,128)(2,1)}, bf16[288,1152]{1,0:T(8,128)(2,1)S(1)}, u32[]{:S(2)}, u32[]{:S(2)}) %collective-permute-start.3) | collective-permute-done | bytes 663584 | tf_op jit(solution)/shard_map/ppermute | solution.py:565
  172.3 0.8 copy-done.7
  173.2 1.1 constant_dynamic-update-slice_fusion.1
  174.3 1.1 constant_dynamic-update-slice_fusion
  177.7 76.2 %all-reduce.1 = bf16[2,4,4032]{2,0,1:T(2,128)(2,1)S(1)} all-reduce(bf16[2,4,4032]{2,0,1:T(2,128)(2,1)S(1)} %copy.72), channel_id=2, replica_groups=mesh['section'=2,'dp'=4,'mh'=2,'ml'=2] {'section','mh','ml'}, use_global_device_ids=true, to_apply=%add | all-reduce | flops 32256 | bytes 129024
  254.0 5.4 all_gather.46
  259.6 1.2 dynamic-slice.9
  261.1 13.9 %all-reduce.2 = f32[2,4,1728]{2,0,1:T(2,128)S(1)} all-reduce(f32[2,4,1728]{2,0,1:T(2,128)S(1)} %fusion.4), channel_id=7, replica_groups=mesh['section'=2,'dp'=4,'mh'=2,'ml'=2] {'dp'}, use_global_device_ids=true, to_apply=%region_0.1.clone | all-reduce | flops 13824 | bytes 110592
  276.4 42.5 %all_gather.47 = f32[8,2,1728]{2,1,0:T(2,128)S(1)} all-gather(f32[1,2,1728]{2,1,0:T(2,128)S(1)} %fusion.8), channel_id=1, replica_groups=mesh['section'=2,'dp'=4,'mh'=2,'ml'=2] {'section','mh','ml'}, dimensions={0}, use_global_device_ids=true | all-gather | bytes 124416 | tf_op jit(solution)/shard_map/all_gather | solution.py:604
  321.2 0.7 fusion.16
  322.0 0.9 slice_bitcast_fusion.2
  322.8 6.7 fusion.13
  329.5 31.9 %att_fwd.2 = (f32[128,1152]{1,0:T(8,128)}, bf16[4,128,1152]{2,1,0:T(8,128)(2,1)}, bf16[3,4,128,288]{3,2,1,0:T(8,128)(2,1)}, bf16[4,128,288]{2,1,0:T(8,128)(2,1)}, f32[128,1152]{1,0:T(8,128)}) custom-call(bf16[128,1152]{1,0:T(8,128)(2,1)} %get-tuple-element.178.hidden_ref, f32[6,1152]{1,0:T(8,128)} %squeeze.127.mod_ref, ...), custom_call_target="tpu_custom_call" | custom-call | tf_op jit(solution)/shard_map/att_fwd/pallas_call | solution.py:464
  361.5 5.4 fusion.15
  366.8 5.3 fusion.14
  372.1 35.2 %mlp_fwd.2 = (bf16[128,1152]{1,0:T(8,128)(2,1)}, bf16[4,128,1152]{2,1,0:T(8,128)(2,1)}, f32[4,128,1152]{2,1,0:T(8,128)}, bf16[4,128,1152]{2,1,0:T(8,128)(2,1)}, f32[128,1152]{1,0:T(8,128)}) custom-call(f32[128,1152]{1,0:T(8,128)} %get-tuple-element.55.middle_ref, f32[6,1152]{1,0:T(8,128)} %squeeze.127.mod_ref, f32[1,1152]{1,0:T(1,128)} %get-tuple-element.185.b1_ref, ...), custom_call_target="tpu_custom_call" | custom-call | tf_op jit(solution)/shard_map/mlp_fwd/pallas_call | solution.py:488
  407.3 38.5 %att_fwd.3 = (f32[128,1152]{1,0:T(8,128)}, bf16[4,128,1152]{2,1,0:T(8,128)(2,1)}, bf16[3,4,128,288]{3,2,1,0:T(8,128)(2,1)}, bf16[4,128,288]{2,1,0:T(8,128)(2,1)}, f32[128,1152]{1,0:T(8,128)}) custom-call(bf16[128,1152]{1,0:T(8,128)(2,1)} %get-tuple-element.56.hidden_ref, f32[6,1152]{1,0:T(8,128)} %squeeze.136.mod_ref, ...), custom_call_target="tpu_custom_call" | custom-call | tf_op jit(solution)/shard_map/att_fwd/pallas_call | solution.py:464
  445.8 33.6 %mlp_fwd.3 = (bf16[128,1152]{1,0:T(8,128)(2,1)}, bf16[4,128,1152]{2,1,0:T(8,128)(2,1)}, f32[4,128,1152]{2,1,0:T(8,128)}, bf16[4,128,1152]{2,1,0:T(8,128)(2,1)}, f32[128,1152]{1,0:T(8,128)}) custom-call(f32[128,1152]{1,0:T(8,128)} %get-tuple-element.57.middle_ref, f32[6,1152]{1,0:T(8,128)} %squeeze.136.mod_ref, f32[1,1152]{1,0:T(1,128)} %get-tuple-element.182.b1_ref, ...), custom_call_target="tpu_custom_call" | custom-call | tf_op jit(solution)/shard_map/mlp_fwd/pallas_call | solution.py:488
  479.4 32.6 %mlp_bwd.2 = (f32[128,1152]{1,0:T(8,128)}, bf16[1152,1152]{1,0:T(8,128)(2,1)}, bf16[1152,1152]{1,0:T(8,128)(2,1)}, f32[1,1152]{1,0:T(1,128)}, f32[1,1152]{1,0:T(1,128)}, /*index=5*/f32[3,1152]{1,0:T(4,128)}) custom-call(bf16[128,1152]{1,0:T(8,128)(2,1)} %get-tuple-element.177.grad_ref, f32[128,1152]{1,0:T(8,128)} %get-tuple-element.57.middle_ref, ...), custom_call_target="tpu_custom_call" | custom-call | tf_op jit(solution)/shard_map/mlp_bwd/pallas_call | solution.py:512
  512.0 44.5 %att_bwd.2 = (f32[128,1152]{1,0:T(8,128)}, bf16[4,1152,288]{2,1,0:T(8,128)(2,1)}, f32[3,1,288]{2,1,0:T(1,128)}, f32[1,1152]{1,0:T(1,128)}, f32[3,1152]{1,0:T(4,128)}) custom-call(f32[128,1152]{1,0:T(8,128)} %get-tuple-element.63.gmid_ref, bf16[128,1152]{1,0:T(8,128)(2,1)} %get-tuple-element.56.hidden_ref, f32[6,1152]{1,0:T(8,128)} %squeeze.136.mod_ref, ...), custom_call_target="tpu_custom_call" | custom-call | tf_op jit(solution)/shard_map/att_bwd/pallas_call | solution.py:539
  556.5 1.8 convert_element_type.40.grad_ref
  558.3 30.8 %mlp_bwd.3 = (f32[128,1152]{1,0:T(8,128)}, bf16[1152,1152]{1,0:T(8,128)(2,1)}, bf16[1152,1152]{1,0:T(8,128)(2,1)}, f32[1,1152]{1,0:T(1,128)}, f32[1,1152]{1,0:T(1,128)}, /*index=5*/f32[3,1152]{1,0:T(4,128)}) custom-call(bf16[128,1152]{1,0:T(8,128)(2,1)} %convert_element_type.40.grad_ref, f32[128,1152]{1,0:T(8,128)} %get-tuple-element.55.middle_ref, ...), custom_call_target="tpu_custom_call" | custom-call | tf_op jit(solution)/shard_map/mlp_bwd/pallas_call | solution.py:512
  589.1 40.8 %att_bwd.3 = (f32[128,1152]{1,0:T(8,128)}, bf16[4,1152,288]{2,1,0:T(8,128)(2,1)}, f32[3,1,288]{2,1,0:T(1,128)}, f32[1,1152]{1,0:T(1,128)}, f32[3,1152]{1,0:T(4,128)}) custom-call(f32[128,1152]{1,0:T(8,128)} %get-tuple-element.73.gmid_ref, bf16[128,1152]{1,0:T(8,128)(2,1)} %get-tuple-element.178.hidden_ref, f32[6,1152]{1,0:T(8,128)} %squeeze.127.mod_ref, ...), custom_call_target="tpu_custom_call" | custom-call | tf_op jit(solution)/shard_map/att_bwd/pallas_call | solution.py:539
  629.9 3.2 fusion.2
  633.5 1.1 copy-done.2
  634.6 3.5 fusion
  638.2 5.4 pad_maximum_fusion.2
  643.7 6.2 pad_maximum_fusion.1
  651.2 0.9 pad_maximum_fusion.5
  652.1 6.0 all-to-all-start
  658.5 1.1 pad_maximum_fusion.3
  659.6 3.5 all-to-all-done
  663.1 6.4 all-to-all-start.2
  669.7 8.1 all-to-all-done.2
  677.8 3.5 all-to-all-start.1
  681.3 35.5 %all-reduce.3 = (f32[1,2,1728]{2,1,0:T(2,128)S(1)}, f32[2,2304]{1,0:T(2,128)S(1)}) all-reduce(f32[1,2,1728]{2,1,0:T(2,128)S(1)} %maximum_bitcast_fusion, f32[2,2304]{1,0:T(2,128)S(1)} %pad_maximum_fusion.9), channel_id=1, replica_groups=mesh['section'=2,'dp'=4,'mh'=2,'ml'=2] {'mh','dp'}, use_global_device_ids=true, to_apply=%region_5.6 | all-reduce | flops 8064 | bytes 64512 | tf_op jit(solution)/shard_map/psum | solution.py:681
  716.8 4.4 all_gather.60
  721.3 25.9 %psum.28 = bf16[2,6912]{1,0:T(2,128)(2,1)S(1)} all-reduce(f32[2,6912]{1,0:T(2,128)S(1)} %pad_maximum_fusion.6), channel_id=1, replica_groups=mesh['section'=2,'dp'=4,'mh'=2,'ml'=2] {'section','ml'}, use_global_device_ids=true, to_apply=%region_1.2 | all-reduce | flops 13824 | bytes 82944 | tf_op jit(solution)/shard_map/psum | solution.py:697
  747.2 16.6 %all-gather.5 = bf16[8,2,6912]{2,1,0:T(2,128)(2,1)S(1)} all-gather(bf16[1,2,6912]{2,1,0:T(2,128)(2,1)S(1)} %bitcast.148), channel_id=6, replica_groups=mesh['section'=2,'dp'=4,'mh'=2,'ml'=2] {'mh','dp'}, dimensions={0}, use_global_device_ids=true | all-gather | bytes 248832 | tf_op jit(solution)/shard_map/all_gather | solution.py:698
  764.0 3.6 all-to-all-start.3
  767.9 83.6 %psum.29 = f32[8,288]{1,0:T(8,128)S(1)} all-reduce(f32[8,288]{1,0:T(8,128)S(1)} %fusion.6), channel_id=1, replica_groups=mesh['section'=2,'dp'=4,'mh'=2,'ml'=2] {'section','mh','ml'}, use_global_device_ids=true, to_apply=%region_2.3 | all-reduce | flops 2304 | bytes 18432 | tf_op jit(solution)/shard_map/psum | solution.py:704
  851.5 5.2 all-gather.6
  858.8 1.9 collective-permute-start.4
  862.0 5.7 collective-permute-start.6
  867.8 1.8 convolution_bitcast_fusion
  869.5 94.5 %reduce-scatter.6.cloned.1.call-done = bf16[1,288,1152]{2,1,0:T(8,128)(2,1)} async-done(((bf16[8,288,1152]{2,1,0:T(8,128)(2,1)}), bf16[1,288,1152]{2,1,0:T(8,128)(2,1)}) %reduce-scatter.6.cloned.1.call-update) | async-done | bytes 663568 | tf_op jit(solution)/shard_map/reduce_scatter | solution.py:674
  964.0 7.5 collective-permute-start.5
  971.6 1.3 convert_element_type.44
  972.8 1.1 slice_bitcast_fusion
  974.0 1.0 copy.81
  975.0 2.2 convert_bitcast_fusion
  977.2 23.8 %collective-permute-done.5 = bf16[288,1152]{1,0:T(8,128)(2,1)} collective-permute-done((bf16[288,1152]{1,0:T(8,128)(2,1)}, bf16[288,1152]{1,0:T(8,128)(2,1)}, u32[]{:S(2)}, u32[]{:S(2)}) %collective-permute-start.5) | collective-permute-done | bytes 663584 | tf_op jit(solution)/shard_map/ppermute | solution.py:565
  1001.0 2.2 bitcast_convert_fusion
  1003.3 0.8 copy.103
  1004.1 1.0 copy.104
  (149 shorter events, 12.0 us)
Async XLA Ops:
  7.2 253.6 %copy-start = (bf16[1,288,1728]{2,1,0:T(8,128)(2,1)S(1)}, bf16[1,288,1728]{2,1,0:T(8,128)(2,1)}, u32[]{:S(2)}) copy-start(bf16[1,288,1728]{2,1,0:T(8,128)(2,1)} %param.16) | copy-start | bytes 2985988
  7.2 47.6 %copy-start.27 = (bf16[1,288,1152]{2,1,0:T(8,128)(2,1)S(1)}, bf16[1,288,1152]{2,1,0:T(8,128)(2,1)}, u32[]{:S(2)}) copy-start(bf16[1,288,1152]{2,1,0:T(8,128)(2,1)} %param.22) | copy-start | bytes 1990660
  7.2 315.6 %all-gather.11.cloned.1.call-start = ((), (), s32[]{:S(2)}) async-start(), calls=%async_computation.10 | async-start | bytes 7962624 | tf_op jit(solution)/shard_map/all_gather | solution.py:627
  9.7 44.0 %collective-permute-start.1 = (bf16[4,288,288]{2,1,0:T(8,128)(2,1)S(1)}, bf16[4,288,288]{2,1,0:T(8,128)(2,1)S(1)}, u32[]{:S(2)}, u32[]{:S(2)}) collective-permute-start(bf16[4,288,288]{2,1,0:T(8,128)(2,1)S(1)} %pad_maximum_fusion.4), channel_id=1, source_target_pairs={{0,0},{2,16},{16,2},{18,18},{1,1},{3,17},{17,3},{19,19},{4,4},{6,2... | collective-permute-start | bytes 1990664 | tf_op jit(solution)/shard_map/ppermute | solution.py:565
  53.8 0.9 copy-start.5
  54.7 120.9 %copy-start.15 = (bf16[1,1152]{1,0:T(2,128)(2,1)S(1)}, bf16[1,1152]{1,0:T(2,128)(2,1)}, u32[]{:S(2)}) copy-start(bf16[1,1152]{1,0:T(2,128)(2,1)} %param.23) | copy-start | bytes 6916
  54.7 121.0 %copy-start.16 = (bf16[1,1152]{1,0:T(2,128)(2,1)S(1)}, bf16[1,1152]{1,0:T(2,128)(2,1)}, u32[]{:S(2)}) copy-start(bf16[1,1152]{1,0:T(2,128)(2,1)} %param.21) | copy-start | bytes 6916
  54.7 121.0 %copy-start.17 = (bf16[1,1152]{1,0:T(2,128)(2,1)S(1)}, bf16[1,1152]{1,0:T(2,128)(2,1)}, u32[]{:S(2)}) copy-start(bf16[1,1152]{1,0:T(2,128)(2,1)} %param.25) | copy-start | bytes 6916
  54.7 121.0 %copy-start.26 = (bf16[1,2,288]{2,1,0:T(2,128)(2,1)S(1)}, bf16[1,2,288]{2,1,0:T(2,128)(2,1)}, u32[]{:S(2)}) copy-start(bf16[1,2,288]{2,1,0:T(2,128)(2,1)} %param.19) | copy-start | bytes 3460
  54.8 121.1 %copy-start.28 = (u32[32]{0:T(128)S(1)}, u32[32]{0:T(128)}, u32[]{:S(2)}) copy-start(u32[32]{0:T(128)} %constant.129) | copy-start | bytes 388
  54.8 306.7 %all-gather.13.cloned.1.call-start = ((), (), s32[]{:S(2)}) async-start(), calls=%async_computation.11 | async-start | bytes 5971968 | tf_op jit(solution)/shard_map/all_gather | solution.py:627
  54.8 52.7 %collective-permute-start.2 = (bf16[288,1152]{1,0:T(8,128)(2,1)S(1)}, bf16[288,1152]{1,0:T(8,128)(2,1)S(1)}, u32[]{:S(2)}, u32[]{:S(2)}) collective-permute-start(bf16[288,1152]{1,0:T(8,128)(2,1)S(1)} %bitcast.152), channel_id=1, source_target_pairs={{0,0},{2,16},{16,2},{18,18},{1,1},{3,17},{17,3},{19,19},{4,4},{6,2... | collective-permute-start | bytes 1990664 | tf_op jit(solution)/shard_map/ppermute | solution.py:565
  107.5 0.8 copy-start.6
  108.4 258.4 %all-gather.15.cloned.1.call-start = ((), (), s32[]{:S(2)}) async-start(), calls=%async_computation.12 | async-start | bytes 5971968 | tf_op jit(solution)/shard_map/all_gather | solution.py:627
  108.4 63.9 %collective-permute-start.3 = (bf16[288,1152]{1,0:T(8,128)(2,1)}, bf16[288,1152]{1,0:T(8,128)(2,1)S(1)}, u32[]{:S(2)}, u32[]{:S(2)}) collective-permute-start(bf16[288,1152]{1,0:T(8,128)(2,1)} %bitcast.153), channel_id=1, source_target_pairs={{0,0},{2,16},{16,2},{18,18},{1,1},{3,17},{17,3},{19,19},{4,4},{6,2... | collective-permute-start | bytes 1990664 | tf_op jit(solution)/shard_map/ppermute | solution.py:565
  172.3 0.8 copy-start.7
  173.2 685.7 %reduce-scatter.4.cloned.1.call-start = ((), (), s32[]{:S(2)}) async-start(), calls=%async_computation.7 | async-start | bytes 7962624 | tf_op jit(solution)/shard_map/reduce_scatter | solution.py:674
  175.5 146.4 %collective-permute-start = (bf16[2,128,1152]{2,1,0:T(8,128)(2,1)S(1)}, bf16[2,128,1152]{2,1,0:T(8,128)(2,1)S(1)}, u32[]{:S(2)}, u32[]{:S(2)}) collective-permute-start(bf16[2,128,1152]{2,1,0:T(8,128)(2,1)S(1)} %dynamic-slice_bitcast_fusion), channel_id=1, source_target_pairs={{0,2},{2,0},{1,3},{3,1},{4,6},{6,4},{5,7},{7,5},{8,10},{10,8},{9,1... | collective-permute-start | bytes 1769480 | tf_op jit(solution)/shard_map/ppermute | solution.py:592
  629.9 3.6 copy-start.1
  629.9 4.7 copy-start.2
  638.1 223.9 %reduce-scatter.8.cloned.1.call-start = ((), (), s32[]{:S(2)}) async-start(), calls=%async_computation.9 | async-start | bytes 5971968 | tf_op jit(solution)/shard_map/reduce_scatter | solution.py:674
  643.6 320.4 %reduce-scatter.6.cloned.1.call-start = ((), (), s32[]{:S(2)}) async-start(), calls=%async_computation.8 | async-start | bytes 5971968 | tf_op jit(solution)/shard_map/reduce_scatter | solution.py:674
  649.9 0.7 copy-start.23
  649.9 0.7 copy-start.22
  649.9 0.8 copy-start.21
  649.9 0.8 copy-start.20
  649.9 0.9 copy-start.13
  649.9 0.9 copy-start.12
  649.9 0.9 copy-start.11
  649.9 0.9 copy-start.10
  650.0 1.1 copy-start.3
  650.0 1.3 copy-start.9
  650.0 8.1 copy-start.25
  650.0 8.2 copy-start.24
  650.0 8.2 copy-start.19
  650.0 8.3 copy-start.18
  650.0 8.5 copy-start.4
  650.0 8.5 copy-start.8
  652.1 11.0 %all-to-all-start = ((bf16[2,128,1152]{2,1,0:T(8,128)(2,1)}), bf16[2,128,1152]{2,1,0:T(8,128)(2,1)}, u32[]{:S(2)}, u32[]{:S(2)}) async-start(bf16[2,128,1152]{2,1,0:T(8,128)(2,1)} %pad_maximum_fusion.5), calls=%async_computation | async-start | bytes 1179648 | tf_op jit(solution)/shard_map/all_to_all | solution.py:712
  663.1 14.6 %all-to-all-start.2 = ((f32[2,128,1152]{2,1,0:T(8,128)}), f32[2,128,1152]{2,1,0:T(8,128)}, u32[]{:S(2)}, u32[]{:S(2)}) async-start(f32[2,128,1152]{2,1,0:T(8,128)} %pad_maximum_fusion.3), calls=%async_computation.2 | async-start | bytes 2359296 | tf_op jit(solution)/shard_map/all_to_all | solution.py:712
  669.6 191.8 %copy-start.14 = (bf16[2,1,1152]{2,0,1:T(2,128)(2,1)S(1)}, bf16[2,1,1152]{2,0,1:T(2,128)(2,1)}, u32[]{:S(2)}) copy-start(bf16[2,1,1152]{2,0,1:T(2,128)(2,1)} %param.14) | copy-start | bytes 13828
  677.8 86.2 %all-to-all-start.1 = ((bf16[2,128,1152]{2,1,0:T(8,128)(2,1)}), bf16[2,128,1152]{2,1,0:T(8,128)(2,1)S(1)}, u32[]{:S(2)}, u32[]{:S(2)}) async-start(bf16[2,128,1152]{2,1,0:T(8,128)(2,1)} %all-to-all-done), calls=%async_computation.1 | async-start | bytes 1179648 | tf_op jit(solution)/shard_map/all_to_all | solution.py:713
  764.0 105.6 %all-to-all-start.3 = ((f32[2,128,1152]{2,1,0:T(8,128)}), f32[2,128,1152]{2,1,0:T(8,128)S(1)}, u32[]{:S(2)}, u32[]{:S(2)}) async-start(f32[2,128,1152]{2,1,0:T(8,128)} %all-to-all-done.2), calls=%async_computation.3 | async-start | bytes 2359296 | tf_op jit(solution)/shard_map/all_to_all | solution.py:713
  858.8 112.7 %collective-permute-start.4 = (bf16[4,288,288]{2,1,0:T(8,128)(2,1)}, bf16[4,288,288]{2,1,0:T(8,128)(2,1)}, u32[]{:S(2)}, u32[]{:S(2)}) collective-permute-start(bf16[4,288,288]{2,1,0:T(8,128)(2,1)} %bitcast.151), channel_id=1, source_target_pairs={{0,0},{2,16},{16,2},{18,18},{1,1},{3,17},{17,3},{19,19},{4,4},{6,2... | collective-permute-start | bytes 1990664 | tf_op jit(solution)/shard_map/ppermute | solution.py:565
  862.0 113.0 %collective-permute-start.6 = (bf16[288,1152]{1,0:T(8,128)(2,1)}, bf16[288,1152]{1,0:T(8,128)(2,1)}, u32[]{:S(2)}, u32[]{:S(2)}) collective-permute-start(bf16[288,1152]{1,0:T(8,128)(2,1)} %bitcast.154), channel_id=1, source_target_pairs={{0,0},{2,16},{16,2},{18,18},{1,1},{3,17},{17,3},{19,19},{4,4},{6,2... | collective-permute-start | bytes 1990664 | tf_op jit(solution)/shard_map/ppermute | solution.py:565
  964.0 37.0 %collective-permute-start.5 = (bf16[288,1152]{1,0:T(8,128)(2,1)}, bf16[288,1152]{1,0:T(8,128)(2,1)}, u32[]{:S(2)}, u32[]{:S(2)}) collective-permute-start(bf16[288,1152]{1,0:T(8,128)(2,1)} %bitcast.155), channel_id=1, source_target_pairs={{0,0},{2,16},{16,2},{18,18},{1,1},{3,17},{17,3},{19,19},{4,4},{6,2... | collective-permute-start | bytes 1990664 | tf_op jit(solution)/shard_map/ppermute | solution.py:565
Sparse Core Ops, SparseCore 0:
  54.8 94.4 all-gather.10
  151.8 100.7 all-gather.12
  255.1 64.1 all-gather.14
  638.2 103.5 reduce-scatter.3
  745.1 102.1 reduce-scatter.7
  850.6 113.4 reduce-scatter.5

commit v2 on v1

v2 whole, which is shorter than its diff:
```python
import jax
import jax.numpy as jnp
from jax import lax
from jax.experimental import pallas as pl
from jax.experimental.pallas import tpu as pltpu
from jax.sharding import Mesh
from jax.sharding import PartitionSpec as P

HEAD_SIZE = 72
EPS = 1e-06
MESH = pl.DeviceIdType.MESH
BF16 = jnp.bfloat16
F32 = jnp.float32
GELU_C = 0.7978845608028654
GELU_A = 0.044715
NT = (((1,), (1,)), ((), ()))
TN = (((0,), (0,)), ((), ()))
VMEM_LIMIT = 60 * 1024 * 1024


def dot_nn(a, b):
    return jnp.dot(a, b, preferred_element_type=F32)


def dot_nt(a, b):
    return lax.dot_general(a, b, NT, preferred_element_type=F32)


def dot_tn(a, b):
    return lax.dot_general(a, b, TN, preferred_element_type=F32)


def norm_parts(values):
    center = values - jnp.mean(values, axis=-1, keepdims=True)
    spread = jnp.mean(center * center, axis=-1, keepdims=True)
    rstd = lax.rsqrt(spread + EPS)
    return center * rstd, rstd


def norm_back(grad, normed, rstd, scale):
    dn = grad * (1.0 + scale)
    first = jnp.mean(dn, axis=-1, keepdims=True)
    second = jnp.mean(dn * normed, axis=-1, keepdims=True)
    return (dn - first - normed * second) * rstd


def col_sum(values):
    return jnp.sum(values, axis=0, keepdims=True)


class Group:
    def __init__(self):
        self.low = lax.axis_size("ml")
        self.size = lax.axis_size("section") * self.low
        self.me = lax.axis_index("section") * self.low + lax.axis_index("ml")

    def device(self, member):
        return (
            lax.div(member, self.low),
            lax.axis_index("dp"),
            lax.axis_index("mh"),
            lax.rem(member, self.low),
        )

    def peer(self, step):
        return lax.rem(self.me + step, self.size)

    def copy(self, src, dst, send_sem, recv_sem, member):
        return pltpu.make_async_remote_copy(
            src_ref=src,
            dst_ref=dst,
            send_sem=send_sem,
            recv_sem=recv_sem,
            device_id=self.device(member),
            device_id_type=MESH,
        )

    def spread(self, buf, send_sem, recv_sem):
        me = self.me
        for step in range(1, self.size):
            self.copy(
                buf.at[me], buf.at[me], send_sem.at[step], recv_sem.at[me], self.peer(step)
            ).start()

    def spread_wait(self, buf, send_sem, recv_sem, member):
        self.copy(buf.at[member], buf.at[member], send_sem.at[1], recv_sem.at[member], member).wait_recv()

    def spread_sent(self, buf, send_sem, recv_sem):
        me = self.me
        for step in range(1, self.size):
            self.copy(
                buf.at[me], buf.at[me], send_sem.at[step], recv_sem.at[me], self.peer(step)
            ).wait_send()

    def reduce_copy(self, stage, landing, send_sem, recv_sem, member):
        return self.copy(
            stage.at[member], landing.at[self.me], send_sem.at[member], recv_sem.at[self.me], member
        )

    def reduce_wait(self, landing, send_sem, recv_sem, member):
        self.copy(
            landing.at[member], landing.at[member], send_sem.at[member], recv_sem.at[member], member
        ).wait_recv()

    def landed_sum(self, own, stage, landing, send_sem, recv_sem):
        total = own
        for step in range(1, self.size):
            member = self.peer(step)
            self.reduce_wait(landing, send_sem, recv_sem, member)
            total = total + landing[member].astype(F32)
        for step in range(1, self.size):
            self.reduce_copy(stage, landing, send_sem, recv_sem, self.peer(step)).wait_send()
        return total


def load(src, dst, sem):
    copy = pltpu.make_async_copy(src, dst, sem)
    copy.start()
    return [copy]


def lane_mask(shape, head):
    lanes = lax.broadcasted_iota(jnp.int32, shape, len(shape) - 1)
    return (lanes >= head * HEAD_SIZE) & (lanes < (head + 1) * HEAD_SIZE)


def row_mask(shape, head):
    rows = lax.broadcasted_iota(jnp.int32, shape, 0)
    return (rows >= head * HEAD_SIZE) & (rows < (head + 1) * HEAD_SIZE)


def stack_heads(block):
    heads = block.shape[-1] // HEAD_SIZE
    zero = jnp.zeros_like(block)
    return jnp.concatenate(
        [jnp.where(lane_mask(block.shape, head), block, zero) for head in range(heads)], axis=0
    )


def identity(size):
    rows = lax.broadcasted_iota(jnp.int32, (size, size), 0)
    cols = lax.broadcasted_iota(jnp.int32, (size, size), 1)
    return jnp.where(rows == cols, 1.0, 0.0).astype(BF16)


def att_fwd_kernel(
    bg,
    hidden_ref, mod_ref, bias_ref, bproj_ref, w_ref,
    middle_ref, normed_ref, proj_ref, att_ref, branch_ref,
    w_buf, wo_buf, stage, landing, w_sem, ag_send, ag_recv, rs_send, rs_recv,
):
    group = Group()
    me, size = group.me, group.size
    tokens, width = hidden_ref.shape
    part_width = att_ref.shape[-1]
    heads = part_width // HEAD_SIZE
    loads = load(w_ref, w_buf, w_sem.at[0])
    hidden = hidden_ref[...].astype(F32)
    normed, _ = norm_parts(hidden)
    normed_ref[me] = (normed * (1.0 + mod_ref[1:2]) + mod_ref[0:1]).astype(BF16)
    Place().greet()
    group.spread(normed_ref, ag_send, ag_recv)
    bg(0)
    for copy in loads:
        copy.wait()

    def project(step, carry):
        member = group.peer(step)

        @pl.when(step > 0)
        def _():
            group.spread_wait(normed_ref, ag_send, ag_recv, member)

        out = dot_nn(normed_ref[member], w_buf[:, : 3 * part_width]) + bias_ref[...]
        for part in range(3):
            cols = slice(part * part_width, (part + 1) * part_width)
            proj_ref[part, member] = out[:, cols].astype(BF16)
        return carry

    wo_buf[...] = w_buf[:, 3 * part_width :]
    lax.fori_loop(0, size, project, 0)
    bg(1)
    seq = size * tokens
    keys = proj_ref[1].reshape(seq, -1)
    values = proj_ref[2].reshape(seq, -1)

    def attend(member):
        stacked = stack_heads(proj_ref[0, member])
        powered = jnp.exp(dot_nt(stacked, keys) * HEAD_SIZE**-0.5)
        probs = powered * (1.0 / jnp.sum(powered, axis=-1, keepdims=True))
        mixed = dot_nn(probs.astype(BF16), values)
        out = mixed[:tokens]
        for head in range(1, heads):
            part = mixed[head * tokens : (head + 1) * tokens]
            out = jnp.where(lane_mask(part.shape, head), part, out)
        low = out.astype(BF16)
        att_ref[member] = low
        return dot_nt(low, wo_buf[...])

    def send(step, carry):
        member = group.peer(step)
        stage[member] = attend(member).astype(BF16)
        group.reduce_copy(stage, landing, rs_send, rs_recv, member).start()
        return carry

    lax.fori_loop(1, size, send, 0)
    bg(2)
    own = attend(me)
    group.spread_sent(normed_ref, ag_send, ag_recv)
    bg(3)
    branch = group.landed_sum(own, stage, landing, rs_send, rs_recv) + bproj_ref[...]
    branch_ref[...] = branch
    middle_ref[...] = hidden_ref[...].astype(F32) + mod_ref[2:3] * branch
    bg(4)


def mlp_fwd_kernel(
    bg,
    middle_ref, mod_ref, b1_ref, b2_ref, w1_ref, w2_ref,
    out_ref, normed_ref, pre_ref, gelu_ref, branch_ref,
    w1_buf, w2_buf, stage, landing, w_sem, ag_send, ag_recv, rs_send, rs_recv,
):
    group = Group()
    me, size = group.me, group.size
    loads = load(w1_ref, w1_buf, w_sem.at[0]) + load(w2_ref, w2_buf, w_sem.at[1])
    normed, _ = norm_parts(middle_ref[...])
    normed_ref[me] = (normed * (1.0 + mod_ref[4:5]) + mod_ref[3:4]).astype(BF16)
    Place().greet()
    group.spread(normed_ref, ag_send, ag_recv)
    bg(0)
    for copy in loads:
        copy.wait()

    def dense(member):
        pre = dot_nn(normed_ref[member], w1_buf[...]) + b1_ref[...]
        pre_ref[member] = pre
        bent = jnp.tanh(GELU_C * (pre + GELU_A * pre * pre * pre))
        low = (0.5 * pre * (1.0 + bent)).astype(BF16)
        gelu_ref[member] = low
        return dot_nt(low, w2_buf[...])

    own = dense(me)

    def send(step, carry):
        member = group.peer(step)
        group.spread_wait(normed_ref, ag_send, ag_recv, member)
        stage[member] = dense(member).astype(BF16)
        group.reduce_copy(stage, landing, rs_send, rs_recv, member).start()
        return carry

    stage[me] = own.astype(BF16)
    bg(1)
    lax.fori_loop(1, size, send, 0)
    bg(2)
    group.spread_sent(normed_ref, ag_send, ag_recv)
    bg(3)
    own = stage[me].astype(F32)
    branch = group.landed_sum(own, stage, landing, rs_send, rs_recv) + b2_ref[...]
    branch_ref[...] = branch
    out_ref[...] = (middle_ref[...] + mod_ref[5:6] * branch).astype(BF16)
    bg(4)


def weight_grad(lhs_ref, rhs, out_ref, tile):
    def body(index, carry):
        cols = pl.ds(pl.multiple_of(index * tile, tile), tile)
        out_ref[cols, :] = dot_tn(lhs_ref[:, cols], rhs).astype(BF16)
        return carry

    lax.fori_loop(0, lhs_ref.shape[-1] // tile, body, 0)


def mlp_bwd_kernel(
    bg,
    grad_ref, middle_ref, mod_ref, branch_ref, normed_ref, pre_ref, gelu_ref, w1_ref, w2_ref,
    gmid_ref, dw1_ref, dw2_ref, db1_ref, db2_ref, dmod_ref,
    w1_buf, w2_buf, dbr, dpre, stage, landing, w_sem, ag_send, ag_recv, rs_send, rs_recv,
):
    group = Group()
    me, size = group.me, group.size
    tokens, width = grad_ref.shape
    loads = load(w1_ref, w1_buf, w_sem.at[0]) + load(w2_ref, w2_buf, w_sem.at[1])
    grad = grad_ref[...].astype(F32)
    dbr[me] = (grad * mod_ref[5:6]).astype(BF16)
    Place().greet()
    group.spread(dbr, ag_send, ag_recv)
    bg(0)
    dmod_ref[2:3] = col_sum(grad * branch_ref[...])
    for copy in loads:
        copy.wait()

    def back(member):
        dgelu = dot_nn(dbr[member], w2_buf[...])
        pre = pre_ref[member]
        bent = jnp.tanh(GELU_C * (pre + GELU_A * pre * pre * pre))
        slope = 0.5 * (1.0 + bent) + 0.5 * pre * (1.0 - bent * bent) * (
            GELU_C * (1.0 + 3.0 * GELU_A * pre * pre)
        )
        low = (dgelu * slope).astype(BF16)
        dpre[member] = low
        return dot_nt(low, w1_buf[...])

    stage[me] = back(me).astype(BF16)
    bg(1)

    def send(step, carry):
        member = group.peer(step)
        group.spread_wait(dbr, ag_send, ag_recv, member)
        stage[member] = back(member).astype(BF16)
        group.reduce_copy(stage, landing, rs_send, rs_recv, member).start()
        return carry

    lax.fori_loop(1, size, send, 0)
    bg(2)
    seq = size * tokens
    dpre_all = dpre[...].reshape(seq, -1)
    gelu_all = gelu_ref[...].reshape(seq, -1)
    db1_ref[...] = col_sum(dpre_all.astype(F32))
    db2_ref[...] = col_sum(dbr[...].reshape(seq, -1).astype(F32))
    weight_grad(normed_ref.reshape(seq, width), dpre_all, dw1_ref, 128)
    weight_grad(dbr.reshape(seq, width), gelu_all, dw2_ref, 128)
    group.spread_sent(dbr, ag_send, ag_recv)
    bg(3)
    total = group.landed_sum(stage[me].astype(F32), stage, landing, rs_send, rs_recv)
    normed, rstd = norm_parts(middle_ref[...])
    dmod_ref[0:1] = col_sum(total)
    dmod_ref[1:2] = col_sum(total * normed)
    gmid_ref[...] = norm_back(total, normed, rstd, mod_ref[4:5]) + grad_ref[...].astype(F32)
    bg(4)


def att_bwd_kernel(
    bg,
    gmid_ref, hidden_ref, mod_ref, branch_ref, normed_ref, proj_ref, att_ref, w_ref,
    gin_ref, dw_ref, dbqkv_ref, dbproj_ref, dmod_ref,
    w_buf, wo_buf, dba, dproj, dkey, dval, stage, landing, w_sem, ag_send, ag_recv, rs_send, rs_recv,
):
    group = Group()
    me, size = group.me, group.size
    tokens, width = gmid_ref.shape
    seq = size * tokens
    part_width = att_ref.shape[-1]
    heads = part_width // HEAD_SIZE
    loads = load(w_ref, w_buf, w_sem.at[0])
    gmid = gmid_ref[...]
    dba[me] = (gmid * mod_ref[2:3]).astype(BF16)
    Place().greet()
    group.spread(dba, ag_send, ag_recv)
    bg(0)
    dmod_ref[2:3] = col_sum(gmid * branch_ref[...])
    keys = proj_ref[1].reshape(seq, part_width)
    values = proj_ref[2].reshape(seq, part_width)
    keys_t = dot_nt(identity(part_width), keys).astype(BF16)
    dkey[...] = jnp.zeros_like(dkey)
    dval[...] = jnp.zeros_like(dval)
    for copy in loads:
        copy.wait()
    wo_buf[...] = w_buf[:, 3 * part_width :]

    def back(step, carry):
        member = group.peer(step)

        if not isinstance(step, int):
            group.spread_wait(dba, ag_send, ag_recv, member)
        datt = dot_nn(dba[member], wo_buf[...]).astype(BF16)
        datt_st = stack_heads(datt)
        query_st = stack_heads(proj_ref[0, member])
        powered = jnp.exp(dot_nt(keys, query_st) * HEAD_SIZE**-0.5)
        probs = powered * (1.0 / jnp.sum(powered, axis=0, keepdims=True))
        dval[...] += dot_nn(probs.astype(BF16), datt_st)
        dprobs = dot_nt(values, datt_st)
        dscore = (probs * (dprobs - jnp.sum(probs * dprobs, axis=0, keepdims=True))).astype(BF16)
        dkey[...] += dot_nn(dscore, query_st)
        dq_t = dot_nn(keys_t, dscore)
        picked = dq_t[:, :tokens]
        for head in range(1, heads):
            part = dq_t[:, head * tokens : (head + 1) * tokens]
            picked = jnp.where(row_mask(part.shape, head), part, picked)
        low = (picked * HEAD_SIZE**-0.5).astype(BF16)
        dproj[member, :, :part_width] = dot_nt(identity(tokens), low).astype(BF16)
        return carry

    back(0, 0)
    bg(1)
    lax.fori_loop(1, size, back, 0)
    for member in range(size):
        rows = slice(member * tokens, (member + 1) * tokens)
        dproj[member, :, part_width : 2 * part_width] = (dkey[rows] * HEAD_SIZE**-0.5).astype(BF16)
        dproj[member, :, 2 * part_width :] = dval[rows].astype(BF16)

    def partial_rows(member):
        return dot_nt(dproj[member], w_buf[:, : 3 * part_width])

    def send(step, carry):
        member = group.peer(step)
        stage[member] = partial_rows(member).astype(BF16)
        group.reduce_copy(stage, landing, rs_send, rs_recv, member).start()
        return carry

    lax.fori_loop(1, size, send, 0)
    stage[me] = partial_rows(me).astype(BF16)
    bg(2)
    grads = dproj[...].reshape(seq, -1)
    dbqkv_ref[...] = col_sum(grads.astype(F32))
    dbproj_ref[...] = col_sum(dba[...].reshape(seq, width).astype(F32))
    mixed = att_ref[...].reshape(seq, part_width)
    normed_rows, dba_rows = normed_ref.reshape(seq, width), dba.reshape(seq, width)

    def weights(index, carry):
        cols = pl.ds(pl.multiple_of(index * 128, 128), 128)
        dw_ref[cols, : 3 * part_width] = dot_tn(normed_rows[:, cols], grads).astype(BF16)
        dw_ref[cols, 3 * part_width :] = dot_tn(dba_rows[:, cols], mixed).astype(BF16)
        return carry

    lax.fori_loop(0, width // 128, weights, 0)
    group.spread_sent(dba, ag_send, ag_recv)
    bg(3)
    total = group.landed_sum(stage[me].astype(F32), stage, landing, rs_send, rs_recv)
    hidden = hidden_ref[...].astype(F32)
    normed, rstd = norm_parts(hidden)
    dmod_ref[0:1] = col_sum(total)
    dmod_ref[1:2] = col_sum(total * normed)
    gin = norm_back(total, normed, rstd, mod_ref[1:2]) + gmid_ref[...]
    gin_ref[...] = gin.astype(BF16)
    bg(4)


class Place:
    def __init__(self):
        self.section, self.dp = lax.axis_index("section"), lax.axis_index("dp")
        self.high, self.low = lax.axis_index("mh"), lax.axis_index("ml")
        self.n_dp, self.n_low = lax.axis_size("dp"), lax.axis_size("ml")
        self.total = 4 * self.n_dp * self.n_low
        self.me = ((self.section * self.n_dp + self.dp) * 2 + self.high) * self.n_low + self.low

    def unflatten(self, number):
        low = lax.rem(number, self.n_low)
        rest = lax.div(number, self.n_low)
        high, rest = lax.rem(rest, 2), lax.div(rest, 2)
        return lax.div(rest, self.n_dp), lax.rem(rest, self.n_dp), high, low

    def greet(self):
        barrier = pltpu.get_barrier_semaphore()
        others = []
        for sec in range(2):
            for step in range(self.n_low):
                if sec or step:
                    section = lax.rem(self.section + sec, 2)
                    others.append((section, self.dp, self.high, lax.rem(self.low + step, self.n_low)))
        for sec in range(2):
            others.append(self.plane(sec, 1 - self.high))
        for step in range(1, self.n_dp // 2):
            others.append((self.section, self.same_core(step), self.high, self.low))
        others.append(self.core_mate())
        for device in others:
            pl.semaphore_signal(barrier, inc=1, device_id=device, device_id_type=MESH)
        pl.semaphore_wait(barrier, len(others))

    def role(self, layer, number):
        same = (self.section == layer) if number < 2 else (self.section != layer)
        return same & ((self.high == layer) if number % 2 == 0 else (self.high != layer))

    def role_device(self, layer, number):
        section = layer if number < 2 else 1 - layer
        return self.plane(section, layer if number % 2 == 0 else 1 - layer)

    def greet_all(self):
        barrier = pltpu.get_barrier_semaphore()

        def body(step, carry):
            pl.semaphore_signal(
                barrier,
                inc=1,
                device_id=self.unflatten(lax.rem(self.me + step, self.total)),
                device_id_type=MESH,
            )
            return carry

        lax.fori_loop(1, self.total, body, 0)
        pl.semaphore_wait(barrier, self.total - 1)

    def copy(self, src, dst, send_sem, recv_sem, device):
        return pltpu.make_async_remote_copy(
            src_ref=src,
            dst_ref=dst,
            send_sem=send_sem,
            recv_sem=recv_sem,
            device_id=device,
            device_id_type=MESH,
        )

    def core_mate(self):
        return (self.section, self.dp + 1 - 2 * lax.rem(self.dp, 2), self.high, self.low)

    def same_core(self, step):
        return lax.rem(self.dp + 2 * step, self.n_dp)

    def plane(self, section, high):
        return (section, self.dp, high, self.low)

    def exchange(self, pick, landing, send_sem, recv_sem):
        landing[self.me] = pick((self.section, self.dp, self.high, self.low))[...]

        def copy(number):
            device = self.unflatten(number)
            return self.copy(
                pick(device), landing.at[self.me], send_sem.at[number], recv_sem.at[self.me], device
            )

        def start(step, carry):
            copy(lax.rem(self.me + step, self.total)).start()
            return carry

        def finish(step, carry):
            number = lax.rem(self.me + step, self.total)
            device = self.unflatten(number)
            self.copy(
                landing.at[number], landing.at[number], send_sem.at[number], recv_sem.at[number], device
            ).wait_recv()
            copy(number).wait_send()
            return carry

        lax.fori_loop(1, self.total, start, 0)
        return lambda: lax.fori_loop(1, self.total, finish, 0)


VM = pl.BlockSpec(memory_space=pltpu.VMEM)
ANY = pl.BlockSpec(memory_space=pl.ANY)
DMA = pltpu.SemaphoreType.DMA


class Handle:
    def __init__(self, shape, dtype):
        self.shape, self.dtype = shape, dtype
        self.array = None
        self.ref = None


class Task:
    inputs = ()
    outs = ()
    scratch = ()
    handles = ()


class Collect(Task):
    def __init__(self, item, tensor, layer, handle):
        self.tensor, self.layer, self.handle = tensor, layer, handle
        self.inputs = ((item, VM),)
        self.handles = (handle,)
        self.chunk = item.shape[1]
        self.scratch = (DMA((2,)), DMA, DMA)

    def run(self, phase, refs):
        (item,), _, (send, recv, own) = refs
        place = Place()
        source = item.at[self.tensor]
        rows = self.handle.ref.at[pl.ds(pl.multiple_of(place.dp * self.chunk, 16), self.chunk)]

        def to(number, role):
            return place.copy(
                source, rows, send.at[number], recv, place.role_device(self.layer, role)
            )

        targets = {0: (1,), 1: (2, 3), 2: (), 3: ()}
        for role in range(4):

            @pl.when(place.role(self.layer, role))
            def _():
                if phase == "a":
                    for number, target in enumerate(targets[role]):
                        to(number, target).start()
                    if role == 0:
                        pltpu.make_async_copy(source, rows, own).start()
                if phase == "b":
                    if role == 0:
                        pltpu.make_async_copy(source, rows, own).wait()
                    else:
                        place.copy(
                            rows, rows, send.at[0], recv, place.role_device(self.layer, 0)
                        ).wait_recv()
                if phase == "c":
                    for number, target in enumerate(targets[role]):
                        to(number, target).wait_send()


class Widen(Task):
    def __init__(self, handle):
        self.handle = handle
        self.handles = (handle,)
        chips = lax.axis_size("dp") // 2
        self.scratch = (DMA((chips,)),) * 4

    def rows(self, index):
        chunk = self.handle.shape[0] // lax.axis_size("dp")
        return self.handle.ref.at[pl.ds(pl.multiple_of(index * chunk, 16), chunk)]

    def run(self, phase, refs):
        _, _, (x_send, x_recv, c_send, c_recv) = refs
        place = Place()
        chips = place.n_dp // 2

        def across(step):
            return place.copy(
                self.rows(place.dp), self.rows(place.dp), x_send.at[step], x_recv.at[step],
                (place.section, place.same_core(step), place.high, place.low),
            )

        def landed(step):
            held = self.rows(place.same_core(chips - step))
            return place.copy(
                held, held, x_send.at[step], x_recv.at[step],
                (place.section, place.same_core(step), place.high, place.low),
            )

        def to_mate(step):
            held = self.rows(place.same_core(step))
            return place.copy(held, held, c_send.at[step], c_recv.at[step], place.core_mate())

        def from_mate(step):
            held = self.rows(lax.rem(place.core_mate()[1] + 2 * step, place.n_dp))
            return place.copy(held, held, c_send.at[step], c_recv.at[step], place.core_mate())

        if phase == "a":
            for step in range(1, chips):
                across(step).start()
            to_mate(0).start()
        if phase == "b":
            for step in range(1, chips):
                landed(step).wait_recv()
                to_mate(chips - step).start()
        if phase == "c":
            for step in range(chips):
                from_mate(step).wait_recv()
                to_mate(step).wait_send()
                if step:
                    across(step).wait_send()


class Narrow(Task):
    def __init__(self, grad):
        n_dp = lax.axis_size("dp")
        chips = n_dp // 2
        self.chunk = grad.shape[0] // n_dp
        block = (chips, self.chunk, grad.shape[1])
        self.inputs = ((grad, ANY),)
        self.outs = (((self.chunk, grad.shape[1]), BF16, VM),)
        self.scratch = (pltpu.VMEM(block, BF16),) * 3 + (DMA((chips,)),) * 5

    def run(self, phase, refs):
        (grad,), (out,), scratch = refs
        own, near, far, own_sem, c_send, c_recv, x_send, x_recv = scratch
        place = Place()
        chips = place.n_dp // 2

        def rows(index):
            return grad.at[pl.ds(pl.multiple_of(index * self.chunk, 16), self.chunk)]

        def to_mate(step):
            other = lax.rem(place.core_mate()[1] + 2 * step, place.n_dp)
            return place.copy(
                rows(other), near.at[step], c_send.at[step], c_recv.at[step], place.core_mate()
            )

        def load_own(step):
            return pltpu.make_async_copy(
                rows(place.same_core(step)), own.at[step], own_sem.at[step]
            )

        def across(step):
            return place.copy(
                own.at[step], far.at[step], x_send.at[step], x_recv.at[step],
                (place.section, place.same_core(step), place.high, place.low),
            )

        order = list(range(1, chips)) + [0]
        if phase == "a":
            for step in order:
                to_mate(step).start()
                load_own(step).start()
        if phase == "b":
            for step in order:
                load_own(step).wait()
                to_mate(step).wait_recv()
                own[step] = (own[step].astype(F32) + near[step].astype(F32)).astype(BF16)
                if step:
                    across(step).start()
        if phase == "c":
            total = own[0].astype(F32)
            for step in range(1, chips):
                across(step).wait_recv()
                total = total + far[step].astype(F32)
            out[...] = total.astype(BF16)
            for step in range(chips):
                to_mate(step).wait_send()
                if step:
                    across(step).wait_send()


class Settle(Task):
    def __init__(self, part, layer, held=None):
        self.layer = layer
        self.held = held
        self.inputs = () if held else ((part, ANY),)
        self.outs = ((part.shape, F32, VM),)
        self.scratch = (
            pltpu.VMEM((2,) + part.shape, BF16), pltpu.VMEM(part.shape, BF16),
            DMA((2,)), DMA((3,)), DMA,
        )

    def run(self, phase, refs):
        ins, (out,), (land, temp, send, recv, own_sem) = refs
        part = self.held() if self.held else ins[0]
        place = Place()
        layer = self.layer

        def to(src, dst, s, r, role):
            return place.copy(src, dst, send.at[s], recv.at[r], place.role_device(layer, role))

        def direct(role):
            if role == 2:
                return to(part, temp, 0, 2, 0)
            return to(part, land.at[0], 0, 0, 0 if role == 1 else 1)

        def relay():
            return to(temp, land.at[1], 1, 1, 1)

        for role in range(4):

            @pl.when(place.role(layer, role))
            def _():
                if phase == "a":
                    if role:
                        direct(role).start()
                    else:
                        pltpu.make_async_copy(part, land.at[1], own_sem).start()
                if phase == "b":
                    if role == 0:
                        to(temp, temp, 0, 2, 0).wait_recv()
                        relay().start()
                    else:
                        direct(role).wait_send()
                if phase == "c":
                    if role == 0:
                        pltpu.make_async_copy(part, land.at[1], own_sem).wait()
                        relay().wait_send()
                    if role < 2:
                        to(land.at[0], land.at[0], 0, 0, role).wait_recv()
                    if role == 1:
                        to(land.at[1], land.at[1], 0, 1, 1).wait_recv()
                    if role < 2:
                        out[...] = land[0].astype(F32) + land[1].astype(F32)


class Deliver(Task):
    def __init__(self, rows, layer):
        self.layer = layer
        self.inputs = ((rows, VM),)
        self.outs = (((2,) + rows.shape, rows.dtype, VM),)
        self.scratch = (pltpu.VMEM(rows.shape, rows.dtype), DMA((2,)), DMA((3,)))

    def run(self, phase, refs):
        (rows,), (out,), (temp, send, recv) = refs
        place = Place()
        layer = self.layer

        def to(src, dst, s, r, role):
            return place.copy(src, dst, send.at[s], recv.at[r], place.role_device(layer, role))

        def direct(role):
            if role == 2:
                return to(rows, temp, 0, 2, 0)
            return to(rows, out.at[1 - layer], 0, 0, 0 if role == 1 else 1)

        def relay():
            return to(temp, out.at[layer], 1, 1, 1)

        for role in range(4):

            @pl.when(place.role(layer, role))
            def _():
                if phase == "a":
                    if role:
                        direct(role).start()
                    else:
                        out[layer] = rows[...]
                if phase == "b" and role == 0:
                    to(temp, temp, 0, 2, 0).wait_recv()
                    relay().start()
                if phase == "c":
                    if role == 0:
                        relay().wait_send()
                    else:
                        direct(role).wait_send()
                    if role < 2:
                        to(out.at[1 - layer], out.at[1 - layer], 0, 0, role).wait_recv()
                    if role == 1:
                        to(out.at[layer], out.at[layer], 0, 1, 1).wait_recv()


class Tokens(Task):
    def __init__(self, rows):
        self.inputs = ((rows, VM),)
        self.outs = ((rows.shape[1:], rows.dtype, VM),)
        self.scratch = (DMA, DMA)

    def run(self, phase, refs):
        (rows,), (out,), (send, recv) = refs
        place = Place()
        local = place.section == place.high
        copy = place.copy(
            rows.at[1 - place.high], out, send, recv, place.plane(place.section, 1 - place.high)
        )

        @pl.when(local)
        def _():
            if phase == "a":
                copy.start()
                out[...] = rows[place.high]
            if phase == "c":
                copy.wait_send()

        @pl.when(jnp.logical_not(local))
        def _():
            if phase == "c":
                copy.wait_recv()


def launch(kernel, operands, outs, scratch, schedule, cid, name):
    tasks = []
    for point in schedule:
        for task, _ in point:
            if task not in tasks:
                tasks.append(task)
    operands, outs, scratch = list(operands), list(outs), list(scratch)
    n_in, n_out, n_scratch = len(operands), len(outs), len(scratch)
    spans = []
    for task in tasks:
        spans.append((len(operands), len(outs), len(scratch)))
        operands += task.inputs
        outs += task.outs
        scratch += task.scratch
    handles = []
    for task in tasks:
        for handle in task.handles:
            if handle not in handles:
                handles.append(handle)
    aliases = {}
    first_handle = len(outs)
    for handle in handles:
        if handle.array is not None:
            aliases[len(operands)] = len(outs)
            operands.append((handle.array, ANY))
        outs.append((handle.shape, handle.dtype, ANY))

    def body(*refs):
        ins = refs[: len(operands)]
        results = refs[len(operands) : len(operands) + len(outs)]
        rest = refs[len(operands) + len(outs) :]
        for number, handle in enumerate(handles):
            handle.ref = results[first_handle + number]
        views = []
        for task, (a, b, c) in zip(tasks, spans):
            views.append(
                (
                    ins[a : a + len(task.inputs)],
                    results[b : b + len(task.outs)],
                    rest[c : c + len(task.scratch)],
                )
            )
            task.refs = views[-1]

        def bg(point):
            for task, phase in schedule[point]:
                task.run(phase, task.refs)

        kernel(bg, *ins[:n_in], *results[:n_out], *rest[:n_scratch])

    done = pl.pallas_call(
        body,
        out_shape=tuple(jax.ShapeDtypeStruct(shape, dtype) for shape, dtype, _ in outs),
        in_specs=[spec for _, spec in operands],
        out_specs=tuple(spec for _, _, spec in outs),
        scratch_shapes=scratch,
        input_output_aliases=aliases,
        compiler_params=pltpu.CompilerParams(
            collective_id=cid, has_side_effects=True, vmem_limit_bytes=VMEM_LIMIT
        ),
        name=name,
    )(*[array for array, _ in operands])
    for number, handle in enumerate(handles):
        handle.array = done[first_handle + number]
        handle.ref = None
    for task, (_, b, _) in zip(tasks, spans):
        task.results = done[b : b + len(task.outs)]
    return done[:n_out]


def group_size():
    return lax.axis_size("section") * lax.axis_size("ml")


def comm_scratch(tokens, width):
    size = group_size()
    return [pltpu.VMEM((size, tokens, width), BF16)] * 2, [DMA((size,))] * 4


def att_fwd(hidden, mod, bias, bproj, w, schedule, cid):
    tokens, width = hidden.shape
    size = group_size()
    part_width = width // size
    bufs, sems = comm_scratch(tokens, width)
    return launch(
        att_fwd_kernel,
        [(hidden, VM), (mod, VM), (bias, VM), (bproj, VM), (w.array, ANY)],
        [
            ((tokens, width), F32, VM),
            ((size, tokens, width), BF16, VM),
            ((3, size, tokens, part_width), BF16, VM),
            ((size, tokens, part_width), BF16, VM),
            ((tokens, width), F32, VM),
        ],
        [pltpu.VMEM(w.shape, BF16), pltpu.VMEM((width, part_width), BF16)]
        + bufs
        + [DMA((1,))]
        + sems,
        schedule,
        cid,
        "att_fwd",
    )


def mlp_fwd(middle, mod, b1, b2, w1, w2, schedule, cid):
    tokens, width = middle.shape
    size = group_size()
    units = w1.shape[1]
    bufs, sems = comm_scratch(tokens, width)
    return launch(
        mlp_fwd_kernel,
        [(middle, VM), (mod, VM), (b1, VM), (b2, VM), (w1.array, ANY), (w2.array, ANY)],
        [
            ((tokens, width), BF16, VM),
            ((size, tokens, width), BF16, VM),
            ((size, tokens, units), F32, VM),
            ((size, tokens, units), BF16, VM),
            ((tokens, width), F32, VM),
        ],
        [pltpu.VMEM(w1.shape, BF16)] * 2 + bufs + [DMA((2,))] + sems,
        schedule,
        cid,
        "mlp_fwd",
    )


def mlp_bwd(grad, middle, mod, branch, normed, pre, gelu, w1, w2, schedule, cid):
    tokens, width = middle.shape
    size = group_size()
    units = w1.shape[1]
    bufs, sems = comm_scratch(tokens, width)
    ins = (grad, middle, mod, branch, normed, pre, gelu)
    return launch(
        mlp_bwd_kernel,
        [(array, VM) for array in ins] + [(w1.array, ANY), (w2.array, ANY)],
        [
            ((tokens, width), F32, VM),
            (w1.shape, BF16, VM),
            (w2.shape, BF16, VM),
            ((1, units), F32, VM),
            ((1, width), F32, VM),
            ((3, width), F32, VM),
        ],
        [pltpu.VMEM(w1.shape, BF16)] * 2
        + [pltpu.VMEM((size, tokens, width), BF16), pltpu.VMEM((size, tokens, units), BF16)]
        + bufs
        + [DMA((2,))]
        + sems,
        schedule,
        cid,
        "mlp_bwd",
    )


def att_bwd(gmid, hidden, mod, branch, normed, proj, att, w, schedule, cid):
    tokens, width = gmid.shape
    size = group_size()
    part_width = width // size
    bufs, sems = comm_scratch(tokens, width)
    seq = size * tokens
    ins = (gmid, hidden, mod, branch, normed, proj, att)
    return launch(
        att_bwd_kernel,
        [(array, VM) for array in ins] + [(w.array, ANY)],
        [
            ((tokens, width), BF16, VM),
            (w.shape, BF16, VM),
            ((1, 3 * part_width), F32, VM),
            ((1, width), F32, VM),
            ((3, width), F32, VM),
        ],
        [
            pltpu.VMEM(w.shape, BF16),
            pltpu.VMEM((width, part_width), BF16),
            pltpu.VMEM((size, tokens, width), BF16),
            pltpu.VMEM((size, tokens, 3 * part_width), BF16),
            pltpu.VMEM((seq, part_width), F32),
            pltpu.VMEM((seq, part_width), F32),
        ]
        + bufs
        + [DMA((1,))]
        + sems,
        schedule,
        cid,
        "att_bwd",
    )


def prologue_kernel(
    bg,
    cond_ref, wada_ref, bada_ref, bias_ref,
    modul_ref, act_ref, bias_out,
    cond_land, share, land, cond_send, cond_recv, mod_send, mod_recv, b_send, b_recv,
):
    place = Place()
    section, dp, high = place.section, place.dp, place.high
    place.greet_all()

    def spread(step):
        other = lax.rem(dp + step, place.n_dp)
        return place.copy(
            cond_ref.at[other], cond_land.at[dp], cond_send.at[step], cond_recv.at[dp],
            (section, other, high, place.low),
        )

    def spread_wait(step):
        other = lax.rem(dp + step, place.n_dp)
        return place.copy(
            cond_land.at[other], cond_land.at[other], cond_send.at[step], cond_recv.at[other],
            (section, other, high, place.low),
        )

    cond_land[dp] = cond_ref[dp]
    for step in range(1, place.n_dp):
        spread(step).start()

    def bias_copy(target):
        return place.copy(
            bias_ref, bias_out.at[section], b_send.at[target], b_recv.at[section],
            place.plane(high, target),
        )

    here = section == high
    for target in range(2):

        @pl.when(jnp.logical_not(here & (high == target)))
        def _():
            bias_copy(target).start()

    @pl.when(here)
    def _():
        bias_out[section] = bias_ref[...]

    bg(0)
    for step in range(1, place.n_dp):
        spread_wait(step).wait_recv()
    parts = [cond_land[index] for index in range(place.n_dp)]
    act = jax.nn.silu(jnp.concatenate(parts, axis=0)).astype(BF16)
    act_ref[...] = act
    bias = jnp.where(dp == 0, bada_ref[...], 0.0)
    product = dot_nn(act, wada_ref[...])
    for row in range(2 * place.n_dp):
        share[row] = product[row : row + 1] + bias
    finish = place.exchange(
        lambda device: share.at[device[1] * 2 + device[2]], land, mod_send, mod_recv
    )
    bg(1)
    bg(2)
    finish()
    for layer in range(2):
        for part in range(2 * place.n_low):
            total = land[layer * place.n_dp * 2 * place.n_low + part]
            for index in range(1, place.n_dp):
                total = total + land[(layer * place.n_dp + index) * 2 * place.n_low + part]
            modul_ref[layer * 2 * place.n_low + part] = total
    bg(3)
    for step in range(1, place.n_dp):
        spread(step).wait_send()
    for target in range(2):

        @pl.when(jnp.logical_not(here & (high == target)))
        def _():
            bias_copy(target).wait_send()

        @pl.when(jnp.logical_not(here & (section == target)))
        def _():
            place.copy(
                bias_out.at[target], bias_out.at[target], b_send.at[0], b_recv.at[target],
                place.plane(section, 1 - high),
            ).wait_recv()

    bg(4)


def prologue(cond, wada, bada, bias, schedule, cid):
    n_dp, _, chunk = cond.shape
    n_mp = 2 * lax.axis_size("ml")
    total = 2 * n_dp * n_mp
    share = wada.shape[1]
    return launch(
        prologue_kernel,
        [(cond, VM), (wada, VM), (bada, VM), (bias, VM)],
        [
            ((2 * n_mp, 1, share), F32, VM),
            ((2 * n_dp, chunk), BF16, VM),
            ((2,) + bias.shape, F32, VM),
        ],
        [
            pltpu.VMEM((n_dp, 2, chunk), F32),
            pltpu.VMEM((2 * n_dp, 1, share), F32),
            pltpu.VMEM((total, 1, share), F32),
            DMA((n_dp,)),
            DMA((n_dp,)),
            DMA((total,)),
            DMA((total,)),
            DMA((2,)),
            DMA((2,)),
        ],
        schedule,
        cid,
        "prologue",
    )


def epilogue_kernel(
    bg,
    dmod_ref, act_ref, wada_ref, dbias_ref,
    gada_ref, gbada_ref, gact_ref, gbias_ref,
    mod_land, act_stage, act_land, bias_land, bias_stage, bias_final,
    mod_send, mod_recv, act_send, act_recv, d_send, d_recv, b_send, b_recv,
):
    place = Place()
    section, dp, high = place.section, place.dp, place.high
    place.greet_all()
    finish_mod = place.exchange(
        lambda device: dmod_ref.at[(device[0] * 2 + device[2]) * place.n_low + device[3]],
        mod_land, mod_send, mod_recv,
    )

    def spread(step):
        other = lax.rem(dp + step, place.n_dp)
        return place.copy(
            dbias_ref, bias_land.at[dp], d_send.at[step], d_recv.at[dp],
            (section, other, high, place.low),
        )

    for step in range(1, place.n_dp):
        spread(step).start()
    bg(0)
    finish_mod()
    parts = 2 * place.n_low
    latents = []
    for index in range(place.n_dp):
        for micro in range(2):
            total = 0.0
            for sec in range(2):
                for low in range(place.n_low):
                    number = ((sec * place.n_dp + index) * 2 + micro) * place.n_low + low
                    total = total + mod_land[number]
            latents.append(total)
    dmod = jnp.concatenate(latents, axis=0).astype(BF16)
    back = dot_nt(dmod, wada_ref[...])
    for index in range(place.n_dp):
        act_stage[index] = back[2 * index : 2 * index + 2]
    finish_act = place.exchange(lambda device: act_stage.at[device[1]], act_land, act_send, act_recv)
    bias_sum = dbias_ref[...]
    for step in range(1, place.n_dp):
        other = lax.rem(dp + step, place.n_dp)
        place.copy(
            bias_land.at[other], bias_land.at[other], d_send.at[step], d_recv.at[other],
            (section, other, high, place.low),
        ).wait_recv()
        bias_sum = bias_sum + bias_land[other]
    bias_stage[...] = bias_sum

    def settle(layer):
        return place.copy(
            bias_stage.at[layer], bias_final.at[high], b_send.at[layer], b_recv.at[high],
            place.plane(layer, section),
        )

    for layer in range(2):
        here = (section == layer) & (high == section)

        @pl.when(here)
        def _():
            bias_final[high] = bias_stage[layer]

        @pl.when(jnp.logical_not(here))
        def _():
            settle(layer).start()

    bg(1)
    gbada_ref[...] = col_sum(dmod.astype(F32))
    gada_ref[...] = dot_tn(act_ref[...], dmod)
    bg(2)
    finish_act()
    for index in range(place.n_dp):
        total = 0.0
        for sec in range(2):
            for part in range(parts):
                total = total + act_land[(sec * place.n_dp + index) * parts + part]
        gact_ref[index] = total
    bg(3)
    for half in range(2):
        here = (section == high) & (high == half)

        @pl.when(jnp.logical_not(here))
        def _():
            place.copy(
                bias_final.at[half], bias_final.at[half], b_send.at[0], b_recv.at[half],
                place.plane(high, half),
            ).wait_recv()

    gbias_ref[...] = bias_final[0] + bias_final[1]
    for layer in range(2):

        @pl.when(jnp.logical_not((section == layer) & (high == section)))
        def _():
            settle(layer).wait_send()

    for step in range(1, place.n_dp):
        spread(step).wait_send()
    bg(4)


def epilogue(dmod, act, wada, dbias, schedule, cid):
    n_dp, n_mp = lax.axis_size("dp"), 2 * lax.axis_size("ml")
    total = 2 * n_dp * n_mp
    chunk, share = wada.shape
    row = dbias.shape[1:]
    return launch(
        epilogue_kernel,
        [(dmod, VM), (act, VM), (wada, VM), (dbias, VM)],
        [
            ((chunk, share), F32, VM),
            ((1, share), F32, VM),
            ((n_dp, 2, chunk), F32, VM),
            (row, F32, VM),
        ],
        [
            pltpu.VMEM((total, 1, share), F32),
            pltpu.VMEM((n_dp, 2, chunk), F32),
            pltpu.VMEM((total, 2, chunk), F32),
            pltpu.VMEM((n_dp,) + dbias.shape, F32),
            pltpu.VMEM(dbias.shape, F32),
            pltpu.VMEM((2,) + row, F32),
            DMA((total,)),
            DMA((total,)),
            DMA((total,)),
            DMA((total,)),
            DMA((n_dp,)),
            DMA((n_dp,)),
            DMA((2,)),
            DMA((2,)),
        ],
        schedule,
        cid,
        "epilogue",
    )


def per_device(
    latents_in, condition, cotangent,
    modulation_weight, modulation_bias, query_key_value_weight, query_value_bias,
    output_proj_weight, output_proj_bias, first_dense_weight, first_dense_bias,
    second_dense_weight, second_dense_bias,
):
    section, dp = lax.axis_index("section"), lax.axis_index("dp")
    n_dp, n_low = lax.axis_size("dp"), lax.axis_size("ml")
    n_mp = 2 * n_low
    width = latents_in.shape[-1]
    rows = modulation_weight.shape[1]
    cols = modulation_weight.shape[2]
    part_width = query_key_value_weight.shape[3]
    units = first_dense_weight.shape[2]

    item = jnp.stack(
        [
            jnp.concatenate(
                [query_key_value_weight[0].reshape(rows, -1), output_proj_weight[0].T], axis=1
            ),
            first_dense_weight[0],
            second_dense_weight[0].T,
        ]
    )
    cond = condition[:, 0].astype(F32)
    packed = jnp.concatenate(
        [
            query_value_bias[0, 0], query_value_bias[0, 1], first_dense_bias[0],
            output_proj_bias[0], second_dense_bias[0],
        ]
    ).astype(F32)[None]
    w = [[Handle((width, units), BF16) for _ in range(3)] for _ in range(2)]
    collect = [[Collect(item, t, l, w[l][t]) for t in range(3)] for l in range(2)]
    widen = [[Widen(w[l][t]) for t in range(3)] for l in range(2)]
    tokens_in = Tokens(latents_in[:, 0])
    tokens_cot = Tokens(cotangent[:, 0])

    def plan(*points):
        out = []
        for point in points:
            out.append([(task, phase) for task, phases in point for phase in phases])
        return out

    c, x = collect, widen
    modul, act_rows, biases = prologue(
        cond.reshape(2, n_dp, rows).transpose(1, 0, 2),
        modulation_weight[0],
        modulation_bias.astype(F32),
        packed,
        plan(
            [(tokens_in, "a"), (c[0][0], "a"), (c[1][0], "a")],
            [(c[0][0], "c"), (c[1][0], "c"), (c[0][1], "a"), (c[1][1], "a")]
            + [(c[0][0], "b"), (x[0][0], "a"), (c[1][0], "b")],
            [(c[0][1], "c"), (c[1][1], "c"), (c[0][2], "a"), (c[1][2], "a")]
            + [(x[0][0], "b"), (c[0][1], "b"), (x[0][1], "a"), (c[1][1], "b")],
            [],
            [(c[0][2], "c"), (c[1][2], "c"), (c[0][2], "b"), (c[1][2], "b"), (x[0][1], "b")]
            + [(tokens_in, "c"), (x[0][0], "c"), (x[0][1], "c")],
        ),
        1,
    )
    modul = modul.reshape(2, 6, width)
    bounds = [0, part_width, 2 * part_width, 2 * part_width + units, 2 * part_width + units + width]
    bqkv = jnp.concatenate(
        [
            biases[..., : bounds[1]], jnp.zeros((2, 1, part_width), F32),
            biases[..., bounds[1] : bounds[2]],
        ],
        axis=-1,
    )
    b1 = biases[..., bounds[2] : bounds[3]]
    bproj = biases[..., bounds[3] : bounds[4]]
    b2 = biases[..., bounds[4] :]

    hidden = [tokens_in.results[0]]
    att_plan = [
        plan(
            [(x[0][2], "a")],
            [],
            [],
            [(x[0][2], "b")],
            [(x[0][2], "c")],
        ),
        plan(
            [(x[1][1], "a"), (x[1][2], "a"), (tokens_cot, "a")],
            [],
            [],
            [(x[1][1], "b"), (x[1][2], "b")],
            [(x[1][1], "c"), (x[1][2], "c"), (tokens_cot, "c")],
        ),
    ]
    saved = []
    for layer in range(2):
        middle, normed, proj, att, branch = att_fwd(
            hidden[layer], modul[layer], bqkv[layer], bproj[layer], w[layer][0], att_plan[layer],
            2 + 2 * layer,
        )
        if layer == 0:
            mlp_plan = plan(
                [(x[1][0], "a")],
                [],
                [],
                [(x[1][0], "b")],
                [(x[1][0], "c")],
            )
        else:
            acts_first = Deliver(hidden[1], 0)
            mlp_plan = plan([], [], [], [], [])
        out, normed2, pre, gelu, branch2 = mlp_fwd(
            middle, modul[layer], b1[layer], b2[layer], w[layer][1], w[layer][2], mlp_plan,
            3 + 2 * layer,
        )
        saved.append((middle, normed, proj, att, branch, normed2, pre, gelu, branch2))
        hidden.append(out)

    grad = tokens_cot.results[0]
    narrow = [[None] * 3 for _ in range(2)]
    settle = [[None] * 3 for _ in range(2)]
    d_bias, d_mod, gins = {}, {}, {}
    acts_second = Deliver(hidden[2], 1)
    for layer in (1, 0):
        middle, normed, proj, att, branch, normed2, pre, gelu, branch2 = saved[layer]
        if layer == 1:
            mlp_plan = plan(
                [(acts_first, "a"), (acts_second, "a")],
                [],
                [(acts_first, "b"), (acts_second, "b")],
                [],
                [(acts_first, "c"), (acts_second, "c")],
            )
        else:
            third = narrow[1][0]
            mlp_plan = plan([(third, "a")], [(third, "b")], [], [], [(third, "c")])
        gmid, dw1, dw2, db1, db2, dmod2 = mlp_bwd(
            grad, middle, modul[layer], branch2, normed2, pre, gelu, w[layer][1], w[layer][2],
            mlp_plan, 6 + 2 * (1 - layer),
        )
        narrow[layer][1], narrow[layer][2] = Narrow(dw1), Narrow(dw2)
        one, two = narrow[layer][1], narrow[layer][2]
        if layer == 0:
            settle[1][0] = Settle(narrow[1][0].results[0], 1)
            gin_second = Deliver(gins[1], 1)
        att_plan = plan(
            [(two, "a"), (one, "a")], [(two, "b"), (one, "b")], [], [], [(two, "c"), (one, "c")]
        )
        gin, dw, dbqkv, dbproj, dmod1 = att_bwd(
            gmid, hidden[layer], modul[layer], branch, normed, proj, att, w[layer][0],
            att_plan, 7 + 2 * (1 - layer),
        )
        for tensor in (1, 2):
            settle[layer][tensor] = Settle(narrow[layer][tensor].results[0], layer)
        narrow[layer][0] = Narrow(dw)
        gins[layer] = grad = gin
        d_bias[layer] = jnp.concatenate(
            [dbqkv[:, :part_width], dbqkv[:, 2 * part_width :], db1, dbproj, db2], axis=1
        )
        d_mod[layer] = jnp.concatenate([dmod1.reshape(-1), dmod2.reshape(-1)])

    last = narrow[0][0]
    final = Settle(jax.ShapeDtypeStruct((rows, units), BF16), 0, held=lambda: last.refs[1][0])
    settle[0][0] = final
    gin_first = Deliver(gins[0], 0)
    dmod = jnp.stack([d_mod[0], d_mod[1]]).reshape(2 * n_mp, 1, cols)
    g_wada, g_bada, g_act, g_bias = epilogue(
        dmod,
        act_rows,
        modulation_weight[0],
        jnp.stack([d_bias[0], d_bias[1]]),
        plan(
            [(last, "a"), (gin_first, "a"), (gin_second, "a")]
            + [(settle[0][2], "a"), (settle[1][2], "a")],
            [(last, "b"), (gin_first, "b"), (gin_second, "b"), (settle[0][2], "b"), (settle[1][2], "b")]
            + [(settle[0][1], "a"), (settle[1][1], "a")],
            [(last, "c"), (settle[0][1], "b"), (settle[1][1], "b"), (final, "a"), (settle[1][0], "a")],
            [(final, "b"), (settle[1][0], "b"), (settle[0][2], "c"), (settle[1][2], "c")],
            [(settle[0][1], "c"), (settle[1][1], "c"), (gin_first, "c"), (gin_second, "c")]
            + [(settle[1][0], "c"), (final, "c")],
        ),
        10,
    )
    g_act = g_act.transpose(1, 0, 2).reshape(2, width)
    low_section = section == 0

    def own_block(first, second):
        return jnp.where(low_section, first.results[0], second.results[0])

    g_att, g_one, g_two = [own_block(settle[0][t], settle[1][t]) for t in range(3)]
    g_qkv = g_att[:, : 3 * part_width].reshape(rows, 3, part_width)
    g_proj = g_att[:, 3 * part_width :].T

    def dp_part(vec):
        size = vec.shape[-1] // n_dp
        return lax.dynamic_slice_in_dim(vec, dp * size, size, vec.ndim - 1)

    g_bias = g_bias[0]
    g_bqv = dp_part(g_bias[: bounds[2]].reshape(2, part_width))
    g_b1 = dp_part(g_bias[bounds[2] : bounds[3]])
    g_bproj = dp_part(g_bias[bounds[3] : bounds[4]])
    g_b2 = dp_part(g_bias[bounds[4] :])
    g_bada = dp_part(g_bada[0])
    _, silu_back = jax.vjp(jax.nn.silu, cond)
    g_cond = silu_back(g_act)[0][:, None]
    acts_out = own_block(acts_first, acts_second)[None, :, None]
    grad_input = own_block(gin_first, gin_second).astype(F32)[None, :, None]
    return (
        acts_out,
        grad_input,
        g_cond,
        g_wada[None],
        g_bada[None],
        g_qkv[None],
        g_bqv[None],
        g_proj[None],
        g_bproj[None],
        g_one[None],
        g_b1[None],
        g_two.T[None],
        g_b2[None],
    )


def solution(mesh):
    sizes = mesh.shape
    grid = mesh.devices.reshape(sizes["section"], sizes["dp"], 2, sizes["mp"] // 2)
    fine = Mesh(grid, ("section", "dp", "mh", "ml"))
    mp = ("mh", "ml")
    in_specs = (
        P(None, "dp", mp, None),
        P(None, "dp", None),
        P(None, "dp", mp, None),
        P("section", "dp", mp),
        P("section", mp),
        P("section", "dp", None, mp),
        P("section", None, mp),
        P("section", mp, "dp"),
        P("section", None),
        P("section", "dp", mp),
        P("section", mp),
        P("section", mp, "dp"),
        P("section", None),
    )
    mpdp = ("mh", "ml", "dp")
    out_specs = (
        P("section", None, "dp", mp, None),
        P("section", None, "dp", mp, None),
        P(None, "dp", None),
        P("section", "dp", mp),
        P("section", mpdp),
        P("section", "dp", None, mp),
        P("section", None, mpdp),
        P("section", mp, "dp"),
        P("section", "dp"),
        P("section", "dp", mp),
        P("section", mpdp),
        P("section", mp, "dp"),
        P("section", "dp"),
    )
    return jax.shard_map(
        per_device, mesh=fine, in_specs=in_specs, out_specs=out_specs, check_vma=False
    )
```

time: 1020 us -> 643 us (0.63)
  blocking collectives: 309 us -> 0 us
  Pallas kernels: 288 us -> 596 us
  waiting for transfers between devices: 282 us -> 0 us
  starting transfers between devices: 43.3 us -> 0 us
  other arithmetic: 31.8 us -> 10.1 us
  between operations: 15.8 us -> 1.23 us
  local copies, waits for them, and re-layouts: 39.5 us -> 26 us
    pallas_call x8 -> x10, Pallas kernels: 288 us -> 596 us  [launch(): pl.pallas_call(body, out_shape=tuple((jax.ShapeDtypeStruct(shape, dtype)...]
    ppermute x7 -> x0, waiting for transfers between devices: 176 us -> none  [the longest x6 176 us: swap(): lax.ppermute(block, ('section', 'mh'), [(s * 2 + h, h * 2 + s) for s in r...]
    psum x3 -> x0, blocking collectives: 145 us -> none  [the longest x1 83.6 us: per_device(): g_act = lax.psum(g_act, ('section', 'mh', 'ml'))]
    reduce_scatter x3 -> x0, waiting for transfers between devices: 94.5 us -> none  [reduce_rows(): out = lax.psum_scatter(block, OTHERS, scatter_dimension=0, tiled=False)]
    unnamed x2 -> x0, blocking collectives: 90.1 us -> none
    all_gather x5 -> x0, blocking collectives: 74.1 us -> none  [the longest x1 42.5 us: per_device(): lax.all_gather(share, ('section', 'mh', 'ml')).reshape(2, n_mp, 2, cols)]
    ppermute x7 -> x0, starting transfers between devices: 23.5 us -> none  [the longest x6 23.4 us: swap(): lax.ppermute(block, ('section', 'mh'), [(s * 2 + h, h * 2 + s) for s in r...]
    all_to_all x4 -> x0, starting transfers between devices: 19.6 us -> none  [the longest x2 12.5 us: deliver(): block = lax.all_to_all(block, 'section', 0, 0, tiled=True)]
  transfers between devices with their start and end apart: 17 -> 0, of which waited for: 7 -> 0; matrix products, arithmetic and copies ran while one was open for 5% -> 0% of each run, Pallas kernels for 3% -> 0%
where the time goes in v2:
time: 643 us; the launch traced here: 633 us
  Pallas kernels  596 us (93%)
  local copies, waits for them, and re-layouts  26 us (4%)
  other arithmetic  10.1 us (2%)
    pallas_call x10, Pallas kernels, launch(): pl.pallas_call(body, out_shape=tuple((jax.ShapeDtypeStruct(shape, dtype)...  596 us

profile of v2, /device:TPU:4, one launch (start us, length us, event | category | flops | bytes accessed | tf_op | source)
XLA Modules:
  0.0 633.2 jit_solution(14851491664021905899)
XLA Ops:
  0.7 0.8 slice_bitcast_fusion.9
  1.4 0.8 concatenate.34
  2.3 0.6 convert_element_type.24.refs_3_
  2.9 1.4 copy.38
  4.3 0.0 copy-start.3
  4.4 0.0 copy-start.4
  4.4 0.3 copy.40
  4.7 0.2 copy.39
  4.9 0.1 maximum_bitcast_fusion
  5.0 0.4 copy-done.3
  5.4 0.2 copy-done.4
  5.6 1.5 pad_maximum_fusion.refs_5_.refs_6_.refs_7_.refs_8_.refs_9_.refs_10_
  7.2 0.0 copy-done.11
  7.2 0.1 reshape.142
  7.3 0.6 copy.49
  7.9 0.6 convert_element_type.23.refs_2_
  8.5 119.6 %prologue.1 = (f32[8,1,1728]{2,1,0:T(1,128)}, bf16[8,288]{1,0:T(8,128)(2,1)}, f32[2,1,4032]{2,1,0:T(1,128)}, bf16[128,1152]{1,0:T(8,128)(2,1)}, bf16[1152,1152]{...) custom-call(f32[4,2,288]{2,1,0:T(2,128)} %bitcast.77, ...), custom_call_target="tpu_custom_call" | custom-call | tf_op jit(solution)/shard_map/prologue/pallas_call | solution.py:879
  128.1 0.8 fusion.3
  129.0 0.1 pad.9.clone
  129.1 0.1 pad_maximum_fusion.5
  129.1 0.6 slice_bitcast_fusion.7
  129.7 1.5 slice_bitcast_fusion.1
  131.2 0.9 slice_reduce_fusion
  132.2 0.7 squeeze.64.refs_1_.refs_2_
  132.9 39.2 %att_fwd.2 = (f32[128,1152]{1,0:T(8,128)}, bf16[4,128,1152]{2,1,0:T(8,128)(2,1)}, bf16[3,4,128,288]{3,2,1,0:T(8,128)(2,1)}, bf16[4,128,288]{2,1,0:T(8,128)(2,1)}...) custom-call(bf16[128,1152]{1,0:T(8,128)(2,1)} %get-tuple-element.89.refs_0_.refs_1_, ...), custom_call_target="tpu_custom_call", output_to_operand_aliasing={{5}: (5, {})} | custom-call | tf_op jit(solution)/shard_map/att_fwd/pallas_call | solution.py:879
  172.0 36.7 %mlp_fwd.2 = (bf16[128,1152]{1,0:T(8,128)(2,1)}, bf16[4,128,1152]{2,1,0:T(8,128)(2,1)}, f32[4,128,1152]{2,1,0:T(8,128)}, bf16[4,128,1152]{2,1,0:T(8,128)(2,1)}, ...) custom-call(f32[128,1152]{1,0:T(8,128)} %get-tuple-element.94.refs_0_.refs_1_, ...), custom_call_target="tpu_custom_call", output_to_operand_aliasing={{5}: (6, {})} | custom-call | tf_op jit(solution)/shard_map/mlp_fwd/pallas_call | solution.py:879
  208.7 0.7 squeeze.69.refs_1_.refs_2_
  209.4 41.6 %att_fwd.3 = (f32[128,1152]{1,0:T(8,128)}, bf16[4,128,1152]{2,1,0:T(8,128)(2,1)}, bf16[3,4,128,288]{3,2,1,0:T(8,128)(2,1)}, bf16[4,128,288]{2,1,0:T(8,128)(2,1)}...) custom-call(bf16[128,1152]{1,0:T(8,128)(2,1)} %get-tuple-element.98., ...), custom_call_target="tpu_custom_call", output_to_operand_aliasing={{6}: (6, {}), {7}: (7, {})} | custom-call | tf_op jit(solution)/shard_map/att_fwd/pallas_call | solution.py:879
  251.0 34.9 %mlp_fwd.3 = (bf16[128,1152]{1,0:T(8,128)(2,1)}, bf16[4,128,1152]{2,1,0:T(8,128)(2,1)}, f32[4,128,1152]{2,1,0:T(8,128)}, bf16[4,128,1152]{2,1,0:T(8,128)(2,1)}, f32[128,1152]{1,0:T(8,128)}) custom-call(f32[128,1152]{1,0:T(8,128)} %get-tuple-element.103.refs_0_.refs_1_, f32[6,1152]{1,0:T(8,128)} %squeeze.69.refs_1_.refs_2_, ...), custom_call_target="tpu_custom_call" | custom-call | tf_op jit(solution)/shard_map/mlp_fwd/pallas_call | solution.py:879
  285.9 45.4 %mlp_bwd.2 = (f32[128,1152]{1,0:T(8,128)}, bf16[1152,1152]{1,0:T(8,128)(2,1)}, bf16[1152,1152]{1,0:T(8,128)(2,1)}, f32[1,1152]{1,0:T(1,128)}, f32[1,1152]{1,0:T(...) custom-call(bf16[128,1152]{1,0:T(8,128)(2,1)} %get-tuple-element.102.refs_0_, ...), custom_call_target="tpu_custom_call" | custom-call | tf_op jit(solution)/shard_map/mlp_bwd/pallas_call | solution.py:879
  331.3 50.0 %att_bwd.2 = (bf16[128,1152]{1,0:T(8,128)(2,1)}, bf16[1152,1152]{1,0:T(8,128)(2,1)}, f32[1,864]{1,0:T(1,128)}, f32[1,1152]{1,0:T(1,128)}, f32[3,1152]{1,0:T(4,12...) custom-call(f32[128,1152]{1,0:T(8,128)} %get-tuple-element.113.refs_0_, ...), custom_call_target="tpu_custom_call" | custom-call | tf_op jit(solution)/shard_map/att_bwd/pallas_call | solution.py:879
  381.3 37.9 %mlp_bwd.3 = (f32[128,1152]{1,0:T(8,128)}, bf16[1152,1152]{1,0:T(8,128)(2,1)}, bf16[1152,1152]{1,0:T(8,128)(2,1)}, f32[1,1152]{1,0:T(1,128)}, f32[1,1152]{1,0:T(...) custom-call(bf16[128,1152]{1,0:T(8,128)(2,1)} %get-tuple-element.120.refs_0_.refs_6_, ...), custom_call_target="tpu_custom_call" | custom-call | tf_op jit(solution)/shard_map/mlp_bwd/pallas_call | solution.py:879
  419.2 0.0 copy-start.17
  419.2 0.0 copy-start.18
  419.2 0.0 copy-start.19
  419.3 42.1 %att_bwd.3 = (bf16[128,1152]{1,0:T(8,128)(2,1)}, bf16[1152,1152]{1,0:T(8,128)(2,1)}, f32[1,864]{1,0:T(1,128)}, f32[1,1152]{1,0:T(1,128)}, f32[3,1152]{1,0:T(4,12...) custom-call(f32[128,1152]{1,0:T(8,128)} %get-tuple-element.126.refs_0_, ...), custom_call_target="tpu_custom_call" | custom-call | tf_op jit(solution)/shard_map/att_bwd/pallas_call | solution.py:879
  461.3 0.7 fusion.5
  462.1 0.8 concatenate.39
  462.9 0.1 fusion.6
  463.0 0.1 concatenate.40
  463.2 0.7 pad_maximum_fusion.2.refs_3_
  463.8 0.7 reshape.134
  464.7 0.1 pad_maximum_fusion.1
  464.8 0.8 reshape.138.refs_0_
  465.5 148.7 %epilogue.1 = (f32[288,1728]{1,0:T(8,128)}, f32[1,1728]{1,0:T(1,128)}, f32[4,2,288]{2,1,0:T(2,128)}, f32[1,4032]{1,0:T(1,128)}, bf16[288,1152]{1,0:T(8,128)(2,1)...) custom-call(f32[8,1,1728]{2,1,0:T(1,128)} %reshape.138.refs_0_, ...), custom_call_target="tpu_custom_call" | custom-call | tf_op jit(solution)/shard_map/epilogue/pallas_call | solution.py:879
  614.2 0.9 fusion.4
  615.1 0.6 constant_dynamic-slice_fusion
  615.7 3.6 select_bitcast_fusion
  619.3 0.1 broadcast_select_fusion
  619.5 1.0 slice.119
  620.5 1.6 copy.42
  622.2 1.6 copy.46
  623.7 0.2 slice_bitcast_fusion
  623.9 1.0 copy.47
  624.9 0.1 copy-done.6
  625.0 2.6 bitcast_convert_fusion
  627.6 0.1 reshape.139
  627.7 0.6 copy.45
  628.3 0.6 constant_dynamic-slice_fusion.2
  628.9 0.7 slice_reduce_fusion.2
  629.6 0.1 reshape.140
  629.7 0.6 fusion.2
  630.3 1.3 constant_dynamic-slice_fusion.4
  631.6 1.3 copy.55
  (41 shorter events, 0.2 us)
Async XLA Ops:
  0.6 4.0 copy-start.7
  4.3 1.1 copy-start.3
  4.4 1.3 copy-start.4
  5.6 1.5 copy-start.11
  5.6 2.2 copy-start.13
  419.2 42.9 %copy-start.17 = (f32[1,1152]{1,0:T(1,128)S(1)}, f32[1,1152]{1,0:T(1,128)}, u32[]{:S(2)}) copy-start(f32[1,1152]{1,0:T(1,128)} %get-tuple-element.139) | copy-start | bytes 13828
  419.2 42.9 %copy-start.18 = (f32[1,1152]{1,0:T(1,128)S(1)}, f32[1,1152]{1,0:T(1,128)}, u32[]{:S(2)}) copy-start(f32[1,1152]{1,0:T(1,128)} %get-tuple-element.141) | copy-start | bytes 13828
  419.2 43.7 %copy-start.19 = (f32[1,864]{1,0:T(1,128)S(1)}, f32[1,864]{1,0:T(1,128)}, u32[]{:S(2)}) copy-start(f32[1,864]{1,0:T(1,128)} %get-tuple-element.142) | copy-start | bytes 10372
  419.2 43.8 %copy-start.14 = (f32[1,1152]{1,0:T(1,128)S(1)}, f32[1,1152]{1,0:T(1,128)}, u32[]{:S(2)}) copy-start(f32[1,1152]{1,0:T(1,128)} %get-tuple-element.143) | copy-start | bytes 13828
  419.2 43.8 %copy-start.15 = (f32[1,1152]{1,0:T(1,128)S(1)}, f32[1,1152]{1,0:T(1,128)}, u32[]{:S(2)}) copy-start(f32[1,1152]{1,0:T(1,128)} %get-tuple-element.145) | copy-start | bytes 13828
  419.2 43.8 %copy-start.16 = (f32[1,1152]{1,0:T(1,128)S(1)}, f32[1,1152]{1,0:T(1,128)}, u32[]{:S(2)}) copy-start(f32[1,1152]{1,0:T(1,128)} %get-tuple-element.144) | copy-start | bytes 13828
  419.2 45.3 %copy-start.10 = (f32[3,1152]{1,0:T(4,128)S(1)}, f32[3,1152]{1,0:T(4,128)}, u32[]{:S(2)}) copy-start(f32[3,1152]{1,0:T(4,128)} %get-tuple-element.134) | copy-start | bytes 41476
  419.3 45.4 %copy-start.9 = (f32[3,1152]{1,0:T(4,128)S(1)}, f32[3,1152]{1,0:T(4,128)}, u32[]{:S(2)}) copy-start(f32[3,1152]{1,0:T(4,128)} %get-tuple-element.135) | copy-start | bytes 41476
  419.3 45.4 %copy-start.8 = (f32[3,1152]{1,0:T(4,128)S(1)}, f32[3,1152]{1,0:T(4,128)}, u32[]{:S(2)}) copy-start(f32[3,1152]{1,0:T(4,128)} %get-tuple-element.136) | copy-start | bytes 41476
  615.7 3.6 copy-start.1
  615.7 3.6 copy-start.2
  623.7 1.2 copy-start.5
  623.7 1.2 copy-start.6
  625.0 2.6 copy-start.12
  625.0 6.7 %copy-start = (f32[288,1728]{1,0:T(8,128)S(1)}, f32[288,1728]{1,0:T(8,128)}, u32[]{:S(2)}) copy-start(f32[288,1728]{1,0:T(8,128)} %get-tuple-element.156) | copy-start | bytes 5971972

commit v3 on v2

--- a/solution.py
+++ b/solution.py
@@ -15,7 +15,7 @@
 GELU_A = 0.044715
 NT = (((1,), (1,)), ((), ()))
 TN = (((0,), (0,)), ((), ()))
-VMEM_LIMIT = 60 * 1024 * 1024
+VMEM_LIMIT = 50 * 1024 * 1024
 
 
 def dot_nn(a, b):
@@ -49,10 +49,12 @@
 
 
 class Group:
-    def __init__(self):
+    def __init__(self, tokens):
         self.low = lax.axis_size("ml")
         self.size = lax.axis_size("section") * self.low
         self.me = lax.axis_index("section") * self.low + lax.axis_index("ml")
+        self.square = self.size == 4
+        self.half = (slice(0, tokens // 2), slice(tokens // 2, tokens))
 
     def device(self, member):
         return (
@@ -62,8 +64,12 @@
             lax.rem(member, self.low),
         )
 
-    def peer(self, step):
-        return lax.rem(self.me + step, self.size)
+    def member(self, step):
+        if not self.square:
+            return lax.rem(self.me + step, self.size)
+        section = lax.rem(lax.axis_index("section") + lax.rem(step, 2), 2)
+        low = lax.rem(lax.axis_index("ml") + lax.div(step, 2), 2)
+        return section * 2 + low
 
     def copy(self, src, dst, send_sem, recv_sem, member):
         return pltpu.make_async_remote_copy(
@@ -75,41 +81,129 @@
             device_id_type=MESH,
         )
 
+    def first_copies(self, buf, send_sem, recv_sem):
+        steps = (1, 2) if self.square else range(1, self.size)
+        mine = buf.at[self.me]
+        return [
+            self.copy(mine, mine, send_sem.at[step], recv_sem.at[self.me], self.member(step))
+            for step in steps
+        ]
+
+    def relay_copy(self, buf, send_sem, recv_sem, step):
+        rows = buf.at[self.member(step), self.half[step - 1]]
+        return self.copy(
+            rows, rows, send_sem.at[2 + step], recv_sem.at[3 + step], self.member(3 - step)
+        )
+
     def spread(self, buf, send_sem, recv_sem):
-        me = self.me
-        for step in range(1, self.size):
-            self.copy(
-                buf.at[me], buf.at[me], send_sem.at[step], recv_sem.at[me], self.peer(step)
-            ).start()
-
-    def spread_wait(self, buf, send_sem, recv_sem, member):
-        self.copy(buf.at[member], buf.at[member], send_sem.at[1], recv_sem.at[member], member).wait_recv()
+        for copy in self.first_copies(buf, send_sem, recv_sem):
+            copy.start()
+
+    def arrive(self, buf, send_sem, recv_sem, step):
+        def landed(rows, sem):
+            self.copy(rows, rows, send_sem.at[1], sem, self.member(1)).wait_recv()
+
+        if not self.square:
+            landed(buf.at[self.member(step)], recv_sem.at[self.member(step)])
+            return
+
+        @pl.when(step == 1)
+        def _():
+            for near in (1, 2):
+                landed(buf.at[self.member(near)], recv_sem.at[self.member(near)])
+                self.relay_copy(buf, send_sem, recv_sem, near).start()
+
+        @pl.when(step == 3)
+        def _():
+            for near in (1, 2):
+                landed(buf.at[self.member(3), self.half[near - 1]], recv_sem.at[3 + near])
 
     def spread_sent(self, buf, send_sem, recv_sem):
-        me = self.me
-        for step in range(1, self.size):
-            self.copy(
-                buf.at[me], buf.at[me], send_sem.at[step], recv_sem.at[me], self.peer(step)
-            ).wait_send()
+        for copy in self.first_copies(buf, send_sem, recv_sem):
+            copy.wait_send()
+        if self.square:
+            for step in (1, 2):
+                self.relay_copy(buf, send_sem, recv_sem, step).wait_send()
+
+    def straight(self, stage, landing, send_sem, recv_sem, step):
+        rows = self.half[step - 1]
+        return self.copy(
+            stage.at[self.member(step), rows], landing.at[step - 1, rows],
+            send_sem.at[step - 1], recv_sem.at[step - 1], self.member(step),
+        )
+
+    def corner(self, stage, landing, send_sem, recv_sem, step):
+        rows = self.half[step - 1]
+        return self.copy(
+            stage.at[self.member(3), rows], landing.at[2, rows],
+            send_sem.at[1 + step], recv_sem.at[1 + step], self.member(step),
+        )
+
+    def summed(self, landing, send_sem, recv_sem, step):
+        rows = self.half[2 - step]
+        return self.copy(
+            landing.at[3, rows], landing.at[step - 1, rows],
+            send_sem.at[3 + step], recv_sem.at[3 + step], self.member(step),
+        )
 
     def reduce_copy(self, stage, landing, send_sem, recv_sem, member):
         return self.copy(
             stage.at[member], landing.at[self.me], send_sem.at[member], recv_sem.at[self.me], member
         )
 
-    def reduce_wait(self, landing, send_sem, recv_sem, member):
-        self.copy(
-            landing.at[member], landing.at[member], send_sem.at[member], recv_sem.at[member], member
-        ).wait_recv()
+    def give(self, stage, landing, send_sem, recv_sem, step):
+        args = (stage, landing, send_sem, recv_sem)
+        if not self.square:
+            self.reduce_copy(*args, self.member(step)).start()
+            return
+        for near in (1, 2):
+
+            @pl.when(step == near)
+            def _():
+                self.straight(*args, near).start()
+
+        @pl.when(step == 3)
+        def _():
+            for near in (1, 2):
+                self.corner(*args, near).start()
+
+    def combine(self, stage, landing, send_sem, recv_sem):
+        if not self.square:
+            return
+        for step in (1, 2):
+            rows = self.half[2 - step]
+            self.copy(
+                landing.at[2, rows], landing.at[2, rows], send_sem.at[0], recv_sem.at[4 - step],
+                self.member(1),
+            ).wait_recv()
+            total = stage[self.member(step), rows].astype(F32) + landing[2, rows].astype(F32)
+            landing[3, rows] = total.astype(BF16)
+            self.summed(landing, send_sem, recv_sem, step).start()
 
     def landed_sum(self, own, stage, landing, send_sem, recv_sem):
+        args = (stage, landing, send_sem, recv_sem)
         total = own
+
+        def landed(rows, sem):
+            self.copy(rows, rows, send_sem.at[0], sem, self.member(1)).wait_recv()
+
+        if self.square:
+            for step in (1, 2):
+                first, second = self.half[step - 1], self.half[2 - step]
+                landed(landing.at[step - 1, first], recv_sem.at[step - 1])
+                landed(landing.at[step - 1, second], recv_sem.at[3 + step])
+                total = total + landing[step - 1].astype(F32)
+            for step in (1, 2):
+                self.straight(*args, step).wait_send()
+                self.corner(*args, step).wait_send()
+                self.summed(landing, send_sem, recv_sem, step).wait_send()
+            return total
         for step in range(1, self.size):
-            member = self.peer(step)
-            self.reduce_wait(landing, send_sem, recv_sem, member)
+            member = self.member(step)
+            landed(landing.at[member], recv_sem.at[member])
             total = total + landing[member].astype(F32)
         for step in range(1, self.size):
-            self.reduce_copy(stage, landing, send_sem, recv_sem, self.peer(step)).wait_send()
+            self.reduce_copy(*args, self.member(step)).wait_send()
         return total
 
 
@@ -149,9 +243,9 @@
     middle_ref, normed_ref, proj_ref, att_ref, branch_ref,
     w_buf, wo_buf, stage, landing, w_sem, ag_send, ag_recv, rs_send, rs_recv,
 ):
-    group = Group()
+    tokens, width = hidden_ref.shape
+    group = Group(tokens)
     me, size = group.me, group.size
-    tokens, width = hidden_ref.shape
     part_width = att_ref.shape[-1]
     heads = part_width // HEAD_SIZE
     loads = load(w_ref, w_buf, w_sem.at[0])
@@ -165,12 +259,9 @@
         copy.wait()
 
     def project(step, carry):
-        member = group.peer(step)
-
-        @pl.when(step > 0)
-        def _():
-            group.spread_wait(normed_ref, ag_send, ag_recv, member)
-
+        member = group.member(step)
+        if not isinstance(step, int):
+            group.arrive(normed_ref, ag_send, ag_recv, step)
         out = dot_nn(normed_ref[member], w_buf[:, : 3 * part_width]) + bias_ref[...]
         for part in range(3):
             cols = slice(part * part_width, (part + 1) * part_width)
@@ -178,7 +269,8 @@
         return carry
 
     wo_buf[...] = w_buf[:, 3 * part_width :]
-    lax.fori_loop(0, size, project, 0)
+    project(0, 0)
+    lax.fori_loop(1, size, project, 0)
     bg(1)
     seq = size * tokens
     keys = proj_ref[1].reshape(seq, -1)
@@ -198,12 +290,13 @@
         return dot_nt(low, wo_buf[...])
 
     def send(step, carry):
-        member = group.peer(step)
+        member = group.member(size - step)
         stage[member] = attend(member).astype(BF16)
-        group.reduce_copy(stage, landing, rs_send, rs_recv, member).start()
+        group.give(stage, landing, rs_send, rs_recv, size - step)
         return carry
 
     lax.fori_loop(1, size, send, 0)
+    group.combine(stage, landing, rs_send, rs_recv)
     bg(2)
     own = attend(me)
     group.spread_sent(normed_ref, ag_send, ag_recv)
@@ -220,7 +313,7 @@
     out_ref, normed_ref, pre_ref, gelu_ref, branch_ref,
     w1_buf, w2_buf, stage, landing, w_sem, ag_send, ag_recv, rs_send, rs_recv,
 ):
-    group = Group()
+    group = Group(middle_ref.shape[0])
     me, size = group.me, group.size
     loads = load(w1_ref, w1_buf, w_sem.at[0]) + load(w2_ref, w2_buf, w_sem.at[1])
     normed, _ = norm_parts(middle_ref[...])
@@ -242,15 +335,16 @@
     own = dense(me)
 
     def send(step, carry):
-        member = group.peer(step)
-        group.spread_wait(normed_ref, ag_send, ag_recv, member)
+        member = group.member(step)
+        group.arrive(normed_ref, ag_send, ag_recv, step)
         stage[member] = dense(member).astype(BF16)
-        group.reduce_copy(stage, landing, rs_send, rs_recv, member).start()
+        group.give(stage, landing, rs_send, rs_recv, step)
         return carry
 
     stage[me] = own.astype(BF16)
     bg(1)
     lax.fori_loop(1, size, send, 0)
+    group.combine(stage, landing, rs_send, rs_recv)
     bg(2)
     group.spread_sent(normed_ref, ag_send, ag_recv)
     bg(3)
@@ -276,9 +370,9 @@
     gmid_ref, dw1_ref, dw2_ref, db1_ref, db2_ref, dmod_ref,
     w1_buf, w2_buf, dbr, dpre, stage, landing, w_sem, ag_send, ag_recv, rs_send, rs_recv,
 ):
-    group = Group()
+    tokens, width = grad_ref.shape
+    group = Group(tokens)
     me, size = group.me, group.size
-    tokens, width = grad_ref.shape
     loads = load(w1_ref, w1_buf, w_sem.at[0]) + load(w2_ref, w2_buf, w_sem.at[1])
     grad = grad_ref[...].astype(F32)
     dbr[me] = (grad * mod_ref[5:6]).astype(BF16)
@@ -304,13 +398,14 @@
     bg(1)
 
     def send(step, carry):
-        member = group.peer(step)
-        group.spread_wait(dbr, ag_send, ag_recv, member)
+        member = group.member(step)
+        group.arrive(dbr, ag_send, ag_recv, step)
         stage[member] = back(member).astype(BF16)
-        group.reduce_copy(stage, landing, rs_send, rs_recv, member).start()
+        group.give(stage, landing, rs_send, rs_recv, step)
         return carry
 
     lax.fori_loop(1, size, send, 0)
+    group.combine(stage, landing, rs_send, rs_recv)
     bg(2)
     seq = size * tokens
     dpre_all = dpre[...].reshape(seq, -1)
@@ -335,9 +430,9 @@
     gin_ref, dw_ref, dbqkv_ref, dbproj_ref, dmod_ref,
     w_buf, wo_buf, dba, dproj, dkey, dval, stage, landing, w_sem, ag_send, ag_recv, rs_send, rs_recv,
 ):
-    group = Group()
+    tokens, width = gmid_ref.shape
+    group = Group(tokens)
     me, size = group.me, group.size
-    tokens, width = gmid_ref.shape
     seq = size * tokens
     part_width = att_ref.shape[-1]
     heads = part_width // HEAD_SIZE
@@ -358,10 +453,9 @@
     wo_buf[...] = w_buf[:, 3 * part_width :]
 
     def back(step, carry):
-        member = group.peer(step)
-
+        member = group.member(step)
         if not isinstance(step, int):
-            group.spread_wait(dba, ag_send, ag_recv, member)
+            group.arrive(dba, ag_send, ag_recv, step)
         datt = dot_nn(dba[member], wo_buf[...]).astype(BF16)
         datt_st = stack_heads(datt)
         query_st = stack_heads(proj_ref[0, member])
@@ -392,13 +486,14 @@
         return dot_nt(dproj[member], w_buf[:, : 3 * part_width])
 
     def send(step, carry):
-        member = group.peer(step)
+        member = group.member(size - step)
         stage[member] = partial_rows(member).astype(BF16)
-        group.reduce_copy(stage, landing, rs_send, rs_recv, member).start()
+        group.give(stage, landing, rs_send, rs_recv, size - step)
         return carry
 
     lax.fori_loop(1, size, send, 0)
     stage[me] = partial_rows(me).astype(BF16)
+    group.combine(stage, landing, rs_send, rs_recv)
     bg(2)
     grads = dproj[...].reshape(seq, -1)
     dbqkv_ref[...] = col_sum(grads.astype(F32))
@@ -525,7 +620,7 @@
 
 
 VM = pl.BlockSpec(memory_space=pltpu.VMEM)
-ANY = pl.BlockSpec(memory_space=pl.ANY)
+ANY = pl.BlockSpec(memory_space=pltpu.HBM)
 DMA = pltpu.SemaphoreType.DMA
 
 
@@ -729,18 +824,22 @@
 
             @pl.when(place.role(layer, role))
             def _():
+                if phase == "z" and role == 1:
+                    direct(role).start()
                 if phase == "a":
-                    if role:
+                    if role > 1:
                         direct(role).start()
-                    else:
+                    if role == 0:
                         pltpu.make_async_copy(part, land.at[1], own_sem).start()
                 if phase == "b":
                     if role == 0:
                         to(temp, temp, 0, 2, 0).wait_recv()
                         relay().start()
-                    else:
+                    if role > 1:
                         direct(role).wait_send()
                 if phase == "c":
+                    if role == 1:
+                        direct(role).wait_send()
                     if role == 0:
                         pltpu.make_async_copy(part, land.at[1], own_sem).wait()
                         relay().wait_send()
@@ -779,10 +878,12 @@
 
             @pl.when(place.role(layer, role))
             def _():
+                if phase == "z" and role == 1:
+                    direct(role).start()
                 if phase == "a":
-                    if role:
+                    if role > 1:
                         direct(role).start()
-                    else:
+                    if role == 0:
                         out[layer] = rows[...]
                 if phase == "b" and role == 0:
                     to(temp, temp, 0, 2, 0).wait_recv()
@@ -802,28 +903,36 @@
     def __init__(self, rows):
         self.inputs = ((rows, VM),)
         self.outs = ((rows.shape[1:], rows.dtype, VM),)
-        self.scratch = (DMA, DMA)
+        self.scratch = (DMA, DMA((2,)))
 
     def run(self, phase, refs):
         (rows,), (out,), (send, recv) = refs
         place = Place()
-        local = place.section == place.high
-        copy = place.copy(
-            rows.at[1 - place.high], out, send, recv, place.plane(place.section, 1 - place.high)
-        )
-
-        @pl.when(local)
+        half = rows.shape[1] // 2
+        parts = (slice(0, half), slice(half, 2 * half))
+
+        def copy(part, section):
+            return place.copy(
+                rows.at[1 - place.high, parts[part]], out.at[parts[part]], send, recv.at[part],
+                place.plane(section, 1 - place.high),
+            )
+
+        @pl.when(place.section == place.high)
         def _():
             if phase == "a":
-                copy.start()
+                copy(0, place.section).start()
                 out[...] = rows[place.high]
             if phase == "c":
-                copy.wait_send()
-
-        @pl.when(jnp.logical_not(local))
+                copy(0, place.section).wait_send()
+
+        @pl.when(place.section != place.high)
         def _():
+            if phase == "a":
+                copy(1, 1 - place.section).start()
             if phase == "c":
-                copy.wait_recv()
+                copy(1, 1 - place.section).wait_send()
+                copy(0, place.section).wait_recv()
+                copy(1, place.section).wait_recv()
 
 
 def launch(kernel, operands, outs, scratch, schedule, cid, name):
@@ -902,7 +1011,7 @@
 
 def comm_scratch(tokens, width):
     size = group_size()
-    return [pltpu.VMEM((size, tokens, width), BF16)] * 2, [DMA((size,))] * 4
+    return [pltpu.VMEM((size, tokens, width), BF16)] * 2, [DMA((max(size, 6),))] * 4
 
 
 def att_fwd(hidden, mod, bias, bproj, w, schedule, cid):
@@ -1392,7 +1501,7 @@
         middle, normed, proj, att, branch, normed2, pre, gelu, branch2 = saved[layer]
         if layer == 1:
             mlp_plan = plan(
-                [(acts_first, "a"), (acts_second, "a")],
+                [(acts_first, "az"), (acts_second, "az")],
                 [],
                 [(acts_first, "b"), (acts_second, "b")],
                 [],
@@ -1437,12 +1546,12 @@
         modulation_weight[0],
         jnp.stack([d_bias[0], d_bias[1]]),
         plan(
-            [(last, "a"), (gin_first, "a"), (gin_second, "a")]
-            + [(settle[0][2], "a"), (settle[1][2], "a")],
-            [(last, "b"), (gin_first, "b"), (gin_second, "b"), (settle[0][2], "b"), (settle[1][2], "b")]
-            + [(settle[0][1], "a"), (settle[1][1], "a")],
-            [(last, "c"), (settle[0][1], "b"), (settle[1][1], "b"), (final, "a"), (settle[1][0], "a")],
-            [(final, "b"), (settle[1][0], "b"), (settle[0][2], "c"), (settle[1][2], "c")],
+            [(last, "a"), (settle[0][2], "az"), (settle[1][2], "az")],
+            [(settle[0][2], "b"), (settle[1][2], "b"), (settle[0][1], "az"), (settle[1][1], "az")]
+            + [(last, "b"), (gin_first, "az"), (gin_second, "az")],
+            [(settle[0][1], "b"), (settle[1][1], "b"), (settle[1][0], "az"), (last, "c"), (final, "az")]
+            + [(gin_first, "b"), (gin_second, "b")],
+            [(settle[1][0], "b"), (final, "b"), (settle[0][2], "c"), (settle[1][2], "c")],
             [(settle[0][1], "c"), (settle[1][1], "c"), (gin_first, "c"), (gin_second, "c")]
             + [(settle[1][0], "c"), (final, "c")],
         ),

time: 643 us -> 570 us (0.89)
  Pallas kernels: 596 us -> 519 us
  local copies, waits for them, and re-layouts: 26 us -> 34.3 us
    pallas_call x10, Pallas kernels: 596 us -> 519 us  [launch(): pl.pallas_call(body, out_shape=tuple((jax.ShapeDtypeStruct(shape, dtype)...]
    unnamed x46 -> x70, local copies, waits for them, and re-layouts: 6.88 us -> 23 us
where the time goes in v3:
time: 570 us; the launch traced here: 563 us
  Pallas kernels  519 us (91%)
  local copies, waits for them, and re-layouts  34.3 us (6%)
  other arithmetic  8.2 us (1%)
    pallas_call x10, Pallas kernels, launch(): pl.pallas_call(body, out_shape=tuple((jax.ShapeDtypeStruct(shape, dtype)...  519 us
    unnamed x70, local copies, waits for them, and re-layouts  23 us

profile of v3, /device:TPU:4, one launch (start us, length us, event | category | flops | bytes accessed | tf_op | source)
XLA Modules:
  0.0 562.6 jit_solution(3796484146172491644)
XLA Ops:
  0.7 0.8 slice_bitcast_fusion.9
  1.4 0.8 concatenate.34
  2.3 1.4 copy.38
  3.7 0.3 copy.40
  4.1 0.2 copy.39
  4.2 0.1 maximum_bitcast_fusion
  4.4 1.6 pad_maximum_fusion.refs_5_.refs_6_.refs_7_.refs_8_.refs_9_.refs_10_
  6.1 0.1 reshape.142
  6.2 1.1 copy-done.11
  7.3 107.9 %prologue.1 = (f32[8,1,1728]{2,1,0:T(1,128)S(1)}, bf16[8,288]{1,0:T(8,128)(2,1)S(1)}, f32[2,1,4032]{2,1,0:T(1,128)S(1)}, bf16[128,1152]{1,0:T(8,128)(2,1)S(1)}, ...) custom-call(f32[4,2,288]{2,1,0:T(2,128)S(1)} %bitcast.70, ...), custom_call_target="tpu_custom_call" | custom-call | tf_op jit(solution)/shard_map/prologue/pallas_call | solution.py:988
  115.1 0.1 fusion.3
  115.2 0.1 pad.9.clone
  115.3 0.1 pad_maximum_fusion.5
  115.4 0.1 slice_bitcast_fusion.1
  115.5 0.2 slice_reduce_fusion
  115.7 0.1 squeeze.64.refs_1_.refs_2_
  115.8 30.8 %att_fwd.2 = (f32[128,1152]{1,0:T(8,128)S(1)}, bf16[4,128,1152]{2,1,0:T(8,128)(2,1)S(1)}, bf16[3,4,128,288]{3,2,1,0:T(8,128)(2,1)}, bf16[4,128,288]{2,1,0:T(8,12...) custom-call(bf16[128,1152]{1,0:T(8,128)(2,1)S(1)} %get-tuple-element.89.refs_0_., ...), custom_call_target="tpu_custom_call", output_to_operand_aliasing={{5}: (5, {})} | custom-call | tf_op jit(solution)/shard_map/att_fwd/pallas_call | solution.py:988
  146.6 1.0 copy-done.1
  147.6 0.8 copy-done.15
  148.4 0.7 copy-done.23
  149.2 26.1 %mlp_fwd.2 = (bf16[128,1152]{1,0:T(8,128)(2,1)S(1)}, bf16[4,128,1152]{2,1,0:T(8,128)(2,1)S(1)}, f32[4,128,1152]{2,1,0:T(8,128)}, bf16[4,128,1152]{2,1,0:T(8,128)...) custom-call(f32[128,1152]{1,0:T(8,128)S(1)} %get-tuple-element.94.refs_0_.refs_1_,, ...), custom_call_target="tpu_custom_call", output_to_operand_aliasing={{5}: (6, {})} | custom-call | tf_op jit(solution)/shard_map/mlp_fwd/pallas_call | solution.py:988
  175.3 1.0 copy-done.2
  176.3 0.8 copy-done.21
  177.1 0.1 squeeze.69.refs_1_.refs_2_
  177.2 35.0 %att_fwd.3 = (f32[128,1152]{1,0:T(8,128)S(1)}, bf16[4,128,1152]{2,1,0:T(8,128)(2,1)S(1)}, bf16[3,4,128,288]{3,2,1,0:T(8,128)(2,1)}, bf16[4,128,288]{2,1,0:T(8,12...) custom-call(bf16[128,1152]{1,0:T(8,128)(2,1)S(1)} %get-tuple-element, ...), custom_call_target="tpu_custom_call", output_to_operand_aliasing={{6}: (6, {}), {7}: (7, {})} | custom-call | tf_op jit(solution)/shard_map/att_fwd/pallas_call | solution.py:988
  212.3 1.0 copy-done.3
  213.3 28.1 %mlp_fwd.3 = (bf16[128,1152]{1,0:T(8,128)(2,1)S(1)}, bf16[4,128,1152]{2,1,0:T(8,128)(2,1)S(1)}, f32[4,128,1152]{2,1,0:T(8,128)}, bf16[4,128,1152]{2,1,0:T(8,128)(2,1)S(1)}, f32[128,1152]{1,0:T(8,128)S(1)}) custom-call(f32[128,1152]{1,0:T(8,128)S(1)} %get-tuple-element.103.refs_0_.refs_1_, f32[6,1152]{1,0:T(8,128)S(1)} %squeeze.69.refs_1_.refs_2_, ...), custom_call_target="tpu_custom_call" | custom-call | tf_op jit(solution)/shard_map/mlp_fwd/pallas_call | solution.py:988
  241.4 1.0 copy-done.4
  242.4 1.0 copy-done.5
  243.4 42.3 %mlp_bwd.2 = (f32[128,1152]{1,0:T(8,128)S(1)}, bf16[1152,1152]{1,0:T(8,128)(2,1)}, bf16[1152,1152]{1,0:T(8,128)(2,1)}, f32[1,1152]{1,0:T(1,128)S(1)}, f32[1,1152...) custom-call(bf16[128,1152]{1,0:T(8,128)(2,1)S(1)} %get-tuple-element, ...), custom_call_target="tpu_custom_call" | custom-call | tf_op jit(solution)/shard_map/mlp_bwd/pallas_call | solution.py:988
  285.7 0.8 copy-done.13
  286.5 38.6 %att_bwd.2 = (bf16[128,1152]{1,0:T(8,128)(2,1)S(1)}, bf16[1152,1152]{1,0:T(8,128)(2,1)}, f32[1,864]{1,0:T(1,128)S(1)}, f32[1,1152]{1,0:T(1,128)S(1)}, f32[3,1152...) custom-call(f32[128,1152]{1,0:T(8,128)S(1)} %get-tuple-element.113.refs_0_, ...), custom_call_target="tpu_custom_call" | custom-call | tf_op jit(solution)/shard_map/att_bwd/pallas_call | solution.py:988
  325.1 0.8 copy-done.6
  325.9 0.8 copy-done.8
  326.8 36.8 %mlp_bwd.3 = (f32[128,1152]{1,0:T(8,128)S(1)}, bf16[1152,1152]{1,0:T(8,128)(2,1)}, bf16[1152,1152]{1,0:T(8,128)(2,1)}, f32[1,1152]{1,0:T(1,128)S(1)}, f32[1,1152...) custom-call(bf16[128,1152]{1,0:T(8,128)(2,1)S(1)} %get-tuple-element.120.refs_0_.refs_10_, ...), custom_call_target="tpu_custom_call" | custom-call | tf_op jit(solution)/shard_map/mlp_bwd/pallas_call | solution.py:988
  363.6 0.8 copy-done.9
  364.5 38.0 %att_bwd.3 = (bf16[128,1152]{1,0:T(8,128)(2,1)S(1)}, bf16[1152,1152]{1,0:T(8,128)(2,1)}, f32[1,864]{1,0:T(1,128)S(1)}, f32[1,1152]{1,0:T(1,128)S(1)}, f32[3,1152...) custom-call(f32[128,1152]{1,0:T(8,128)S(1)} %get-tuple-element.126.refs_0_, ...), custom_call_target="tpu_custom_call" | custom-call | tf_op jit(solution)/shard_map/att_bwd/pallas_call | solution.py:988
  402.5 0.7 copy-done.25
  403.2 0.1 fusion.5
  403.3 0.1 concatenate.39
  403.4 0.1 fusion.6
  403.5 0.1 concatenate.40
  403.9 0.1 reshape.138.refs_0_
  404.0 1.0 copy-done.26
  405.0 135.0 %epilogue.1 = (f32[288,1728]{1,0:T(8,128)}, f32[1,1728]{1,0:T(1,128)S(1)}, f32[4,2,288]{2,1,0:T(2,128)S(1)}, f32[1,4032]{1,0:T(1,128)S(1)}, bf16[288,1152]{1,0:T...) custom-call(f32[8,1,1728]{2,1,0:T(1,128)S(1)} %reshape.138.refs_0_, ...), custom_call_target="tpu_custom_call" | custom-call | tf_op jit(solution)/shard_map/epilogue/pallas_call | solution.py:988
  540.1 0.8 copy-done.17
  540.9 0.8 copy-done.19
  541.7 0.1 fusion.4
  541.8 0.6 constant_dynamic-slice_fusion
  542.4 3.6 select_bitcast_fusion
  546.1 1.2 broadcast_select_fusion
  547.3 2.2 slice.119
  549.5 1.6 copy.42
  551.2 1.6 copy.46
  552.7 1.3 slice_bitcast_fusion
  554.1 1.0 copy.47
  555.0 1.4 bitcast_convert_fusion
  556.4 0.1 reshape.139
  556.5 0.6 copy.45
  557.1 0.6 constant_dynamic-slice_fusion.2
  557.8 0.1 reshape.140
  557.9 0.6 fusion.2
  558.5 0.7 constant_dynamic-slice_fusion.4
  559.2 3.0 copy.55
  (65 shorter events, 0.4 us)
Async XLA Ops:
  0.6 3.4 copy-start.29
  4.4 1.7 copy-start.30
  4.4 1.8 copy-start.31
  4.4 1.8 copy-start
  6.2 1.1 copy-start.11
  146.6 1.0 copy-start.1
  147.6 0.8 copy-start.15
  148.4 0.7 copy-start.23
  149.2 28.0 %copy-start.12 = (bf16[2,1,128,1152]{3,2,1,0:T(8,128)(2,1)S(1)}, bf16[2,1,128,1152]{3,2,1,0:T(8,128)(2,1)}, u32[]{:S(2)}) copy-start(bf16[2,1,128,1152]{3,2,1,0:T(8,128)(2,1)} %param.15) | copy-start | bytes 1769476
  175.3 1.0 copy-start.2
  176.3 0.8 copy-start.21
  212.2 1.0 copy-start.3
  241.4 1.0 copy-start.4
  242.4 1.0 copy-start.5
  285.7 0.8 copy-start.13
  286.5 40.3 %copy-start.22 = (f32[128,1152]{1,0:T(8,128)S(1)}, f32[128,1152]{1,0:T(8,128)}, u32[]{:S(2)}) copy-start(f32[128,1152]{1,0:T(8,128)} %copy-done.21) | copy-start | bytes 1769476
  325.1 0.8 copy-start.6
  325.9 0.8 copy-start.8
  326.8 37.7 %copy-start.16 = (f32[128,1152]{1,0:T(8,128)S(1)}, f32[128,1152]{1,0:T(8,128)}, u32[]{:S(2)}) copy-start(f32[128,1152]{1,0:T(8,128)} %copy-done.15) | copy-start | bytes 1769476
  326.8 37.7 %copy-start.24 = (bf16[4,128,288]{2,1,0:T(8,128)(2,1)S(1)}, bf16[4,128,288]{2,1,0:T(8,128)(2,1)}, u32[]{:S(2)}) copy-start(bf16[4,128,288]{2,1,0:T(8,128)(2,1)} %copy-done.23) | copy-start | bytes 884740
  363.6 0.8 copy-start.9
  364.5 39.6 %copy-start.7 = (bf16[288,1152]{1,0:T(8,128)(2,1)S(1)}, bf16[288,1152]{1,0:T(8,128)(2,1)}, u32[]{:S(2)}) copy-start(bf16[288,1152]{1,0:T(8,128)(2,1)} %copy-done.6) | copy-start | bytes 1990660
  402.5 0.7 copy-start.25
  403.2 0.8 copy-start.10
  404.0 1.0 copy-start.26
  540.0 0.8 copy-start.17
  540.9 0.8 copy-start.19
  542.4 3.6 copy-start.27
  542.4 3.6 copy-start.28
  552.7 2.3 copy-start.14
  552.7 2.3 copy-start.18
  552.7 2.3 copy-start.20

commit v4 on v3

--- a/solution.py
+++ b/solution.py
@@ -104,7 +104,11 @@
             self.copy(rows, rows, send_sem.at[1], sem, self.member(1)).wait_recv()
 
         if not self.square:
-            landed(buf.at[self.member(step)], recv_sem.at[self.member(step)])
+
+            @pl.when(step > 0)
+            def _():
+                landed(buf.at[self.member(step)], recv_sem.at[self.member(step)])
+
             return
 
         @pl.when(step == 1)
@@ -154,7 +158,11 @@
     def give(self, stage, landing, send_sem, recv_sem, step):
         args = (stage, landing, send_sem, recv_sem)
         if not self.square:
-            self.reduce_copy(*args, self.member(step)).start()
+
+            @pl.when(step > 0)
+            def _():
+                self.reduce_copy(*args, self.member(step)).start()
+
             return
         for near in (1, 2):
 
@@ -260,8 +268,7 @@
 
     def project(step, carry):
         member = group.member(step)
-        if not isinstance(step, int):
-            group.arrive(normed_ref, ag_send, ag_recv, step)
+        group.arrive(normed_ref, ag_send, ag_recv, step)
         out = dot_nn(normed_ref[member], w_buf[:, : 3 * part_width]) + bias_ref[...]
         for part in range(3):
             cols = slice(part * part_width, (part + 1) * part_width)
@@ -269,8 +276,7 @@
         return carry
 
     wo_buf[...] = w_buf[:, 3 * part_width :]
-    project(0, 0)
-    lax.fori_loop(1, size, project, 0)
+    lax.fori_loop(0, size, project, 0)
     bg(1)
     seq = size * tokens
     keys = proj_ref[1].reshape(seq, -1)
@@ -290,17 +296,20 @@
         return dot_nt(low, wo_buf[...])
 
     def send(step, carry):
+        @pl.when(step == size)
+        def _():
+            group.combine(stage, landing, rs_send, rs_recv)
+            bg(2)
+
         member = group.member(size - step)
         stage[member] = attend(member).astype(BF16)
         group.give(stage, landing, rs_send, rs_recv, size - step)
         return carry
 
-    lax.fori_loop(1, size, send, 0)
-    group.combine(stage, landing, rs_send, rs_recv)
-    bg(2)
-    own = attend(me)
+    lax.fori_loop(1, size + 1, send, 0)
     group.spread_sent(normed_ref, ag_send, ag_recv)
     bg(3)
+    own = stage[me].astype(F32)
     branch = group.landed_sum(own, stage, landing, rs_send, rs_recv) + bproj_ref[...]
     branch_ref[...] = branch
     middle_ref[...] = hidden_ref[...].astype(F32) + mod_ref[2:3] * branch
@@ -332,18 +341,18 @@
         gelu_ref[member] = low
         return dot_nt(low, w2_buf[...])
 
-    own = dense(me)
-
     def send(step, carry):
+        @pl.when(step == 1)
+        def _():
+            bg(1)
+
         member = group.member(step)
         group.arrive(normed_ref, ag_send, ag_recv, step)
         stage[member] = dense(member).astype(BF16)
         group.give(stage, landing, rs_send, rs_recv, step)
         return carry
 
-    stage[me] = own.astype(BF16)
-    bg(1)
-    lax.fori_loop(1, size, send, 0)
+    lax.fori_loop(0, size, send, 0)
     group.combine(stage, landing, rs_send, rs_recv)
     bg(2)
     group.spread_sent(normed_ref, ag_send, ag_recv)
@@ -453,9 +462,12 @@
     wo_buf[...] = w_buf[:, 3 * part_width :]
 
     def back(step, carry):
+        @pl.when(step == 1)
+        def _():
+            bg(1)
+
         member = group.member(step)
-        if not isinstance(step, int):
-            group.arrive(dba, ag_send, ag_recv, step)
+        group.arrive(dba, ag_send, ag_recv, step)
         datt = dot_nn(dba[member], wo_buf[...]).astype(BF16)
         datt_st = stack_heads(datt)
         query_st = stack_heads(proj_ref[0, member])
@@ -474,9 +486,7 @@
         dproj[member, :, :part_width] = dot_nt(identity(tokens), low).astype(BF16)
         return carry
 
-    back(0, 0)
-    bg(1)
-    lax.fori_loop(1, size, back, 0)
+    lax.fori_loop(0, size, back, 0)
     for member in range(size):
         rows = slice(member * tokens, (member + 1) * tokens)
         dproj[member, :, part_width : 2 * part_width] = (dkey[rows] * HEAD_SIZE**-0.5).astype(BF16)
@@ -491,8 +501,7 @@
         group.give(stage, landing, rs_send, rs_recv, size - step)
         return carry
 
-    lax.fori_loop(1, size, send, 0)
-    stage[me] = partial_rows(me).astype(BF16)
+    lax.fori_loop(1, size + 1, send, 0)
     group.combine(stage, landing, rs_send, rs_recv)
     bg(2)
     grads = dproj[...].reshape(seq, -1)
@@ -793,18 +802,20 @@
 
 
 class Settle(Task):
-    def __init__(self, part, layer, held=None):
+    def __init__(self, part, layer, held=None, into=None):
         self.layer = layer
         self.held = held
+        self.into = into
         self.inputs = () if held else ((part, ANY),)
-        self.outs = ((part.shape, F32, VM),)
+        self.outs = () if into else ((part.shape, F32, VM),)
         self.scratch = (
             pltpu.VMEM((2,) + part.shape, BF16), pltpu.VMEM(part.shape, BF16),
             DMA((2,)), DMA((3,)), DMA,
         )
 
     def run(self, phase, refs):
-        ins, (out,), (land, temp, send, recv, own_sem) = refs
+        ins, outs, (land, temp, send, recv, own_sem) = refs
+        (out,) = self.into.refs[1] if self.into else outs
         part = self.held() if self.held else ins[0]
         place = Place()
         layer = self.layer
@@ -837,12 +848,14 @@
                         relay().start()
                     if role > 1:
                         direct(role).wait_send()
-                if phase == "c":
+                if phase == "s":
+                    if role == 0:
+                        relay().wait_send()
                     if role == 1:
                         direct(role).wait_send()
+                if phase == "c":
                     if role == 0:
                         pltpu.make_async_copy(part, land.at[1], own_sem).wait()
-                        relay().wait_send()
                     if role < 2:
                         to(land.at[0], land.at[0], 0, 0, role).wait_recv()
                     if role == 1:
@@ -852,14 +865,16 @@
 
 
 class Deliver(Task):
-    def __init__(self, rows, layer):
+    def __init__(self, rows, layer, into=None):
         self.layer = layer
+        self.into = into
         self.inputs = ((rows, VM),)
-        self.outs = (((2,) + rows.shape, rows.dtype, VM),)
+        self.outs = () if into else (((2,) + rows.shape, rows.dtype, VM),)
         self.scratch = (pltpu.VMEM(rows.shape, rows.dtype), DMA((2,)), DMA((3,)))
 
     def run(self, phase, refs):
-        (rows,), (out,), (temp, send, recv) = refs
+        (rows,), outs, (temp, send, recv) = refs
+        (out,) = self.into.refs[1] if self.into else outs
         place = Place()
         layer = self.layer
 
@@ -1383,7 +1398,7 @@
     output_proj_weight, output_proj_bias, first_dense_weight, first_dense_bias,
     second_dense_weight, second_dense_bias,
 ):
-    section, dp = lax.axis_index("section"), lax.axis_index("dp")
+    dp = lax.axis_index("dp")
     n_dp, n_low = lax.axis_size("dp"), lax.axis_size("ml")
     n_mp = 2 * n_low
     width = latents_in.shape[-1]
@@ -1496,7 +1511,7 @@
     narrow = [[None] * 3 for _ in range(2)]
     settle = [[None] * 3 for _ in range(2)]
     d_bias, d_mod, gins = {}, {}, {}
-    acts_second = Deliver(hidden[2], 1)
+    acts_second = Deliver(hidden[2], 1, acts_first)
     for layer in (1, 0):
         middle, normed, proj, att, branch, normed2, pre, gelu, branch2 = saved[layer]
         if layer == 1:
@@ -1527,7 +1542,8 @@
             att_plan, 7 + 2 * (1 - layer),
         )
         for tensor in (1, 2):
-            settle[layer][tensor] = Settle(narrow[layer][tensor].results[0], layer)
+            into = None if layer else settle[1][tensor]
+            settle[layer][tensor] = Settle(narrow[layer][tensor].results[0], layer, into=into)
         narrow[layer][0] = Narrow(dw)
         gins[layer] = grad = gin
         d_bias[layer] = jnp.concatenate(
@@ -1536,9 +1552,9 @@
         d_mod[layer] = jnp.concatenate([dmod1.reshape(-1), dmod2.reshape(-1)])
 
     last = narrow[0][0]
-    final = Settle(jax.ShapeDtypeStruct((rows, units), BF16), 0, held=lambda: last.refs[1][0])
+    final = Settle(jax.ShapeDtypeStruct((rows, units), BF16), 0, held=lambda: last.refs[1][0], into=settle[1][0])
     settle[0][0] = final
-    gin_first = Deliver(gins[0], 0)
+    gin_first = Deliver(gins[0], 0, gin_second)
     dmod = jnp.stack([d_mod[0], d_mod[1]]).reshape(2 * n_mp, 1, cols)
     g_wada, g_bada, g_act, g_bias = epilogue(
         dmod,
@@ -1546,24 +1562,20 @@
         modulation_weight[0],
         jnp.stack([d_bias[0], d_bias[1]]),
         plan(
-            [(last, "a"), (settle[0][2], "az"), (settle[1][2], "az")],
-            [(settle[0][2], "b"), (settle[1][2], "b"), (settle[0][1], "az"), (settle[1][1], "az")]
-            + [(last, "b"), (gin_first, "az"), (gin_second, "az")],
-            [(settle[0][1], "b"), (settle[1][1], "b"), (settle[1][0], "az"), (last, "c"), (final, "az")]
-            + [(gin_first, "b"), (gin_second, "b")],
-            [(settle[1][0], "b"), (final, "b"), (settle[0][2], "c"), (settle[1][2], "c")],
-            [(settle[0][1], "c"), (settle[1][1], "c"), (gin_first, "c"), (gin_second, "c")]
+            [(gin_first, "az"), (gin_second, "az"), (last, "a"), (gin_first, "b"), (gin_second, "b")]
+            + [(settle[0][2], "az"), (settle[1][2], "az")],
+            [(settle[0][2], "b"), (settle[1][2], "b"), (settle[0][1], "a"), (settle[1][1], "a"), (last, "b")]
+            + [(settle[0][2], "s"), (settle[1][2], "s"), (settle[0][1], "bz"), (settle[1][1], "bz")],
+            [(last, "c"), (settle[1][0], "a"), (final, "a"), (settle[0][1], "s"), (settle[1][1], "s")]
+            + [(settle[1][0], "bz"), (final, "bz")],
+            [(settle[0][2], "c"), (settle[1][2], "c"), (settle[0][1], "c"), (settle[1][1], "c")],
+            [(gin_first, "c"), (gin_second, "c"), (settle[1][0], "s"), (final, "s")]
             + [(settle[1][0], "c"), (final, "c")],
         ),
         10,
     )
     g_act = g_act.transpose(1, 0, 2).reshape(2, width)
-    low_section = section == 0
-
-    def own_block(first, second):
-        return jnp.where(low_section, first.results[0], second.results[0])
-
-    g_att, g_one, g_two = [own_block(settle[0][t], settle[1][t]) for t in range(3)]
+    g_att, g_one, g_two = [settle[1][t].results[0] for t in range(3)]
     g_qkv = g_att[:, : 3 * part_width].reshape(rows, 3, part_width)
     g_proj = g_att[:, 3 * part_width :].T
 
@@ -1579,8 +1591,8 @@
     g_bada = dp_part(g_bada[0])
     _, silu_back = jax.vjp(jax.nn.silu, cond)
     g_cond = silu_back(g_act)[0][:, None]
-    acts_out = own_block(acts_first, acts_second)[None, :, None]
-    grad_input = own_block(gin_first, gin_second).astype(F32)[None, :, None]
+    acts_out = acts_first.results[0][None, :, None]
+    grad_input = gin_second.results[0].astype(F32)[None, :, None]
     return (
         acts_out,
         grad_input,

time: 570 us -> 564 us (0.989)
    unnamed x70 -> x63, local copies, waits for them, and re-layouts: 23 us -> 24.3 us
where the time goes in v4:
time: 564 us; the launch traced here: 556 us
  Pallas kernels  517 us (92%)
  local copies, waits for them, and re-layouts  35.5 us (6%)
    pallas_call x10, Pallas kernels, launch(): pl.pallas_call(body, out_shape=tuple((jax.ShapeDtypeStruct(shape, dtype)...  517 us
    unnamed x63, local copies, waits for them, and re-layouts  24.3 us

profile of v4, /device:TPU:4, one launch (start us, length us, event | category | flops | bytes accessed | tf_op | source)
XLA Modules:
  0.0 556.4 jit_solution(414735304546560960)
XLA Ops:
  0.7 0.8 slice_bitcast_fusion.9
  1.4 0.8 concatenate.34
  2.3 1.4 copy.38
  3.7 0.3 copy.40
  4.1 0.2 copy.39
  4.2 0.1 maximum_bitcast_fusion
  4.4 1.6 pad_maximum_fusion.refs_5_.refs_6_.refs_7_.refs_8_.refs_9_.refs_10_
  6.1 0.1 reshape.142
  6.2 1.1 copy-done.10
  7.3 107.9 %prologue.1 = (f32[8,1,1728]{2,1,0:T(1,128)S(1)}, bf16[8,288]{1,0:T(8,128)(2,1)S(1)}, f32[2,1,4032]{2,1,0:T(1,128)S(1)}, bf16[128,1152]{1,0:T(8,128)(2,1)S(1)}, ...) custom-call(f32[4,2,288]{2,1,0:T(2,128)S(1)} %bitcast.68, ...), custom_call_target="tpu_custom_call" | custom-call | tf_op jit(solution)/shard_map/prologue/pallas_call | solution.py:1003
  115.1 0.1 fusion.3
  115.2 0.1 pad.9.clone
  115.3 0.1 pad_maximum_fusion.5
  115.4 0.1 slice_bitcast_fusion.1
  115.5 0.2 slice_reduce_fusion
  115.7 0.1 squeeze.64.refs_1_.refs_2_
  115.8 30.4 %att_fwd.2 = (f32[128,1152]{1,0:T(8,128)S(1)}, bf16[4,128,1152]{2,1,0:T(8,128)(2,1)S(1)}, bf16[3,4,128,288]{3,2,1,0:T(8,128)(2,1)}, bf16[4,128,288]{2,1,0:T(8,12...) custom-call(bf16[128,1152]{1,0:T(8,128)(2,1)S(1)} %get-tuple-element.84.refs_0_., ...), custom_call_target="tpu_custom_call", output_to_operand_aliasing={{5}: (5, {})} | custom-call | tf_op jit(solution)/shard_map/att_fwd/pallas_call | solution.py:1003
  146.2 1.0 copy-done.1
  147.2 0.8 copy-done.12
  148.1 0.7 copy-done.18
  148.8 26.1 %mlp_fwd.2 = (bf16[128,1152]{1,0:T(8,128)(2,1)S(1)}, bf16[4,128,1152]{2,1,0:T(8,128)(2,1)S(1)}, f32[4,128,1152]{2,1,0:T(8,128)}, bf16[4,128,1152]{2,1,0:T(8,128)...) custom-call(f32[128,1152]{1,0:T(8,128)S(1)} %get-tuple-element.89.refs_0_.refs_1_,, ...), custom_call_target="tpu_custom_call", output_to_operand_aliasing={{5}: (6, {})} | custom-call | tf_op jit(solution)/shard_map/mlp_fwd/pallas_call | solution.py:1003
  174.9 1.0 copy-done.2
  175.9 0.8 copy-done.16
  176.7 0.1 squeeze.69.refs_1_.refs_2_
  176.8 35.1 %att_fwd.3 = (f32[128,1152]{1,0:T(8,128)S(1)}, bf16[4,128,1152]{2,1,0:T(8,128)(2,1)S(1)}, bf16[3,4,128,288]{3,2,1,0:T(8,128)(2,1)}, bf16[4,128,288]{2,1,0:T(8,12...) custom-call(bf16[128,1152]{1,0:T(8,128)(2,1)S(1)} %get-tuple-element, ...), custom_call_target="tpu_custom_call", output_to_operand_aliasing={{6}: (6, {}), {7}: (7, {})} | custom-call | tf_op jit(solution)/shard_map/att_fwd/pallas_call | solution.py:1003
  212.0 1.0 copy-done.3
  213.0 28.2 %mlp_fwd.3 = (bf16[128,1152]{1,0:T(8,128)(2,1)S(1)}, bf16[4,128,1152]{2,1,0:T(8,128)(2,1)S(1)}, f32[4,128,1152]{2,1,0:T(8,128)}, bf16[4,128,1152]{2,1,0:T(8,128)(2,1)S(1)}, f32[128,1152]{1,0:T(8,128)S(1)}) custom-call(f32[128,1152]{1,0:T(8,128)S(1)} %get-tuple-element.98.refs_0_.refs_1_, f32[6,1152]{1,0:T(8,128)S(1)} %squeeze.69.refs_1_.refs_2_, ...), custom_call_target="tpu_custom_call" | custom-call | tf_op jit(solution)/shard_map/mlp_fwd/pallas_call | solution.py:1003
  241.2 1.0 copy-done.4
  242.2 1.0 copy-done.5
  243.2 42.8 %mlp_bwd.2 = (f32[128,1152]{1,0:T(8,128)S(1)}, bf16[1152,1152]{1,0:T(8,128)(2,1)}, bf16[1152,1152]{1,0:T(8,128)(2,1)}, f32[1,1152]{1,0:T(1,128)S(1)}, f32[1,1152...) custom-call(bf16[128,1152]{1,0:T(8,128)(2,1)S(1)} %get-tuple-element.97.refs_0_, ...), custom_call_target="tpu_custom_call" | custom-call | tf_op jit(solution)/shard_map/mlp_bwd/pallas_call | solution.py:1003
  286.0 38.3 %att_bwd.2 = (bf16[128,1152]{1,0:T(8,128)(2,1)S(1)}, bf16[1152,1152]{1,0:T(8,128)(2,1)}, f32[1,864]{1,0:T(1,128)S(1)}, f32[1,1152]{1,0:T(1,128)S(1)}, f32[3,1152...) custom-call(f32[128,1152]{1,0:T(8,128)S(1)} %get-tuple-element.107.refs_0_, ...), custom_call_target="tpu_custom_call" | custom-call | tf_op jit(solution)/shard_map/att_bwd/pallas_call | solution.py:1003
  324.4 0.8 copy-done.6
  325.2 0.8 copy-done.8
  326.0 40.8 %mlp_bwd.3 = (f32[128,1152]{1,0:T(8,128)S(1)}, bf16[1152,1152]{1,0:T(8,128)(2,1)}, bf16[1152,1152]{1,0:T(8,128)(2,1)}, f32[1,1152]{1,0:T(1,128)S(1)}, f32[1,1152...) custom-call(bf16[128,1152]{1,0:T(8,128)(2,1)S(1)} %get-tuple-element.114.refs_0_.refs_5_, ...), custom_call_target="tpu_custom_call" | custom-call | tf_op jit(solution)/shard_map/mlp_bwd/pallas_call | solution.py:1003
  366.8 0.8 copy-done.9
  367.7 39.2 %att_bwd.3 = (bf16[128,1152]{1,0:T(8,128)(2,1)S(1)}, bf16[1152,1152]{1,0:T(8,128)(2,1)}, f32[1,864]{1,0:T(1,128)S(1)}, f32[1,1152]{1,0:T(1,128)S(1)}, f32[3,1152...) custom-call(f32[128,1152]{1,0:T(8,128)S(1)} %get-tuple-element.120.refs_0_, ...), custom_call_target="tpu_custom_call" | custom-call | tf_op jit(solution)/shard_map/att_bwd/pallas_call | solution.py:1003
  406.8 0.7 copy-done.20
  407.5 0.1 fusion.5
  407.6 0.1 concatenate.39
  407.8 0.1 fusion.6
  407.8 0.1 concatenate.40
  408.2 0.1 pad_maximum_fusion.1
  408.2 0.1 reshape.138.refs_0_
  408.4 1.0 copy-done.21
  409.4 127.8 %epilogue.1 = (f32[288,1728]{1,0:T(8,128)}, f32[1,1728]{1,0:T(1,128)S(1)}, f32[4,2,288]{2,1,0:T(2,128)S(1)}, f32[1,4032]{1,0:T(1,128)S(1)}, bf16[2,128,1152]{2,1...) custom-call(f32[8,1,1728]{2,1,0:T(1,128)S(1)} %reshape.138.refs_0_, ...), custom_call_target="tpu_custom_call" | custom-call | tf_op jit(solution)/shard_map/epilogue/pallas_call | solution.py:1003
  537.2 0.1 fusion.4
  537.3 0.6 constant_dynamic-slice_fusion
  537.9 2.2 slice.111
  540.2 1.6 copy.42
  541.8 1.6 copy.46
  543.4 1.1 bitcast_convert_fusion
  544.5 1.2 slice_bitcast_fusion
  545.7 1.0 copy.47
  546.7 0.1 reshape.139
  546.8 0.6 copy.45
  547.4 0.6 constant_dynamic-slice_fusion.2
  548.0 0.1 reshape.140
  548.1 0.6 fusion.2
  548.8 0.7 constant_dynamic-slice_fusion.4
  549.4 0.8 copy.58
  550.2 3.1 copy.59
  553.4 1.1 copy.60
  554.4 0.7 copy-done.22
  555.2 1.1 copy.61
  (56 shorter events, 0.3 us)
Async XLA Ops:
  0.6 3.4 copy-start.24
  4.4 1.7 copy-start.25
  4.4 1.8 copy-start.26
  4.4 1.8 copy-start
  6.2 1.1 copy-start.10
  146.2 1.0 copy-start.1
  147.2 0.8 copy-start.12
  148.1 0.7 copy-start.18
  148.8 28.0 %copy-start.11 = (bf16[2,1,128,1152]{3,2,1,0:T(8,128)(2,1)S(1)}, bf16[2,1,128,1152]{3,2,1,0:T(8,128)(2,1)}, u32[]{:S(2)}) copy-start(bf16[2,1,128,1152]{3,2,1,0:T(8,128)(2,1)} %param.15) | copy-start | bytes 1769476
  174.9 1.0 copy-start.2
  175.9 0.8 copy-start.16
  212.0 1.0 copy-start.3
  241.2 1.0 copy-start.4
  242.2 1.0 copy-start.5
  286.0 38.4 %copy-start.14 = (bf16[2,128,1152]{2,1,0:T(8,128)(2,1)}, bf16[2,128,1152]{2,1,0:T(8,128)(2,1)S(1)}, u32[]{:S(2)}) copy-start(bf16[2,128,1152]{2,1,0:T(8,128)(2,1)S(1)} %get-tuple-element.106) | copy-start | bytes 1769476
  286.0 40.1 %copy-start.17 = (f32[128,1152]{1,0:T(8,128)S(1)}, f32[128,1152]{1,0:T(8,128)}, u32[]{:S(2)}) copy-start(f32[128,1152]{1,0:T(8,128)} %copy-done.16) | copy-start | bytes 1769476
  324.3 0.8 copy-start.6
  325.2 0.8 copy-start.8
  326.0 41.6 %copy-start.13 = (f32[128,1152]{1,0:T(8,128)S(1)}, f32[128,1152]{1,0:T(8,128)}, u32[]{:S(2)}) copy-start(f32[128,1152]{1,0:T(8,128)} %copy-done.12) | copy-start | bytes 1769476
  326.0 41.6 %copy-start.19 = (bf16[4,128,288]{2,1,0:T(8,128)(2,1)S(1)}, bf16[4,128,288]{2,1,0:T(8,128)(2,1)}, u32[]{:S(2)}) copy-start(bf16[4,128,288]{2,1,0:T(8,128)(2,1)} %copy-done.18) | copy-start | bytes 884740
  366.8 0.8 copy-start.9
  367.7 40.7 %copy-start.7 = (bf16[288,1152]{1,0:T(8,128)(2,1)S(1)}, bf16[288,1152]{1,0:T(8,128)(2,1)}, u32[]{:S(2)}) copy-start(bf16[288,1152]{1,0:T(8,128)(2,1)} %copy-done.6) | copy-start | bytes 1990660
  406.8 0.7 copy-start.20
  408.4 1.0 copy-start.21
  543.4 6.0 %copy-start.15 = (bf16[2,128,1152]{2,1,0:T(8,128)(2,1)S(1)}, bf16[2,128,1152]{2,1,0:T(8,128)(2,1)}, u32[]{:S(2)}) copy-start(bf16[2,128,1152]{2,1,0:T(8,128)(2,1)} %copy-done.14) | copy-start | bytes 1769476
  550.2 3.1 copy-start.23
  553.4 1.8 copy-start.22

commit v5 on v4

--- a/solution.py
+++ b/solution.py
@@ -421,8 +421,8 @@
     gelu_all = gelu_ref[...].reshape(seq, -1)
     db1_ref[...] = col_sum(dpre_all.astype(F32))
     db2_ref[...] = col_sum(dbr[...].reshape(seq, -1).astype(F32))
-    weight_grad(normed_ref.reshape(seq, width), dpre_all, dw1_ref, 128)
-    weight_grad(dbr.reshape(seq, width), gelu_all, dw2_ref, 128)
+    weight_grad(normed_ref.reshape(seq, width), dpre_all, dw1_ref, 384)
+    weight_grad(dbr.reshape(seq, width), gelu_all, dw2_ref, 384)
     group.spread_sent(dbr, ag_send, ag_recv)
     bg(3)
     total = group.landed_sum(stage[me].astype(F32), stage, landing, rs_send, rs_recv)
@@ -511,12 +511,12 @@
     normed_rows, dba_rows = normed_ref.reshape(seq, width), dba.reshape(seq, width)
 
     def weights(index, carry):
-        cols = pl.ds(pl.multiple_of(index * 128, 128), 128)
+        cols = pl.ds(pl.multiple_of(index * 384, 128), 384)
         dw_ref[cols, : 3 * part_width] = dot_tn(normed_rows[:, cols], grads).astype(BF16)
         dw_ref[cols, 3 * part_width :] = dot_tn(dba_rows[:, cols], mixed).astype(BF16)
         return carry
 
-    lax.fori_loop(0, width // 128, weights, 0)
+    lax.fori_loop(0, width // 384, weights, 0)
     group.spread_sent(dba, ag_send, ag_recv)
     bg(3)
     total = group.landed_sum(stage[me].astype(F32), stage, landing, rs_send, rs_recv)
@@ -648,17 +648,17 @@
 
 
 class Collect(Task):
-    def __init__(self, item, tensor, layer, handle):
-        self.tensor, self.layer, self.handle = tensor, layer, handle
+    def __init__(self, item, layer, handle):
+        self.layer, self.handle = layer, handle
         self.inputs = ((item, VM),)
         self.handles = (handle,)
-        self.chunk = item.shape[1]
+        self.chunk = item.shape[0]
         self.scratch = (DMA((2,)), DMA, DMA)
 
     def run(self, phase, refs):
         (item,), _, (send, recv, own) = refs
         place = Place()
-        source = item.at[self.tensor]
+        source = item
         rows = self.handle.ref.at[pl.ds(pl.multiple_of(place.dp * self.chunk, 16), self.chunk)]
 
         def to(number, role):
@@ -1256,8 +1256,8 @@
 
 def epilogue_kernel(
     bg,
-    dmod_ref, act_ref, wada_ref, dbias_ref,
-    gada_ref, gbada_ref, gact_ref, gbias_ref,
+    dmod_ref, wada_ref, dbias_ref,
+    dmod_out, gbada_ref, gact_ref, gbias_ref,
     mod_land, act_stage, act_land, bias_land, bias_stage, bias_final,
     mod_send, mod_recv, act_send, act_recv, d_send, d_recv, b_send, b_recv,
 ):
@@ -1324,7 +1324,7 @@
 
     bg(1)
     gbada_ref[...] = col_sum(dmod.astype(F32))
-    gada_ref[...] = dot_tn(act_ref[...], dmod)
+    dmod_out[...] = dmod
     bg(2)
     finish_act()
     for index in range(place.n_dp):
@@ -1356,16 +1356,16 @@
     bg(4)
 
 
-def epilogue(dmod, act, wada, dbias, schedule, cid):
+def epilogue(dmod, wada, dbias, schedule, cid):
     n_dp, n_mp = lax.axis_size("dp"), 2 * lax.axis_size("ml")
     total = 2 * n_dp * n_mp
     chunk, share = wada.shape
     row = dbias.shape[1:]
     return launch(
         epilogue_kernel,
-        [(dmod, VM), (act, VM), (wada, VM), (dbias, VM)],
+        [(dmod, VM), (wada, VM), (dbias, VM)],
         [
-            ((chunk, share), F32, VM),
+            ((2 * n_dp, share), BF16, VM),
             ((1, share), F32, VM),
             ((n_dp, 2, chunk), F32, VM),
             (row, F32, VM),
@@ -1407,14 +1407,12 @@
     part_width = query_key_value_weight.shape[3]
     units = first_dense_weight.shape[2]
 
-    item = jnp.stack(
-        [
-            jnp.concatenate(
-                [query_key_value_weight[0].reshape(rows, -1), output_proj_weight[0].T], axis=1
-            ),
-            first_dense_weight[0],
-            second_dense_weight[0].T,
-        ]
+    item = (
+        jnp.concatenate(
+            [query_key_value_weight[0].reshape(rows, -1), output_proj_weight[0].T], axis=1
+        ),
+        first_dense_weight[0],
+        second_dense_weight[0].T,
     )
     cond = condition[:, 0].astype(F32)
     packed = jnp.concatenate(
@@ -1424,7 +1422,7 @@
         ]
     ).astype(F32)[None]
     w = [[Handle((width, units), BF16) for _ in range(3)] for _ in range(2)]
-    collect = [[Collect(item, t, l, w[l][t]) for t in range(3)] for l in range(2)]
+    collect = [[Collect(item[t], l, w[l][t]) for t in range(3)] for l in range(2)]
     widen = [[Widen(w[l][t]) for t in range(3)] for l in range(2)]
     tokens_in = Tokens(latents_in[:, 0])
     tokens_cot = Tokens(cotangent[:, 0])
@@ -1516,9 +1514,9 @@
         middle, normed, proj, att, branch, normed2, pre, gelu, branch2 = saved[layer]
         if layer == 1:
             mlp_plan = plan(
-                [(acts_first, "az"), (acts_second, "az")],
+                [(acts_first, "a"), (acts_second, "a")],
                 [],
-                [(acts_first, "b"), (acts_second, "b")],
+                [(acts_first, "zb"), (acts_second, "zb")],
                 [],
                 [(acts_first, "c"), (acts_second, "c")],
             )
@@ -1556,9 +1554,8 @@
     settle[0][0] = final
     gin_first = Deliver(gins[0], 0, gin_second)
     dmod = jnp.stack([d_mod[0], d_mod[1]]).reshape(2 * n_mp, 1, cols)
-    g_wada, g_bada, g_act, g_bias = epilogue(
+    dmod_all, g_bada, g_act, g_bias = epilogue(
         dmod,
-        act_rows,
         modulation_weight[0],
         jnp.stack([d_bias[0], d_bias[1]]),
         plan(
@@ -1574,6 +1571,7 @@
         ),
         10,
     )
+    g_wada = dot_tn(act_rows, dmod_all)
     g_act = g_act.transpose(1, 0, 2).reshape(2, width)
     g_att, g_one, g_two = [settle[1][t].results[0] for t in range(3)]
     g_qkv = g_att[:, : 3 * part_width].reshape(rows, 3, part_width)

time: 564 us -> 554 us (0.982)
  Pallas kernels: 517 us -> 506 us
    pallas_call x10, Pallas kernels: 517 us -> 506 us  [launch(): pl.pallas_call(body, out_shape=tuple((jax.ShapeDtypeStruct(shape, dtype)...]
    unnamed x63 -> x68, local copies, waits for them, and re-layouts: 24.3 us -> 21.2 us
where the time goes in v5:
time: 554 us; the launch traced here: 545 us
  Pallas kernels  506 us (91%)
  local copies, waits for them, and re-layouts  33.3 us (6%)
    pallas_call x10, Pallas kernels, launch(): pl.pallas_call(body, out_shape=tuple((jax.ShapeDtypeStruct(shape, dtype)...  506 us
    unnamed x68, local copies, waits for them, and re-layouts  21.2 us

profile of v5, /device:TPU:4, one launch (start us, length us, event | category | flops | bytes accessed | tf_op | source)
XLA Modules:
  0.0 544.9 jit_solution(10395170163605273359)
XLA Ops:
  0.7 0.8 slice_bitcast_fusion.9
  1.4 0.8 concatenate.34
  2.3 1.4 copy.38
  3.7 0.0 copy-start.27
  3.8 1.1 copy.40
  4.9 0.2 copy.39
  5.0 1.2 pad_maximum_fusion.refs_5_.refs_6_
  6.2 0.1 reshape.142
  6.4 1.1 copy-done.17
  7.4 107.9 %prologue.1 = (f32[8,1,1728]{2,1,0:T(1,128)S(1)}, bf16[8,288]{1,0:T(8,128)(2,1)S(1)}, f32[2,1,4032]{2,1,0:T(1,128)S(1)}, bf16[128,1152]{1,0:T(8,128)(2,1)S(1)}, ...) custom-call(f32[4,2,288]{2,1,0:T(2,128)S(1)} %bitcast.72, ...), custom_call_target="tpu_custom_call" | custom-call | tf_op jit(solution)/shard_map/prologue/pallas_call | solution.py:1003
  115.3 0.1 fusion.3
  115.4 0.1 pad.9.clone
  115.5 0.1 pad_maximum_fusion.5
  115.6 0.1 slice_bitcast_fusion.1
  115.7 0.2 slice_reduce_fusion
  115.9 0.1 squeeze.68.refs_1_.refs_2_
  116.0 30.4 %att_fwd.2 = (f32[128,1152]{1,0:T(8,128)S(1)}, bf16[4,128,1152]{2,1,0:T(8,128)(2,1)S(1)}, bf16[3,4,128,288]{3,2,1,0:T(8,128)(2,1)}, bf16[4,128,288]{2,1,0:T(8,12...) custom-call(bf16[128,1152]{1,0:T(8,128)(2,1)S(1)} %get-tuple-element.84.refs_0_., ...), custom_call_target="tpu_custom_call", output_to_operand_aliasing={{5}: (5, {})} | custom-call | tf_op jit(solution)/shard_map/att_fwd/pallas_call | solution.py:1003
  146.4 1.0 copy-done.3
  147.4 0.8 copy-done.13
  148.2 0.7 copy-done.20
  149.0 26.1 %mlp_fwd.2 = (bf16[128,1152]{1,0:T(8,128)(2,1)S(1)}, bf16[4,128,1152]{2,1,0:T(8,128)(2,1)S(1)}, f32[4,128,1152]{2,1,0:T(8,128)}, bf16[4,128,1152]{2,1,0:T(8,128)...) custom-call(f32[128,1152]{1,0:T(8,128)S(1)} %get-tuple-element.89.refs_0_.refs_1_,, ...), custom_call_target="tpu_custom_call", output_to_operand_aliasing={{5}: (6, {})} | custom-call | tf_op jit(solution)/shard_map/mlp_fwd/pallas_call | solution.py:1003
  175.1 1.0 copy-done.4
  176.1 0.9 copy-done.18
  176.9 0.1 squeeze.73.refs_1_.refs_2_
  177.0 35.1 %att_fwd.3 = (f32[128,1152]{1,0:T(8,128)S(1)}, bf16[4,128,1152]{2,1,0:T(8,128)(2,1)S(1)}, bf16[3,4,128,288]{3,2,1,0:T(8,128)(2,1)}, bf16[4,128,288]{2,1,0:T(8,12...) custom-call(bf16[128,1152]{1,0:T(8,128)(2,1)S(1)} %get-tuple-element, ...), custom_call_target="tpu_custom_call", output_to_operand_aliasing={{6}: (6, {}), {7}: (7, {})} | custom-call | tf_op jit(solution)/shard_map/att_fwd/pallas_call | solution.py:1003
  212.1 1.0 copy-done.5
  213.1 28.1 %mlp_fwd.3 = (bf16[128,1152]{1,0:T(8,128)(2,1)S(1)}, bf16[4,128,1152]{2,1,0:T(8,128)(2,1)S(1)}, f32[4,128,1152]{2,1,0:T(8,128)}, bf16[4,128,1152]{2,1,0:T(8,128)(2,1)S(1)}, f32[128,1152]{1,0:T(8,128)S(1)}) custom-call(f32[128,1152]{1,0:T(8,128)S(1)} %get-tuple-element.98.refs_0_.refs_1_, f32[6,1152]{1,0:T(8,128)S(1)} %squeeze.73.refs_1_.refs_2_, ...), custom_call_target="tpu_custom_call" | custom-call | tf_op jit(solution)/shard_map/mlp_fwd/pallas_call | solution.py:1003
  241.3 1.0 copy-done.6
  242.3 1.0 copy-done.7
  243.3 40.4 %mlp_bwd.2 = (f32[128,1152]{1,0:T(8,128)S(1)}, bf16[1152,1152]{1,0:T(8,128)(2,1)}, bf16[1152,1152]{1,0:T(8,128)(2,1)}, f32[1,1152]{1,0:T(1,128)S(1)}, f32[1,1152...) custom-call(bf16[128,1152]{1,0:T(8,128)(2,1)S(1)} %get-tuple-element.97.refs_0_, ...), custom_call_target="tpu_custom_call" | custom-call | tf_op jit(solution)/shard_map/mlp_bwd/pallas_call | solution.py:1003
  283.7 40.6 %att_bwd.2 = (bf16[128,1152]{1,0:T(8,128)(2,1)S(1)}, bf16[1152,1152]{1,0:T(8,128)(2,1)}, f32[1,864]{1,0:T(1,128)S(1)}, f32[1,1152]{1,0:T(1,128)S(1)}, f32[3,1152...) custom-call(f32[128,1152]{1,0:T(8,128)S(1)} %get-tuple-element.107.refs_0_, ...), custom_call_target="tpu_custom_call" | custom-call | tf_op jit(solution)/shard_map/att_bwd/pallas_call | solution.py:1003
  324.3 0.8 copy-done.8
  325.1 0.8 copy-done.10
  326.0 32.0 %mlp_bwd.3 = (f32[128,1152]{1,0:T(8,128)S(1)}, bf16[1152,1152]{1,0:T(8,128)(2,1)}, bf16[1152,1152]{1,0:T(8,128)(2,1)}, f32[1,1152]{1,0:T(1,128)S(1)}, f32[1,1152...) custom-call(bf16[128,1152]{1,0:T(8,128)(2,1)S(1)} %get-tuple-element.114.refs_0_.refs_4_, ...), custom_call_target="tpu_custom_call" | custom-call | tf_op jit(solution)/shard_map/mlp_bwd/pallas_call | solution.py:1003
  358.0 0.8 copy-done.11
  358.8 39.7 %att_bwd.3 = (bf16[128,1152]{1,0:T(8,128)(2,1)S(1)}, bf16[1152,1152]{1,0:T(8,128)(2,1)}, f32[1,864]{1,0:T(1,128)S(1)}, f32[1,1152]{1,0:T(1,128)S(1)}, f32[3,1152...) custom-call(f32[128,1152]{1,0:T(8,128)S(1)} %get-tuple-element.120.refs_0_, ...), custom_call_target="tpu_custom_call" | custom-call | tf_op jit(solution)/shard_map/att_bwd/pallas_call | solution.py:1003
  398.6 0.7 copy-done.22
  399.3 0.1 fusion.5
  399.4 0.1 concatenate.39
  399.5 0.1 fusion.6
  399.6 0.1 concatenate.40
  399.9 0.1 pad_maximum_fusion.1
  400.0 0.1 reshape.138.refs_0_
  400.1 1.0 copy-done.23
  401.1 125.7 %epilogue.1 = (bf16[8,1728]{1,0:T(8,128)(2,1)S(1)}, f32[1,1728]{1,0:T(1,128)S(1)}, f32[4,2,288]{2,1,0:T(2,128)S(1)}, f32[1,4032]{1,0:T(1,128)S(1)}, bf16[2,128,1...) custom-call(f32[8,1,1728]{2,1,0:T(1,128)S(1)} %reshape.138.refs_0_, ...), custom_call_target="tpu_custom_call" | custom-call | tf_op jit(solution)/shard_map/epilogue/pallas_call | solution.py:1003
  526.8 0.1 fusion.4
  526.9 0.6 constant_dynamic-slice_fusion
  527.6 2.2 slice.111
  529.8 1.6 copy.42
  531.5 1.6 copy.46
  533.0 1.8 convolution_bitcast_fusion
  534.8 1.1 bitcast_convert_fusion
  535.9 1.3 slice_bitcast_fusion
  537.3 1.0 copy.47
  538.2 0.1 reshape.139
  538.4 0.6 copy.45
  539.0 0.6 constant_dynamic-slice_fusion.2
  539.6 0.1 reshape.140
  539.7 0.6 fusion.2
  540.3 0.7 constant_dynamic-slice_fusion.4
  541.0 0.8 copy.57
  541.8 1.1 copy.58
  542.9 0.7 copy-done.24
  543.6 1.1 copy.59
  (61 shorter events, 0.3 us)
Async XLA Ops:
  0.6 4.2 copy-start.26
  3.7 2.5 copy-start.27
  3.7 2.6 copy-start.29
  3.8 2.6 copy-start
  3.8 2.6 copy-start.1
  3.8 2.6 copy-start.2
  6.4 1.1 copy-start.17
  146.4 1.0 copy-start.3
  147.4 0.8 copy-start.13
  148.2 0.7 copy-start.20
  149.0 28.0 %copy-start.12 = (bf16[2,1,128,1152]{3,2,1,0:T(8,128)(2,1)S(1)}, bf16[2,1,128,1152]{3,2,1,0:T(8,128)(2,1)}, u32[]{:S(2)}) copy-start(bf16[2,1,128,1152]{3,2,1,0:T(8,128)(2,1)} %param.15) | copy-start | bytes 1769476
  175.1 1.0 copy-start.4
  176.1 0.9 copy-start.18
  212.1 1.0 copy-start.5
  241.3 1.0 copy-start.6
  242.3 1.0 copy-start.7
  283.7 40.6 %copy-start.15 = (bf16[2,128,1152]{2,1,0:T(8,128)(2,1)}, bf16[2,128,1152]{2,1,0:T(8,128)(2,1)S(1)}, u32[]{:S(2)}) copy-start(bf16[2,128,1152]{2,1,0:T(8,128)(2,1)S(1)} %get-tuple-element.106) | copy-start | bytes 1769476
  283.7 42.3 %copy-start.19 = (f32[128,1152]{1,0:T(8,128)S(1)}, f32[128,1152]{1,0:T(8,128)}, u32[]{:S(2)}) copy-start(f32[128,1152]{1,0:T(8,128)} %copy-done.18) | copy-start | bytes 1769476
  324.3 0.8 copy-start.8
  325.1 0.8 copy-start.10
  326.0 32.9 %copy-start.14 = (f32[128,1152]{1,0:T(8,128)S(1)}, f32[128,1152]{1,0:T(8,128)}, u32[]{:S(2)}) copy-start(f32[128,1152]{1,0:T(8,128)} %copy-done.13) | copy-start | bytes 1769476
  326.0 32.9 %copy-start.21 = (bf16[4,128,288]{2,1,0:T(8,128)(2,1)S(1)}, bf16[4,128,288]{2,1,0:T(8,128)(2,1)}, u32[]{:S(2)}) copy-start(bf16[4,128,288]{2,1,0:T(8,128)(2,1)} %copy-done.20) | copy-start | bytes 884740
  358.0 0.8 copy-start.11
  358.8 41.3 %copy-start.9 = (bf16[288,1152]{1,0:T(8,128)(2,1)S(1)}, bf16[288,1152]{1,0:T(8,128)(2,1)}, u32[]{:S(2)}) copy-start(bf16[288,1152]{1,0:T(8,128)(2,1)} %copy-done.8) | copy-start | bytes 1990660
  398.6 0.7 copy-start.22
  400.1 1.0 copy-start.23
  534.8 3.5 copy-start.28
  535.9 5.1 copy-start.16
  535.9 5.9 %copy-start.25 = (f32[288,1152]{1,0:T(8,128)S(1)}, f32[288,1152]{1,0:T(8,128)}, u32[]{:S(2)}) copy-start(f32[288,1152]{1,0:T(8,128)} %get-tuple-element.153) | copy-start | bytes 3981316
  541.8 1.8 copy-start.24

commit v6 on v5

--- a/solution.py
+++ b/solution.py
@@ -46,6 +46,10 @@
 
 def col_sum(values):
     return jnp.sum(values, axis=0, keepdims=True)
+
+
+def row_total(low):
+    return dot_nn(jnp.ones((16, low.shape[0]), BF16), low)[0:1]
 
 
 class Group:
@@ -221,6 +225,15 @@
     return [copy]
 
 
+def flush(pairs, sems):
+    copies = [
+        pltpu.make_async_copy(src, dst, sems.at[number]) for number, (src, dst) in enumerate(pairs)
+    ]
+    for copy in copies:
+        copy.start()
+    return copies
+
+
 def lane_mask(shape, head):
     lanes = lax.broadcasted_iota(jnp.int32, shape, len(shape) - 1)
     return (lanes >= head * HEAD_SIZE) & (lanes < (head + 1) * HEAD_SIZE)
@@ -248,7 +261,8 @@
 def att_fwd_kernel(
     bg,
     hidden_ref, mod_ref, bias_ref, bproj_ref, w_ref,
-    middle_ref, normed_ref, proj_ref, att_ref, branch_ref,
+    middle_ref, normed_out, proj_out, att_out, branch_ref,
+    normed_ref, proj_ref, att_ref, out_sem,
     w_buf, wo_buf, stage, landing, w_sem, ag_send, ag_recv, rs_send, rs_recv,
 ):
     tokens, width = hidden_ref.shape
@@ -308,18 +322,24 @@
 
     lax.fori_loop(1, size + 1, send, 0)
     group.spread_sent(normed_ref, ag_send, ag_recv)
+    flushed = flush(
+        [(normed_ref, normed_out), (proj_ref, proj_out), (att_ref, att_out)], out_sem
+    )
     bg(3)
     own = stage[me].astype(F32)
     branch = group.landed_sum(own, stage, landing, rs_send, rs_recv) + bproj_ref[...]
     branch_ref[...] = branch
     middle_ref[...] = hidden_ref[...].astype(F32) + mod_ref[2:3] * branch
     bg(4)
+    for copy in flushed:
+        copy.wait()
 
 
 def mlp_fwd_kernel(
     bg,
     middle_ref, mod_ref, b1_ref, b2_ref, w1_ref, w2_ref,
-    out_ref, normed_ref, pre_ref, gelu_ref, branch_ref,
+    out_ref, normed_out, pre_out, gelu_out, branch_ref,
+    normed_ref, pre_ref, gelu_ref, out_sem,
     w1_buf, w2_buf, stage, landing, w_sem, ag_send, ag_recv, rs_send, rs_recv,
 ):
     group = Group(middle_ref.shape[0])
@@ -356,12 +376,17 @@
     group.combine(stage, landing, rs_send, rs_recv)
     bg(2)
     group.spread_sent(normed_ref, ag_send, ag_recv)
+    flushed = flush(
+        [(normed_ref, normed_out), (pre_ref, pre_out), (gelu_ref, gelu_out)], out_sem
+    )
     bg(3)
     own = stage[me].astype(F32)
     branch = group.landed_sum(own, stage, landing, rs_send, rs_recv) + b2_ref[...]
     branch_ref[...] = branch
     out_ref[...] = (middle_ref[...] + mod_ref[5:6] * branch).astype(BF16)
     bg(4)
+    for copy in flushed:
+        copy.wait()
 
 
 def weight_grad(lhs_ref, rhs, out_ref, tile):
@@ -375,14 +400,17 @@
 
 def mlp_bwd_kernel(
     bg,
-    grad_ref, middle_ref, mod_ref, branch_ref, normed_ref, pre_ref, gelu_ref, w1_ref, w2_ref,
-    gmid_ref, dw1_ref, dw2_ref, db1_ref, db2_ref, dmod_ref,
+    grad_ref, middle_ref, mod_ref, branch_ref, normed_in, pre_in, gelu_in, w1_ref, w2_ref,
+    gmid_ref, dw1_out, dw2_out, db1_ref, db2_ref, dmod_ref,
+    dw1_ref, dw2_ref, out_sem, normed_ref, pre_ref, gelu_ref, in_sem,
     w1_buf, w2_buf, dbr, dpre, stage, landing, w_sem, ag_send, ag_recv, rs_send, rs_recv,
 ):
     tokens, width = grad_ref.shape
     group = Group(tokens)
     me, size = group.me, group.size
-    loads = load(w1_ref, w1_buf, w_sem.at[0]) + load(w2_ref, w2_buf, w_sem.at[1])
+    loads = load(w2_ref, w2_buf, w_sem.at[1]) + load(pre_in, pre_ref, in_sem.at[0])
+    loads += load(w1_ref, w1_buf, w_sem.at[0]) + load(gelu_in, gelu_ref, in_sem.at[1])
+    loads += load(normed_in, normed_ref, in_sem.at[2])
     grad = grad_ref[...].astype(F32)
     dbr[me] = (grad * mod_ref[5:6]).astype(BF16)
     Place().greet()
@@ -419,10 +447,11 @@
     seq = size * tokens
     dpre_all = dpre[...].reshape(seq, -1)
     gelu_all = gelu_ref[...].reshape(seq, -1)
-    db1_ref[...] = col_sum(dpre_all.astype(F32))
-    db2_ref[...] = col_sum(dbr[...].reshape(seq, -1).astype(F32))
+    db1_ref[...] = row_total(dpre_all)
+    db2_ref[...] = row_total(dbr[...].reshape(seq, -1))
     weight_grad(normed_ref.reshape(seq, width), dpre_all, dw1_ref, 384)
     weight_grad(dbr.reshape(seq, width), gelu_all, dw2_ref, 384)
+    flushed = flush([(dw1_ref, dw1_out), (dw2_ref, dw2_out)], out_sem)
     group.spread_sent(dbr, ag_send, ag_recv)
     bg(3)
     total = group.landed_sum(stage[me].astype(F32), stage, landing, rs_send, rs_recv)
@@ -431,34 +460,38 @@
     dmod_ref[1:2] = col_sum(total * normed)
     gmid_ref[...] = norm_back(total, normed, rstd, mod_ref[4:5]) + grad_ref[...].astype(F32)
     bg(4)
+    for copy in flushed:
+        copy.wait()
 
 
 def att_bwd_kernel(
     bg,
-    gmid_ref, hidden_ref, mod_ref, branch_ref, normed_ref, proj_ref, att_ref, w_ref,
-    gin_ref, dw_ref, dbqkv_ref, dbproj_ref, dmod_ref,
+    gmid_ref, hidden_ref, mod_ref, branch_ref, normed_in, proj_in, att_in, w_ref,
+    gin_ref, dw_out, dbqkv_ref, dbproj_ref, dmod_ref,
+    dw_ref, out_sem, normed_ref, proj_ref, att_ref, in_sem,
     w_buf, wo_buf, dba, dproj, dkey, dval, stage, landing, w_sem, ag_send, ag_recv, rs_send, rs_recv,
 ):
     tokens, width = gmid_ref.shape
     group = Group(tokens)
     me, size = group.me, group.size
     seq = size * tokens
-    part_width = att_ref.shape[-1]
+    part_width = att_in.shape[-1]
     heads = part_width // HEAD_SIZE
-    loads = load(w_ref, w_buf, w_sem.at[0])
+    loads = load(proj_in, proj_ref, in_sem.at[0]) + load(w_ref, w_buf, w_sem.at[0])
+    loads += load(att_in, att_ref, in_sem.at[1]) + load(normed_in, normed_ref, in_sem.at[2])
     gmid = gmid_ref[...]
     dba[me] = (gmid * mod_ref[2:3]).astype(BF16)
     Place().greet()
     group.spread(dba, ag_send, ag_recv)
     bg(0)
     dmod_ref[2:3] = col_sum(gmid * branch_ref[...])
+    for copy in loads:
+        copy.wait()
     keys = proj_ref[1].reshape(seq, part_width)
     values = proj_ref[2].reshape(seq, part_width)
     keys_t = dot_nt(identity(part_width), keys).astype(BF16)
     dkey[...] = jnp.zeros_like(dkey)
     dval[...] = jnp.zeros_like(dval)
-    for copy in loads:
-        copy.wait()
     wo_buf[...] = w_buf[:, 3 * part_width :]
 
     def back(step, carry):
@@ -505,18 +538,19 @@
     group.combine(stage, landing, rs_send, rs_recv)
     bg(2)
     grads = dproj[...].reshape(seq, -1)
-    dbqkv_ref[...] = col_sum(grads.astype(F32))
-    dbproj_ref[...] = col_sum(dba[...].reshape(seq, width).astype(F32))
+    dbqkv_ref[...] = row_total(grads)
+    dbproj_ref[...] = row_total(dba[...].reshape(seq, width))
     mixed = att_ref[...].reshape(seq, part_width)
     normed_rows, dba_rows = normed_ref.reshape(seq, width), dba.reshape(seq, width)
 
     def weights(index, carry):
-        cols = pl.ds(pl.multiple_of(index * 384, 128), 384)
+        cols = pl.ds(pl.multiple_of(index * 128, 128), 128)
         dw_ref[cols, : 3 * part_width] = dot_tn(normed_rows[:, cols], grads).astype(BF16)
         dw_ref[cols, 3 * part_width :] = dot_tn(dba_rows[:, cols], mixed).astype(BF16)
         return carry
 
-    lax.fori_loop(0, width // 384, weights, 0)
+    lax.fori_loop(0, width // 128, weights, 0)
+    flushed = flush([(dw_ref, dw_out)], out_sem)
     group.spread_sent(dba, ag_send, ag_recv)
     bg(3)
     total = group.landed_sum(stage[me].astype(F32), stage, landing, rs_send, rs_recv)
@@ -527,6 +561,8 @@
     gin = norm_back(total, normed, rstd, mod_ref[1:2]) + gmid_ref[...]
     gin_ref[...] = gin.astype(BF16)
     bg(4)
+    for copy in flushed:
+        copy.wait()
 
 
 class Place:
@@ -631,6 +667,16 @@
 VM = pl.BlockSpec(memory_space=pltpu.VMEM)
 ANY = pl.BlockSpec(memory_space=pltpu.HBM)
 DMA = pltpu.SemaphoreType.DMA
+
+
+def by_rows(count, body):
+    block = count // 9 if count % 144 == 0 else count
+
+    def step(index, carry):
+        body(pl.ds(pl.multiple_of(index * block, 16), block))
+        return carry
+
+    lax.fori_loop(0, count // block, step, 0)
 
 
 class Handle:
@@ -786,15 +832,25 @@
             for step in order:
                 load_own(step).wait()
                 to_mate(step).wait_recv()
-                own[step] = (own[step].astype(F32) + near[step].astype(F32)).astype(BF16)
+
+                def add(rows):
+                    total = own[step, rows].astype(F32) + near[step, rows].astype(F32)
+                    own[step, rows] = total.astype(BF16)
+
+                by_rows(self.chunk, add)
                 if step:
                     across(step).start()
         if phase == "c":
-            total = own[0].astype(F32)
             for step in range(1, chips):
                 across(step).wait_recv()
-                total = total + far[step].astype(F32)
-            out[...] = total.astype(BF16)
+
+            def add(rows):
+                total = own[0, rows].astype(F32)
+                for step in range(1, chips):
+                    total = total + far[step, rows].astype(F32)
+                out[rows] = total.astype(BF16)
+
+            by_rows(self.chunk, add)
             for step in range(chips):
                 to_mate(step).wait_send()
                 if step:
@@ -861,7 +917,11 @@
                     if role == 1:
                         to(land.at[1], land.at[1], 0, 1, 1).wait_recv()
                     if role < 2:
-                        out[...] = land[0].astype(F32) + land[1].astype(F32)
+
+                        def add(rows):
+                            out[rows] = land[0, rows].astype(F32) + land[1, rows].astype(F32)
+
+                        by_rows(part.shape[0], add)
 
 
 class Deliver(Task):
@@ -1039,12 +1099,18 @@
         [(hidden, VM), (mod, VM), (bias, VM), (bproj, VM), (w.array, ANY)],
         [
             ((tokens, width), F32, VM),
-            ((size, tokens, width), BF16, VM),
-            ((3, size, tokens, part_width), BF16, VM),
-            ((size, tokens, part_width), BF16, VM),
+            ((size, tokens, width), BF16, ANY),
+            ((3, size, tokens, part_width), BF16, ANY),
+            ((size, tokens, part_width), BF16, ANY),
             ((tokens, width), F32, VM),
         ],
-        [pltpu.VMEM(w.shape, BF16), pltpu.VMEM((width, part_width), BF16)]
+        [
+            pltpu.VMEM((size, tokens, width), BF16),
+            pltpu.VMEM((3, size, tokens, part_width), BF16),
+            pltpu.VMEM((size, tokens, part_width), BF16),
+            DMA((3,)),
+        ]
+        + [pltpu.VMEM(w.shape, BF16), pltpu.VMEM((width, part_width), BF16)]
         + bufs
         + [DMA((1,))]
         + sems,
@@ -1064,12 +1130,18 @@
         [(middle, VM), (mod, VM), (b1, VM), (b2, VM), (w1.array, ANY), (w2.array, ANY)],
         [
             ((tokens, width), BF16, VM),
-            ((size, tokens, width), BF16, VM),
-            ((size, tokens, units), F32, VM),
-            ((size, tokens, units), BF16, VM),
+            ((size, tokens, width), BF16, ANY),
+            ((size, tokens, units), F32, ANY),
+            ((size, tokens, units), BF16, ANY),
             ((tokens, width), F32, VM),
         ],
-        [pltpu.VMEM(w1.shape, BF16)] * 2 + bufs + [DMA((2,))] + sems,
+        [
+            pltpu.VMEM((size, tokens, width), BF16),
+            pltpu.VMEM((size, tokens, units), F32),
+            pltpu.VMEM((size, tokens, units), BF16),
+            DMA((3,)),
+        ]
+        + [pltpu.VMEM(w1.shape, BF16)] * 2 + bufs + [DMA((2,))] + sems,
         schedule,
         cid,
         "mlp_fwd",
@@ -1084,16 +1156,25 @@
     ins = (grad, middle, mod, branch, normed, pre, gelu)
     return launch(
         mlp_bwd_kernel,
-        [(array, VM) for array in ins] + [(w1.array, ANY), (w2.array, ANY)],
+        [(array, spec) for array, spec in zip(ins, [VM] * 4 + [ANY] * 3)]
+        + [(w1.array, ANY), (w2.array, ANY)],
         [
             ((tokens, width), F32, VM),
-            (w1.shape, BF16, VM),
-            (w2.shape, BF16, VM),
+            (w1.shape, BF16, ANY),
+            (w2.shape, BF16, ANY),
             ((1, units), F32, VM),
             ((1, width), F32, VM),
             ((3, width), F32, VM),
         ],
         [pltpu.VMEM(w1.shape, BF16)] * 2
+        + [
+            DMA((2,)),
+            pltpu.VMEM(normed.shape, BF16),
+            pltpu.VMEM(pre.shape, F32),
+            pltpu.VMEM(gelu.shape, BF16),
+            DMA((3,)),
+        ]
+        + [pltpu.VMEM(w1.shape, BF16)] * 2
         + [pltpu.VMEM((size, tokens, width), BF16), pltpu.VMEM((size, tokens, units), BF16)]
         + bufs
         + [DMA((2,))]
@@ -1113,15 +1194,21 @@
     ins = (gmid, hidden, mod, branch, normed, proj, att)
     return launch(
         att_bwd_kernel,
-        [(array, VM) for array in ins] + [(w.array, ANY)],
+        [(array, spec) for array, spec in zip(ins, [VM] * 4 + [ANY] * 3)] + [(w.array, ANY)],
         [
             ((tokens, width), BF16, VM),
-            (w.shape, BF16, VM),
+            (w.shape, BF16, ANY),
             ((1, 3 * part_width), F32, VM),
             ((1, width), F32, VM),
             ((3, width), F32, VM),
         ],
         [
+            pltpu.VMEM(w.shape, BF16),
+            DMA((1,)),
+            pltpu.VMEM(normed.shape, BF16),
+            pltpu.VMEM(proj.shape, BF16),
+            pltpu.VMEM(att.shape, BF16),
+            DMA((3,)),
             pltpu.VMEM(w.shape, BF16),
             pltpu.VMEM((width, part_width), BF16),
             pltpu.VMEM((size, tokens, width), BF16),

time: 554 us -> 526 us (0.949); the launches traced: 545 us -> 526 us
  Pallas kernels: 506 us -> 487 us
    pallas_call x10, Pallas kernels: 506 us -> 487 us  [launch(): pl.pallas_call(body, out_shape=tuple((jax.ShapeDtypeStruct(shape, dtype)...]
where the time goes in v6:
time: 526 us
  Pallas kernels  487 us (93%)
  local copies, waits for them, and re-layouts  33.3 us (6%)
    pallas_call x10, Pallas kernels, launch(): pl.pallas_call(body, out_shape=tuple((jax.ShapeDtypeStruct(shape, dtype)...  487 us
    unnamed x68, local copies, waits for them, and re-layouts  21.2 us

profile of v6, /device:TPU:4, one launch (start us, length us, event | category | flops | bytes accessed | tf_op | source)
XLA Modules:
  0.0 525.9 jit_solution(2489577255891721262)
XLA Ops:
  0.7 0.8 slice_bitcast_fusion.9
  1.4 0.8 concatenate.34
  2.3 1.4 copy.38
  3.7 0.0 copy-start.27
  3.8 1.1 copy.40
  4.9 0.2 copy.39
  5.0 1.2 pad_maximum_fusion.refs_5_.refs_6_
  6.2 0.1 reshape.142
  6.4 1.1 copy-done.17
  7.4 107.9 %prologue.1 = (f32[8,1,1728]{2,1,0:T(1,128)S(1)}, bf16[8,288]{1,0:T(8,128)(2,1)S(1)}, f32[2,1,4032]{2,1,0:T(1,128)S(1)}, bf16[128,1152]{1,0:T(8,128)(2,1)S(1)}, ...) custom-call(f32[4,2,288]{2,1,0:T(2,128)S(1)} %bitcast.72, ...), custom_call_target="tpu_custom_call" | custom-call | tf_op jit(solution)/shard_map/prologue/pallas_call | solution.py:1063
  115.3 0.1 fusion.3
  115.4 0.1 pad.9.clone
  115.5 0.1 pad_maximum_fusion.5
  115.6 0.1 slice_bitcast_fusion.1
  115.7 0.2 slice_reduce_fusion
  115.9 0.1 squeeze.68.refs_1_.refs_2_
  116.0 29.4 %att_fwd.2 = (f32[128,1152]{1,0:T(8,128)S(1)}, bf16[4,128,1152]{2,1,0:T(8,128)(2,1)S(1)}, bf16[3,4,128,288]{3,2,1,0:T(8,128)(2,1)}, bf16[4,128,288]{2,1,0:T(8,12...) custom-call(bf16[128,1152]{1,0:T(8,128)(2,1)S(1)} %get-tuple-element.84.refs_0_., ...), custom_call_target="tpu_custom_call", output_to_operand_aliasing={{5}: (5, {})} | custom-call | tf_op jit(solution)/shard_map/att_fwd/pallas_call | solution.py:1063
  145.4 1.0 copy-done.3
  146.4 0.8 copy-done.13
  147.2 0.7 copy-done.20
  148.0 24.7 %mlp_fwd.2 = (bf16[128,1152]{1,0:T(8,128)(2,1)S(1)}, bf16[4,128,1152]{2,1,0:T(8,128)(2,1)S(1)}, f32[4,128,1152]{2,1,0:T(8,128)}, bf16[4,128,1152]{2,1,0:T(8,128)...) custom-call(f32[128,1152]{1,0:T(8,128)S(1)} %get-tuple-element.89.refs_0_.refs_1_,, ...), custom_call_target="tpu_custom_call", output_to_operand_aliasing={{5}: (6, {})} | custom-call | tf_op jit(solution)/shard_map/mlp_fwd/pallas_call | solution.py:1063
  172.7 1.0 copy-done.4
  173.7 0.9 copy-done.18
  174.5 0.1 squeeze.73.refs_1_.refs_2_
  174.6 34.1 %att_fwd.3 = (f32[128,1152]{1,0:T(8,128)S(1)}, bf16[4,128,1152]{2,1,0:T(8,128)(2,1)S(1)}, bf16[3,4,128,288]{3,2,1,0:T(8,128)(2,1)}, bf16[4,128,288]{2,1,0:T(8,12...) custom-call(bf16[128,1152]{1,0:T(8,128)(2,1)S(1)} %get-tuple-element, ...), custom_call_target="tpu_custom_call", output_to_operand_aliasing={{6}: (6, {}), {7}: (7, {})} | custom-call | tf_op jit(solution)/shard_map/att_fwd/pallas_call | solution.py:1063
  208.8 1.0 copy-done.5
  209.8 26.7 %mlp_fwd.3 = (bf16[128,1152]{1,0:T(8,128)(2,1)S(1)}, bf16[4,128,1152]{2,1,0:T(8,128)(2,1)S(1)}, f32[4,128,1152]{2,1,0:T(8,128)}, bf16[4,128,1152]{2,1,0:T(8,128)(2,1)S(1)}, f32[128,1152]{1,0:T(8,128)S(1)}) custom-call(f32[128,1152]{1,0:T(8,128)S(1)} %get-tuple-element.98.refs_0_.refs_1_, f32[6,1152]{1,0:T(8,128)S(1)} %squeeze.73.refs_1_.refs_2_, ...), custom_call_target="tpu_custom_call" | custom-call | tf_op jit(solution)/shard_map/mlp_fwd/pallas_call | solution.py:1063
  236.5 1.0 copy-done.6
  237.5 1.0 copy-done.7
  238.5 36.0 %mlp_bwd.2 = (f32[128,1152]{1,0:T(8,128)S(1)}, bf16[1152,1152]{1,0:T(8,128)(2,1)}, bf16[1152,1152]{1,0:T(8,128)(2,1)}, f32[1,1152]{1,0:T(1,128)S(1)}, f32[1,1152...) custom-call(bf16[128,1152]{1,0:T(8,128)(2,1)S(1)} %get-tuple-element.97.refs_0_, ...), custom_call_target="tpu_custom_call" | custom-call | tf_op jit(solution)/shard_map/mlp_bwd/pallas_call | solution.py:1063
  274.5 37.1 %att_bwd.2 = (bf16[128,1152]{1,0:T(8,128)(2,1)S(1)}, bf16[1152,1152]{1,0:T(8,128)(2,1)}, f32[1,864]{1,0:T(1,128)S(1)}, f32[1,1152]{1,0:T(1,128)S(1)}, f32[3,1152...) custom-call(f32[128,1152]{1,0:T(8,128)S(1)} %get-tuple-element.107.refs_0_, ...), custom_call_target="tpu_custom_call" | custom-call | tf_op jit(solution)/shard_map/att_bwd/pallas_call | solution.py:1063
  311.7 0.8 copy-done.8
  312.5 0.8 copy-done.10
  313.4 27.9 %mlp_bwd.3 = (f32[128,1152]{1,0:T(8,128)S(1)}, bf16[1152,1152]{1,0:T(8,128)(2,1)}, bf16[1152,1152]{1,0:T(8,128)(2,1)}, f32[1,1152]{1,0:T(1,128)S(1)}, f32[1,1152...) custom-call(bf16[128,1152]{1,0:T(8,128)(2,1)S(1)} %get-tuple-element.114.refs_0_.refs_4_, ...), custom_call_target="tpu_custom_call" | custom-call | tf_op jit(solution)/shard_map/mlp_bwd/pallas_call | solution.py:1063
  341.3 0.8 copy-done.11
  342.1 36.6 %att_bwd.3 = (bf16[128,1152]{1,0:T(8,128)(2,1)S(1)}, bf16[1152,1152]{1,0:T(8,128)(2,1)}, f32[1,864]{1,0:T(1,128)S(1)}, f32[1,1152]{1,0:T(1,128)S(1)}, f32[3,1152...) custom-call(f32[128,1152]{1,0:T(8,128)S(1)} %get-tuple-element.120.refs_0_, ...), custom_call_target="tpu_custom_call" | custom-call | tf_op jit(solution)/shard_map/att_bwd/pallas_call | solution.py:1063
  378.8 0.7 copy-done.22
  379.5 0.1 fusion.5
  379.6 0.1 concatenate.39
  379.7 0.1 fusion.6
  379.8 0.1 concatenate.40
  380.1 0.1 pad_maximum_fusion.1
  380.2 0.1 reshape.138.refs_0_
  380.3 1.0 copy-done.23
  381.3 126.7 %epilogue.1 = (bf16[8,1728]{1,0:T(8,128)(2,1)S(1)}, f32[1,1728]{1,0:T(1,128)S(1)}, f32[4,2,288]{2,1,0:T(2,128)S(1)}, f32[1,4032]{1,0:T(1,128)S(1)}, bf16[2,128,1...) custom-call(f32[8,1,1728]{2,1,0:T(1,128)S(1)} %reshape.138.refs_0_, ...), custom_call_target="tpu_custom_call" | custom-call | tf_op jit(solution)/shard_map/epilogue/pallas_call | solution.py:1063
  508.0 0.1 fusion.4
  508.1 0.6 constant_dynamic-slice_fusion
  508.8 2.2 slice.111
  511.0 1.6 copy.42
  512.7 1.6 copy.46
  514.2 1.8 convolution_bitcast_fusion
  516.0 1.1 bitcast_convert_fusion
  517.1 1.3 slice_bitcast_fusion
  518.5 1.0 copy.47
  519.4 0.1 reshape.139
  519.6 0.6 copy.45
  520.2 0.6 constant_dynamic-slice_fusion.2
  520.8 0.1 reshape.140
  520.9 0.6 fusion.2
  521.5 0.7 constant_dynamic-slice_fusion.4
  522.2 0.8 copy.57
  523.0 1.1 copy.58
  524.1 0.7 copy-done.24
  524.8 1.1 copy.59
  (61 shorter events, 0.3 us)
Async XLA Ops:
  0.6 4.2 copy-start.26
  3.7 2.5 copy-start.27
  3.7 2.6 copy-start.29
  3.8 2.6 copy-start
  3.8 2.6 copy-start.1
  3.8 2.6 copy-start.2
  6.4 1.1 copy-start.17
  145.4 1.0 copy-start.3
  146.4 0.8 copy-start.13
  147.2 0.7 copy-start.20
  148.0 26.7 %copy-start.12 = (bf16[2,1,128,1152]{3,2,1,0:T(8,128)(2,1)S(1)}, bf16[2,1,128,1152]{3,2,1,0:T(8,128)(2,1)}, u32[]{:S(2)}) copy-start(bf16[2,1,128,1152]{3,2,1,0:T(8,128)(2,1)} %param.15) | copy-start | bytes 1769476
  172.6 1.0 copy-start.4
  173.7 0.9 copy-start.18
  208.7 1.0 copy-start.5
  236.5 1.0 copy-start.6
  237.5 1.0 copy-start.7
  274.5 37.2 %copy-start.15 = (bf16[2,128,1152]{2,1,0:T(8,128)(2,1)}, bf16[2,128,1152]{2,1,0:T(8,128)(2,1)S(1)}, u32[]{:S(2)}) copy-start(bf16[2,128,1152]{2,1,0:T(8,128)(2,1)S(1)} %get-tuple-element.106) | copy-start | bytes 1769476
  274.5 38.8 %copy-start.19 = (f32[128,1152]{1,0:T(8,128)S(1)}, f32[128,1152]{1,0:T(8,128)}, u32[]{:S(2)}) copy-start(f32[128,1152]{1,0:T(8,128)} %copy-done.18) | copy-start | bytes 1769476
  311.7 0.8 copy-start.8
  312.5 0.8 copy-start.10
  313.4 28.8 %copy-start.14 = (f32[128,1152]{1,0:T(8,128)S(1)}, f32[128,1152]{1,0:T(8,128)}, u32[]{:S(2)}) copy-start(f32[128,1152]{1,0:T(8,128)} %copy-done.13) | copy-start | bytes 1769476
  313.4 28.8 %copy-start.21 = (bf16[4,128,288]{2,1,0:T(8,128)(2,1)S(1)}, bf16[4,128,288]{2,1,0:T(8,128)(2,1)}, u32[]{:S(2)}) copy-start(bf16[4,128,288]{2,1,0:T(8,128)(2,1)} %copy-done.20) | copy-start | bytes 884740
  341.3 0.8 copy-start.11
  342.1 38.2 %copy-start.9 = (bf16[288,1152]{1,0:T(8,128)(2,1)S(1)}, bf16[288,1152]{1,0:T(8,128)(2,1)}, u32[]{:S(2)}) copy-start(bf16[288,1152]{1,0:T(8,128)(2,1)} %copy-done.8) | copy-start | bytes 1990660
  378.8 0.7 copy-start.22
  380.3 1.0 copy-start.23
  516.0 3.5 copy-start.28
  517.1 5.1 copy-start.16
  517.1 5.9 %copy-start.25 = (f32[288,1152]{1,0:T(8,128)S(1)}, f32[288,1152]{1,0:T(8,128)}, u32[]{:S(2)}) copy-start(f32[288,1152]{1,0:T(8,128)} %get-tuple-element.153) | copy-start | bytes 3981316
  523.0 1.8 copy-start.24

commit v7 on v6

--- a/solution.py
+++ b/solution.py
@@ -1600,13 +1600,7 @@
     for layer in (1, 0):
         middle, normed, proj, att, branch, normed2, pre, gelu, branch2 = saved[layer]
         if layer == 1:
-            mlp_plan = plan(
-                [(acts_first, "a"), (acts_second, "a")],
-                [],
-                [(acts_first, "zb"), (acts_second, "zb")],
-                [],
-                [(acts_first, "c"), (acts_second, "c")],
-            )
+            mlp_plan = plan([], [], [], [], [])
         else:
             third = narrow[1][0]
             mlp_plan = plan([(third, "a")], [(third, "b")], [], [], [(third, "c")])
@@ -1622,6 +1616,11 @@
         att_plan = plan(
             [(two, "a"), (one, "a")], [(two, "b"), (one, "b")], [], [], [(two, "c"), (one, "c")]
         )
+        if layer == 1:
+            for task in (acts_first, acts_second):
+                att_plan[0].append((task, "a"))
+                att_plan[1] += [(task, "z"), (task, "b")]
+                att_plan[4].append((task, "c"))
         gin, dw, dbqkv, dbproj, dmod1 = att_bwd(
             gmid, hidden[layer], modul[layer], branch, normed, proj, att, w[layer][0],
             att_plan, 7 + 2 * (1 - layer),

time: 526 us -> 524 us (level)
    unnamed x68 -> x64, local copies, waits for them, and re-layouts: 21.2 us -> 20.2 us
where the time goes in v7:
time: 524 us; the launch traced here: 523 us
  Pallas kernels  486 us (93%)
  local copies, waits for them, and re-layouts  32.2 us (6%)
    pallas_call x10, Pallas kernels, launch(): pl.pallas_call(body, out_shape=tuple((jax.ShapeDtypeStruct(shape, dtype)...  486 us
    unnamed x64, local copies, waits for them, and re-layouts  20.2 us

profile of v7, /device:TPU:4, one launch (start us, length us, event | category | flops | bytes accessed | tf_op | source)
XLA Modules:
  0.0 523.5 jit_solution(14042110274829102520)
XLA Ops:
  0.7 0.8 slice_bitcast_fusion.9
  1.4 0.8 concatenate.34
  2.3 1.4 copy.38
  3.8 0.0 copy-start
  3.8 0.0 copy-start.1
  3.8 1.1 copy.40
  4.9 0.2 copy.39
  5.0 1.2 pad_maximum_fusion.refs_5_.refs_6_
  6.2 0.1 reshape.142
  6.4 1.1 copy-done.15
  7.4 107.9 %prologue.1 = (f32[8,1,1728]{2,1,0:T(1,128)S(1)}, bf16[8,288]{1,0:T(8,128)(2,1)S(1)}, f32[2,1,4032]{2,1,0:T(1,128)S(1)}, bf16[128,1152]{1,0:T(8,128)(2,1)S(1)}, ...) custom-call(f32[4,2,288]{2,1,0:T(2,128)S(1)} %bitcast.72, ...), custom_call_target="tpu_custom_call" | custom-call | tf_op jit(solution)/shard_map/prologue/pallas_call | solution.py:1063
  115.3 0.1 fusion.3
  115.4 0.1 pad.9.clone
  115.5 0.1 pad_maximum_fusion.5
  115.6 0.1 slice_bitcast_fusion.1
  115.7 0.2 slice_reduce_fusion
  115.9 0.1 squeeze.68.refs_1_.refs_2_
  116.0 29.4 %att_fwd.2 = (f32[128,1152]{1,0:T(8,128)S(1)}, bf16[4,128,1152]{2,1,0:T(8,128)(2,1)S(1)}, bf16[3,4,128,288]{3,2,1,0:T(8,128)(2,1)}, bf16[4,128,288]{2,1,0:T(8,12...) custom-call(bf16[128,1152]{1,0:T(8,128)(2,1)S(1)} %get-tuple-element.84.refs_0_., ...), custom_call_target="tpu_custom_call", output_to_operand_aliasing={{5}: (5, {})} | custom-call | tf_op jit(solution)/shard_map/att_fwd/pallas_call | solution.py:1063
  145.4 1.0 copy-done.4
  146.4 0.8 copy-done.11
  147.2 0.7 copy-done.18
  148.0 24.7 %mlp_fwd.2 = (bf16[128,1152]{1,0:T(8,128)(2,1)S(1)}, bf16[4,128,1152]{2,1,0:T(8,128)(2,1)S(1)}, f32[4,128,1152]{2,1,0:T(8,128)}, bf16[4,128,1152]{2,1,0:T(8,128)...) custom-call(f32[128,1152]{1,0:T(8,128)S(1)} %get-tuple-element.89.refs_0_.refs_1_,, ...), custom_call_target="tpu_custom_call", output_to_operand_aliasing={{5}: (6, {})} | custom-call | tf_op jit(solution)/shard_map/mlp_fwd/pallas_call | solution.py:1063
  172.7 1.0 copy-done.5
  173.7 0.8 copy-done.16
  174.5 0.1 squeeze.73.refs_1_.refs_2_
  174.6 34.1 %att_fwd.3 = (f32[128,1152]{1,0:T(8,128)S(1)}, bf16[4,128,1152]{2,1,0:T(8,128)(2,1)S(1)}, bf16[3,4,128,288]{3,2,1,0:T(8,128)(2,1)}, bf16[4,128,288]{2,1,0:T(8,12...) custom-call(bf16[128,1152]{1,0:T(8,128)(2,1)S(1)} %get-tuple-element, ...), custom_call_target="tpu_custom_call", output_to_operand_aliasing={{6}: (6, {}), {7}: (7, {})} | custom-call | tf_op jit(solution)/shard_map/att_fwd/pallas_call | solution.py:1063
  208.7 1.0 copy-done.3
  209.7 26.7 %mlp_fwd.3 = (bf16[128,1152]{1,0:T(8,128)(2,1)S(1)}, bf16[4,128,1152]{2,1,0:T(8,128)(2,1)S(1)}, f32[4,128,1152]{2,1,0:T(8,128)}, bf16[4,128,1152]{2,1,0:T(8,128)(2,1)S(1)}, f32[128,1152]{1,0:T(8,128)S(1)}) custom-call(f32[128,1152]{1,0:T(8,128)S(1)} %get-tuple-element.98.refs_0_.refs_1_, f32[6,1152]{1,0:T(8,128)S(1)} %squeeze.73.refs_1_.refs_2_, ...), custom_call_target="tpu_custom_call" | custom-call | tf_op jit(solution)/shard_map/mlp_fwd/pallas_call | solution.py:1063
  236.4 1.0 copy-done.6
  237.4 27.2 %mlp_bwd.2 = (f32[128,1152]{1,0:T(8,128)S(1)}, bf16[1152,1152]{1,0:T(8,128)(2,1)}, bf16[1152,1152]{1,0:T(8,128)(2,1)}, f32[1,1152]{1,0:T(1,128)S(1)}, f32[1,1152]{1,0:T(1,128)S(1)}, /*index=5*/f32[3,1152]{1,0:T(4,128)S(1)}) custom-call(bf16[128,1152]{1,0:T(8,128)(2,1)S(1)} %get-tuple-element.97.refs_0_, f32[128,1152]{1,0:T(8,128)S(1)} %get-tuple-element.98.refs_0_.refs_1_, ...), custom_call_target="tpu_custom_call" | custom-call | tf_op jit(solution)/shard_map/mlp_bwd/pallas_call | solution.py:1063
  264.6 41.0 %att_bwd.2 = (bf16[128,1152]{1,0:T(8,128)(2,1)S(1)}, bf16[1152,1152]{1,0:T(8,128)(2,1)}, f32[1,864]{1,0:T(1,128)S(1)}, f32[1,1152]{1,0:T(1,128)S(1)}, f32[3,1152...) custom-call(f32[128,1152]{1,0:T(8,128)S(1)} %get-tuple-element.105.r, ...), custom_call_target="tpu_custom_call" | custom-call | tf_op jit(solution)/shard_map/att_bwd/pallas_call | solution.py:1063
  305.6 0.8 copy-done.7
  306.5 0.8 copy-done.13
  307.3 29.6 %mlp_bwd.3 = (f32[128,1152]{1,0:T(8,128)S(1)}, bf16[1152,1152]{1,0:T(8,128)(2,1)}, bf16[1152,1152]{1,0:T(8,128)(2,1)}, f32[1,1152]{1,0:T(1,128)S(1)}, f32[1,1152...) custom-call(bf16[128,1152]{1,0:T(8,128)(2,1)S(1)} %get-tuple-element.114.refs_0_.refs_4_, ...), custom_call_target="tpu_custom_call" | custom-call | tf_op jit(solution)/shard_map/mlp_bwd/pallas_call | solution.py:1063
  336.9 0.8 copy-done.9
  337.8 37.1 %att_bwd.3 = (bf16[128,1152]{1,0:T(8,128)(2,1)S(1)}, bf16[1152,1152]{1,0:T(8,128)(2,1)}, f32[1,864]{1,0:T(1,128)S(1)}, f32[1,1152]{1,0:T(1,128)S(1)}, f32[3,1152...) custom-call(f32[128,1152]{1,0:T(8,128)S(1)} %get-tuple-element.120.refs_0_, ...), custom_call_target="tpu_custom_call" | custom-call | tf_op jit(solution)/shard_map/att_bwd/pallas_call | solution.py:1063
  374.9 0.7 copy-done.20
  375.6 0.1 fusion.5
  375.6 0.1 concatenate.39
  375.8 0.1 fusion.6
  375.8 0.1 concatenate.40
  376.2 0.1 pad_maximum_fusion.1
  376.3 0.1 reshape.138.refs_0_
  376.4 1.0 copy-done.21
  377.4 128.3 %epilogue.1 = (bf16[8,1728]{1,0:T(8,128)(2,1)S(1)}, f32[1,1728]{1,0:T(1,128)S(1)}, f32[4,2,288]{2,1,0:T(2,128)S(1)}, f32[1,4032]{1,0:T(1,128)S(1)}, bf16[2,128,1...) custom-call(f32[8,1,1728]{2,1,0:T(1,128)S(1)} %reshape.138.refs_0_, ...), custom_call_target="tpu_custom_call" | custom-call | tf_op jit(solution)/shard_map/epilogue/pallas_call | solution.py:1063
  505.6 0.1 fusion.4
  505.7 0.6 constant_dynamic-slice_fusion
  506.4 2.2 slice.111
  508.6 1.6 copy.42
  510.3 1.6 copy.46
  511.9 1.8 convolution_bitcast_fusion
  513.6 1.1 bitcast_convert_fusion
  514.7 1.3 slice_bitcast_fusion
  516.1 1.0 copy.47
  517.0 0.1 reshape.139
  517.2 0.6 copy.45
  517.8 0.6 constant_dynamic-slice_fusion.2
  518.4 0.1 reshape.140
  518.5 0.6 fusion.2
  519.2 0.7 constant_dynamic-slice_fusion.4
  519.8 0.8 copy.57
  520.6 1.1 copy.58
  521.7 0.7 copy-done.22
  522.4 1.1 copy.59
  (57 shorter events, 0.3 us)
Async XLA Ops:
  0.6 4.2 copy-start.24
  3.7 2.5 copy-start.25
  3.7 2.6 copy-start.27
  3.8 2.6 copy-start
  3.8 2.6 copy-start.1
  3.8 2.6 copy-start.2
  6.4 1.1 copy-start.15
  145.4 1.0 copy-start.4
  146.4 0.8 copy-start.11
  147.2 0.7 copy-start.18
  148.0 26.6 %copy-start.10 = (bf16[2,1,128,1152]{3,2,1,0:T(8,128)(2,1)S(1)}, bf16[2,1,128,1152]{3,2,1,0:T(8,128)(2,1)}, u32[]{:S(2)}) copy-start(bf16[2,1,128,1152]{3,2,1,0:T(8,128)(2,1)} %param.15) | copy-start | bytes 1769476
  172.7 1.0 copy-start.5
  173.7 0.8 copy-start.16
  208.7 1.0 copy-start.3
  236.4 1.0 copy-start.6
  264.6 42.6 %copy-start.17 = (f32[128,1152]{1,0:T(8,128)S(1)}, f32[128,1152]{1,0:T(8,128)}, u32[]{:S(2)}) copy-start(f32[128,1152]{1,0:T(8,128)} %copy-done.16) | copy-start | bytes 1769476
  305.6 0.8 copy-start.7
  306.5 0.8 copy-start.13
  307.3 30.5 %copy-start.12 = (f32[128,1152]{1,0:T(8,128)S(1)}, f32[128,1152]{1,0:T(8,128)}, u32[]{:S(2)}) copy-start(f32[128,1152]{1,0:T(8,128)} %copy-done.11) | copy-start | bytes 1769476
  307.3 30.5 %copy-start.19 = (bf16[4,128,288]{2,1,0:T(8,128)(2,1)S(1)}, bf16[4,128,288]{2,1,0:T(8,128)(2,1)}, u32[]{:S(2)}) copy-start(bf16[4,128,288]{2,1,0:T(8,128)(2,1)} %copy-done.18) | copy-start | bytes 884740
  336.9 0.8 copy-start.9
  337.8 38.6 %copy-start.8 = (bf16[288,1152]{1,0:T(8,128)(2,1)S(1)}, bf16[288,1152]{1,0:T(8,128)(2,1)}, u32[]{:S(2)}) copy-start(bf16[288,1152]{1,0:T(8,128)(2,1)} %copy-done.7) | copy-start | bytes 1990660
  374.8 0.7 copy-start.20
  376.4 1.0 copy-start.21
  513.6 3.5 copy-start.26
  514.7 5.1 copy-start.14
  514.7 5.9 %copy-start.23 = (f32[288,1152]{1,0:T(8,128)S(1)}, f32[288,1152]{1,0:T(8,128)}, u32[]{:S(2)}) copy-start(f32[288,1152]{1,0:T(8,128)} %get-tuple-element.153) | copy-start | bytes 3981316
  520.6 1.8 copy-start.22
